TPU v7x, 512 devices: a whole 4x4x16 slice. The times are simulated.
512 devices in a mesh: patch: 128 (over x, z, core), chan: 4 (over y).
Axes of the slice: x: 4, y: 4, z: 16, core: 2. Of those that a mesh axis runs over, the one named last changes fastest.
Arguments:
- grid_latent: bfloat16 [32768, 512], P('patch', 'chan'), may hold values from -6 to 6
- mesh_latent: bfloat16 [8192, 512], P('patch', 'chan'), may hold values from -6 to 6
- w_source: bfloat16 [512, 512], replicated, may hold values from -0.25 to 0.25
- w_dest: bfloat16 [512, 512], replicated, may hold values from -0.25 to 0.25
- w_out: bfloat16 [512, 512], replicated, may hold values from -0.25 to 0.25
- edge_bias: float32 [512], P('chan'), may hold values from -3 to 3
- norm_gain: float32 [512], P('chan'), may hold values from 0.5 to 1.5
- edge_source: int32 [65536], P('patch'), may hold values from 0 to 255
- edge_patch: int32 [65536, 1], P('patch'), may hold values from 0 to 127; in each aligned block of 512 rows (0 to 511, 512 to 1023, ...) at most 8 rows name the same one
- edge_node: int32 [65536], P('patch'), may hold values from 0 to 63
- cotangent: bfloat16 [8192, 512], P('patch', 'chan'), may hold values from -6 to 6
Outputs:
- updated: bfloat16 [8192, 512], P('patch', 'chan')
- grad_grid: bfloat16 [32768, 512], P('patch', 'chan')
- grad_mesh: bfloat16 [8192, 512], P('patch', 'chan')
- grad_w_source: float32 [512, 512], P(None, 'chan')
- grad_w_dest: float32 [512, 512], P(None, 'chan')
- grad_w_out: float32 [512, 512], P(None, 'chan')
- grad_bias: float32 [512], P('chan')
- grad_gain: float32 [512], P('chan')
Inputs may be any that keep to these rules, and one draw needn't show every extreme that they name: `edge_patch`: the edges of band b are rows b * 512 to (b + 1) * 512 - 1; in the rows of one band no patch is named by more than 8 edges, and one patch is named by exactly 8.
All inputs are finite; a program needn't handle non-finite values.
Results may differ from a plain program's by a relative error of at most 0.0095.
Values may be sent and summed in bfloat16 or wider, within the bound.
No kernel may reach another device: no remote copies, remote signals or barrier semaphores. Data moves between devices by JAX's collectives and lax.ppermute only.
A program may use at most 64 MiB of HBM per device.

v0:
```python
import math

import jax
import jax.numpy as jnp
from jax import lax
from jax.sharding import Mesh
from jax.sharding import PartitionSpec as P

PATCH = ("patch_0", "patch_1", "patch_2")


norm_eps = 1e-05


def joined_along(blocks, dim):
    shape = list(blocks.shape[1:])
    shape[dim] *= blocks.shape[0]
    return jnp.moveaxis(blocks, 0, dim).reshape(shape)


def from_everyone(x, axis):
    copies = jnp.broadcast_to(x, (lax.axis_size(axis), *x.shape))
    return lax.all_to_all(copies, axis, split_axis=0, concat_axis=0, tiled=True)


def gather_directly(x, axis, dim):
    return joined_along(from_everyone(x, axis), dim)


def taken_together(x, axis):
    everything = from_everyone(x, axis)
    return jnp.sum(everything, axis=0)


def together(arrays, axis):
    flat, at, done = (jnp.concatenate([a.reshape(-1) for a in arrays]), 0, [])
    so_far = taken_together(flat, axis)
    for a in arrays:
        done.append(so_far[at : at + a.size].reshape(a.shape))
        at += a.size
    return tuple(done)


def filled_up(lines, size):
    spare = -len(lines) % size
    return jnp.pad(lines, [(0, spare)] + [(0, 0)] * (lines.ndim - 1))


def gather_axes(x, axes, dim):
    far, near = axes
    blocks = from_everyone(from_everyone(x, far), near)
    return joined_along(blocks.swapaxes(0, 1).reshape(-1, *x.shape), dim)


def split_up(x, dim, size):
    shape = x.shape
    blocks = x.reshape(*shape[:dim], size, shape[dim] // size, *shape[dim + 1 :])
    return jnp.moveaxis(blocks, dim, 0)


def summed_on_arrival(x, axis, dim):
    size = lax.axis_size(axis)
    blocks = lax.all_to_all(split_up(x, dim, size), axis, 0, 0, tiled=True)
    return jnp.sum(blocks, axis=0)


def sum_by_axis(x, axes, dim):
    far, near = axes
    blocks = split_up(x, dim, lax.axis_size(far))
    nearer = summed_on_arrival(blocks, near, dim + 1)
    arrived = lax.all_to_all(nearer, far, split_axis=0, concat_axis=0, tiled=True)
    return arrived.sum(axis=0)


def total_of(x, axes):
    padded = filled_up(x, lax.axis_size(axes[0]) * lax.axis_size(axes[1]))
    whole = gather_axes(sum_by_axis(padded, axes, 0), axes, 0)
    return lax.slice_in_dim(whole, 0, len(x)).reshape(x.shape)


def in_one(arrays, axis):
    flat, at, done = (jnp.concatenate([a.reshape(-1) for a in arrays]), 0, [])
    so_far = total_of(flat, axis)
    for a in arrays:
        done.append(so_far[at : at + a.size].reshape(a.shape))
        at += a.size
    return tuple(done)


def slot_ranks(dest_patch, patches):
    edge_count = dest_patch.shape[0]
    block_width = math.gcd(edge_count, 128)
    onehot = (
        dest_patch.reshape(edge_count // block_width, block_width)[:, :, None]
        == jnp.arange(patches, dtype=jnp.int32)[None, None, :]
    ).astype(jnp.float32)
    strict_lower = (jnp.arange(block_width)[:, None] > jnp.arange(block_width)[None, :]).astype(
        jnp.float32
    )
    within = jnp.einsum("ij,bjp->bip", strict_lower, onehot, precision=lax.Precision.HIGHEST)
    counts = jnp.sum(onehot, axis=1)
    before = jnp.cumsum(counts, axis=0) - counts
    position = jnp.sum((within + before[:, None, :]) * onehot, axis=2)
    return position.reshape(edge_count).astype(jnp.int32)


def contract_rows(left, right):
    return lax.dot_general(
        left, right, (((0,), (0,)), ((), ())), preferred_element_type=jnp.float32
    )


def contract_cols(left, right):
    return lax.dot_general(
        left, right, (((1,), (1,)), ((), ())), preferred_element_type=jnp.float32
    )


def on_device(
    grid_latent,
    mesh_latent,
    w_source,
    w_dest,
    w_out,
    edge_bias,
    norm_gain,
    edge_source,
    edge_patch,
    edge_node,
    cotangent,
):
    patches = lax.axis_size(PATCH)
    slice_width = grid_latent.shape[1]
    latent_width = w_source.shape[0]
    offset = lax.axis_index("chan") * slice_width
    grid_count = grid_latent.shape[0]
    mesh_count = mesh_latent.shape[0]
    edge_count = edge_source.shape[0]
    capacity = max(2, 2 * edge_count // patches)
    slots = patches * capacity
    dest_patch = edge_patch[:, 0]
    slot_index = dest_patch * capacity + slot_ranks(dest_patch, patches)
    grid_full = gather_directly(grid_latent, "chan", 1)
    mesh_full = gather_directly(mesh_latent, "chan", 1)
    source_cols = lax.dynamic_slice_in_dim(w_source, offset, slice_width, 1)
    dest_cols = lax.dynamic_slice_in_dim(w_dest, offset, slice_width, 1)
    out_cols = lax.dynamic_slice_in_dim(w_out, offset, slice_width, 1)
    mesh_proj = jnp.dot(mesh_full, dest_cols, preferred_element_type=jnp.float32)
    empty_rows = jnp.zeros((slots, slice_width), jnp.bfloat16)
    projected = jnp.dot(grid_full, source_cols, preferred_element_type=jnp.float32).astype(
        jnp.bfloat16
    )
    outgoing = empty_rows.at[slot_index].set(projected[edge_source])
    targets = jnp.full((slots,), mesh_count, jnp.int32).at[slot_index].set(edge_node)
    arrived = lax.all_to_all(
        outgoing.reshape(patches, capacity, slice_width),
        PATCH,
        split_axis=0,
        concat_axis=0,
        tiled=True,
    )
    landed = lax.all_to_all(
        targets.reshape(patches, capacity), PATCH, split_axis=0, concat_axis=0, tiled=True
    )
    edge_values = arrived.reshape(slots, slice_width)
    landed = landed.reshape(slots)
    is_live = landed < mesh_count
    safe_node = jnp.minimum(landed, mesh_count - 1)
    pre_act = edge_values.astype(jnp.float32) + mesh_proj[safe_node] + edge_bias
    message = jnp.where(is_live[:, None], jax.nn.silu(pre_act), 0.0)
    summed = jax.ops.segment_sum(message, safe_node, num_segments=mesh_count).astype(jnp.bfloat16)
    summed_full = gather_directly(summed, "chan", 1)
    mixed = jnp.dot(summed_full, out_cols, preferred_element_type=jnp.float32)
    row_total, row_square = together(
        (jnp.sum(mixed, axis=1), jnp.sum(mixed * mixed, axis=1)), "chan"
    )
    row_mean = row_total / latent_width
    row_var = jnp.maximum(row_square / latent_width - row_mean * row_mean, 0.0)
    inv_scale = lax.rsqrt(row_var + norm_eps)
    normed = (mixed - row_mean[:, None]) * inv_scale[:, None]
    updated = (mesh_latent.astype(jnp.float32) + normed * norm_gain).astype(jnp.bfloat16)
    cotan_full = cotangent.astype(jnp.float32)
    gain_local = jnp.sum(cotan_full * normed, axis=0)
    scaled = cotan_full * norm_gain
    scaled_total, cross_total = together(
        (jnp.sum(scaled, axis=1), jnp.sum(scaled * normed, axis=1)), "chan"
    )
    grad_mixed = (
        (
            scaled
            - scaled_total[:, None] / latent_width
            - normed * (cross_total[:, None] / latent_width)
        )
        * inv_scale[:, None]
    ).astype(jnp.bfloat16)
    out_local = contract_rows(summed_full, grad_mixed)
    grad_full = gather_directly(grad_mixed, "chan", 1)
    grad_summed = contract_cols(grad_full, lax.dynamic_slice_in_dim(w_out, offset, slice_width, 0))
    sigmoid_val = jax.nn.sigmoid(pre_act)
    silu_slope = sigmoid_val * (1.0 + pre_act * (1.0 - sigmoid_val))
    grad_pre = jnp.where(is_live[:, None], grad_summed[safe_node] * silu_slope, 0.0).astype(
        jnp.bfloat16
    )
    grad_edges = grad_pre.astype(jnp.float32)
    bias_local = jnp.sum(grad_edges, axis=0)
    grad_mesh_proj = jax.ops.segment_sum(grad_edges, safe_node, num_segments=mesh_count).astype(
        jnp.bfloat16
    )
    returned = lax.all_to_all(
        grad_pre.reshape(patches, capacity, slice_width),
        PATCH,
        split_axis=0,
        concat_axis=0,
        tiled=True,
    )
    per_edge = returned.reshape(slots, slice_width)[slot_index]
    grad_projected = jax.ops.segment_sum(
        per_edge.astype(jnp.float32), edge_source, num_segments=grid_count
    ).astype(jnp.bfloat16)
    dest_local = contract_rows(mesh_full, grad_mesh_proj)
    source_local = contract_rows(grid_full, grad_projected)
    node_full = gather_directly(grad_mesh_proj, "chan", 1)
    grad_mesh = (
        cotan_full
        + contract_cols(node_full, lax.dynamic_slice_in_dim(w_dest, offset, slice_width, 0))
    ).astype(jnp.bfloat16)
    source_full = gather_directly(grad_projected, "chan", 1)
    grad_grid = contract_cols(
        source_full, lax.dynamic_slice_in_dim(w_source, offset, slice_width, 0)
    ).astype(jnp.bfloat16)
    grad_w_source, grad_w_dest, grad_w_out, grad_bias, grad_gain = in_one(
        (source_local, dest_local, out_local, bias_local, gain_local),
        (("patch_0", "patch_1"), "patch_2"),
    )
    return (
        updated,
        grad_grid,
        grad_mesh,
        grad_w_source,
        grad_w_dest,
        grad_w_out,
        grad_bias,
        grad_gain,
    )


def solution(mesh):
    torus = Mesh(
        mesh.devices.reshape(4, 16, 2, mesh.shape["chan"]),
        ("patch_0", "patch_1", "patch_2", "chan"),
    )
    return jax.shard_map(
        on_device,
        mesh=torus,
        in_specs=(
            P(PATCH, "chan"),
            P(PATCH, "chan"),
            P(),
            P(),
            P(),
            P("chan"),
            P("chan"),
            P(PATCH),
            P(PATCH, None),
            P(PATCH),
            P(PATCH, "chan"),
        ),
        out_specs=(
            P(PATCH, "chan"),
            P(PATCH, "chan"),
            P(PATCH, "chan"),
            P(None, "chan"),
            P(None, "chan"),
            P(None, "chan"),
            P("chan"),
            P("chan"),
        ),
        check_vma=False,
    )
```

profile of v0, /device:TPU:1, one launch (start us, length us, event | category | flops | bytes accessed | tf_op | source)
XLA Modules:
  0.0 273.0 jit_solution(6263987963606913491)
XLA Ops:
  2.5 2.6 scatter_custom_fusion
  5.8 20.5 %all-to-all-start = ((s32[128,1,8]{2,1,0:T(1,128)}), s32[128,1,8]{2,1,0:T(1,128)S(1)}, u32[]{:S(2)}, u32[]{:S(2)}) async-start(s32[128,1,8]{2,1,0:T(1,128)} %bitcast.5), calls=%async_computation | async-start | bytes 131072 | tf_op jit(solution)/shard_map/all_to_all | solution.py:162
  26.4 14.9 %all-to-all-done = s32[128,1,8]{2,1,0:T(1,128)S(1)} async-done(((s32[128,1,8]{2,1,0:T(1,128)}), s32[128,1,8]{2,1,0:T(1,128)S(1)}, u32[]{:S(2)}, u32[]{:S(2)}) %all-to-all-start) | async-done | bytes 4128 | tf_op jit(solution)/shard_map/all_to_all | solution.py:162
  42.0 4.3 %all-to-all-start.1 = ((bf16[4,256,128]{1,2,0:T(8,128)(2,1)}), bf16[4,256,128]{1,2,0:T(8,128)(2,1)S(1)}, u32[]{:S(2)}, u32[]{:S(2)}) async-start(bf16[4,256,128]{1,2,0:T(8,128)(2,1)} %broadcast_in_dim.85), calls=%async_computation.1 | async-start | bytes 524288 | tf_op jit(solution)/shard_map/all_to_all | solution.py:23
  46.4 5.4 %all-to-all-done.1 = bf16[4,256,128]{1,2,0:T(8,128)(2,1)S(1)} async-done(((bf16[4,256,128]{1,2,0:T(8,128)(2,1)}), bf16[4,256,128]{1,2,0:T(8,128)(2,1)S(1)}, u32[]{:S(2)}, u32[]{:S(2)}) %all-to-all-start.1) | async-done | bytes 262176 | tf_op jit(solution)/shard_map/all_to_all | solution.py:23
  52.5 3.3 %all-to-all-start.3 = ((bf16[4,64,128]{2,1,0:T(8,128)(2,1)}), bf16[4,64,128]{2,1,0:T(8,128)(2,1)S(1)}, u32[]{:S(2)}, u32[]{:S(2)}) async-start(bf16[4,64,128]{2,1,0:T(8,128)(2,1)} %broadcast_in_dim.87), calls=%async_computation.3 | async-start | bytes 131072 | tf_op jit(solution)/shard_map/all_to_all | solution.py:23
  56.2 3.7 %scatter_custom_fusion.1 = bf16[1024,128]{1,0:T(8,128)(2,1)} fusion(s32[512]{0:T(512)S(1)} %bitcast.138, bf16[256,128]{1,0:T(8,128)(2,1)S(1)} %copy.75, s32[1024]{0:T(1024)S(1)} %pad_clamp_fusion.1, bf16[]{:T(256)} %constant.20.clone.1), kind=kCustom, calls=%fused_computation.50 | custom fusion | bytes 262146 | tf_op jit(solution)/shard_map/scatter | solution.py:153
  60.2 9.2 %all-to-all-start.2 = ((bf16[128,8,128]{2,1,0:T(8,128)(2,1)}), bf16[128,8,128]{2,1,0:T(8,128)(2,1)S(1)}, u32[]{:S(2)}, u32[]{:S(2)}) async-start(bf16[128,8,128]{2,1,0:T(8,128)(2,1)} %bitcast.9), calls=%async_computation.2 | async-start | bytes 524288 | tf_op jit(solution)/shard_map/all_to_all | solution.py:155
  70.3 2.8 %gather_fusion = f32[1024,128]{1,0:T(8,128)S(1)} fusion(f32[64,128]{1,0:T(8,128)S(1)} %convolution_bitcast_fusion.3, s32[1024]{0:T(1024)S(1)} %broadcast_clamp_fusion), kind=kCustom, calls=%fused_computation.1 | custom fusion | bytes 1052672 | tf_op jit(solution)/shard_map/gather | solution.py:169
  73.1 18.8 %all-to-all-done.2 = bf16[128,8,128]{2,1,0:T(8,128)(2,1)S(1)} async-done(((bf16[128,8,128]{2,1,0:T(8,128)(2,1)}), bf16[128,8,128]{2,1,0:T(8,128)(2,1)S(1)}, u32[]{:S(2)}, u32[]{:S(2)}) %all-to-all-start.2) | async-done | bytes 262176 | tf_op jit(solution)/shard_map/all_to_all | solution.py:155
  91.9 6.2 %scatter_custom_fusion.2 = f32[64,128]{1,0:T(8,128)S(1)} fusion(s32[1024]{0:T(1024)S(1)} %reshape.233, f32[1024,128]{1,0:T(8,128)S(1)} %gather_fusion, bf16[128,8,128]{2,1,0:T(8,128)(2,1)S(1)} %all-to-all-done.2, f32[]{:T(128)} %constant.14.clone.1, f32[]{:T(128)} %constant.11.clone.1, f32[128]{0:T(128)S(1)} %copy-done.7, pred[1024]{0:T(1024)(128)(4,1)S(1)} %lt.44), kind=kCustom, calls=%fused_computation.35 | custom fusion | flops 1179648 | bytes 822272 | tf_op jit(solution)/shard_map/scatter-add | solution.py:171
  98.2 7.3 %all_to_all.89 = bf16[4,64,128]{2,1,0:T(8,128)(2,1)S(1)} all-to-all(bf16[4,64,128]{2,1,0:T(8,128)(2,1)S(1)} %broadcast_in_dim.89), channel_id=1, replica_groups=mesh['patch_0'=4,'patch_1'=16,'patch_2'=2,'chan'=4] {'chan'}, dimensions={0} | all-to-all | bytes 131072 | tf_op jit(solution)/shard_map/all_to_all | solution.py:23
  105.8 6.5 %all_to_all.90 = f32[4,1,128]{2,1,0:T(1,128)S(1)} all-to-all(f32[4,1,128]{2,1,0:T(1,128)S(1)} %broadcast_in_dim.90), channel_id=1, replica_groups=mesh['patch_0'=4,'patch_1'=16,'patch_2'=2,'chan'=4] {'chan'}, dimensions={0} | all-to-all | bytes 4096 | tf_op jit(solution)/shard_map/all_to_all | solution.py:23
  113.3 6.5 %all_to_all.91 = f32[4,1,128]{2,1,0:T(1,128)S(1)} all-to-all(f32[4,1,128]{2,1,0:T(1,128)S(1)} %broadcast_in_dim.94), channel_id=1, replica_groups=mesh['patch_0'=4,'patch_1'=16,'patch_2'=2,'chan'=4] {'chan'}, dimensions={0} | all-to-all | bytes 4096 | tf_op jit(solution)/shard_map/all_to_all | solution.py:23
  121.2 3.3 %all-to-all-start.7 = ((bf16[4,64,128]{2,1,0:T(8,128)(2,1)}), bf16[4,64,128]{2,1,0:T(8,128)(2,1)S(1)}, u32[]{:S(2)}, u32[]{:S(2)}) async-start(bf16[4,64,128]{2,1,0:T(8,128)(2,1)} %broadcast_in_dim.95), calls=%async_computation.7 | async-start | bytes 131072 | tf_op jit(solution)/shard_map/all_to_all | solution.py:23
  124.7 4.3 %all-to-all-done.7 = bf16[4,64,128]{2,1,0:T(8,128)(2,1)S(1)} async-done(((bf16[4,64,128]{2,1,0:T(8,128)(2,1)}), bf16[4,64,128]{2,1,0:T(8,128)(2,1)S(1)}, u32[]{:S(2)}, u32[]{:S(2)}) %all-to-all-start.7) | async-done | bytes 65568 | tf_op jit(solution)/shard_map/all_to_all | solution.py:23
  129.1 2.8 %gather_fusion.1 = f32[1024,128]{1,0:T(8,128)S(1)} fusion(f32[64,128]{1,0:T(8,128)S(1)} %fusion.27, s32[1024]{0:T(1024)S(1)} %broadcast_clamp_fusion), kind=kCustom, calls=%fused_computation.2 | custom fusion | bytes 1052672 | tf_op jit(solution)/shard_map/gather | solution.py:201
  133.0 12.3 %all-to-all-start.8 = ((bf16[128,8,128]{2,1,0:T(8,128)(2,1)}), bf16[128,8,128]{2,1,0:T(8,128)(2,1)S(1)}, u32[]{:S(2)}, u32[]{:S(2)}) async-start(bf16[128,8,128]{2,1,0:T(8,128)(2,1)} %get-tuple-element.14), calls=%async_computation.8 | async-start | bytes 524288 | tf_op jit(solution)/shard_map/all_to_all | solution.py:209
  145.3 6.8 %scatter_custom_fusion.4 = f32[64,128]{1,0:T(8,128)S(1)} fusion(s32[1024]{0:T(1024)S(1)} %reshape.233, f32[1024,128]{1,0:T(8,128)S(1)} %gather_fusion.1, f32[1024,128]{1,0:T(8,128)S(1)} %gather_fusion, bf16[128,8,128]{2,1,0:T(8,128)(2,1)S(1)} %all-to-all-done.2, f32[]{:T(128)} %constant.14.clone.1, f32[]{:T(128)} %constant.11.clone.1, ...), kind=kCustom, calls=%fused_computation.32 | custom fusion | flops 1835008 | bytes 1346560 | tf_op jit(solution)/shard_map/scatter-add | solution.py:206
  152.4 15.4 %all-to-all-done.8 = bf16[128,8,128]{2,1,0:T(8,128)(2,1)S(1)} async-done(((bf16[128,8,128]{2,1,0:T(8,128)(2,1)}), bf16[128,8,128]{2,1,0:T(8,128)(2,1)S(1)}, u32[]{:S(2)}, u32[]{:S(2)}) %all-to-all-start.8) | async-done | bytes 262176 | tf_op jit(solution)/shard_map/all_to_all | solution.py:209
  167.8 3.5 %scatter_custom_fusion.3 = f32[256,128]{1,0:T(8,128)S(1)} fusion(s32[512]{0:T(512)S(1)} %copy-done.9, f32[]{:T(128)} %constant.14.clone.1, bf16[1024,128]{1,0:T(8,128)(2,1)S(1)} %bitcast.133, s32[1024]{0:T(1024)S(1)} %pad_clamp_fusion), kind=kCustom, calls=%fused_computation.42 | custom fusion | flops 131072 | bytes 397316 | tf_op jit(solution)/shard_map/scatter-add | solution.py:217
  172.9 6.3 %all_to_all.92 = f32[2,64,1538]{2,1,0:T(8,128)S(1)} all-to-all(f32[2,64,1538]{2,1,0:T(8,128)S(1)} %copy.86), channel_id=1, replica_groups=mesh['patch_0'=4,'patch_1'=16,'patch_2'=2,'chan'=4] {'patch_2'}, dimensions={0} | all-to-all | bytes 1574912 | tf_op jit(solution)/shard_map/all_to_all | solution.py:63
  179.9 3.3 %all-to-all-start.10 = ((bf16[4,64,128]{2,1,0:T(8,128)(2,1)}), bf16[4,64,128]{2,1,0:T(8,128)(2,1)S(1)}, u32[]{:S(2)}, u32[]{:S(2)}) async-start(bf16[4,64,128]{2,1,0:T(8,128)(2,1)} %broadcast_in_dim.98), calls=%async_computation.10 | async-start | bytes 131072 | tf_op jit(solution)/shard_map/all_to_all | solution.py:23
  183.2 1.0 all_to_all.69
  184.3 3.3 %all-to-all-done.10 = bf16[4,64,128]{2,1,0:T(8,128)(2,1)S(1)} async-done(((bf16[4,64,128]{2,1,0:T(8,128)(2,1)}), bf16[4,64,128]{2,1,0:T(8,128)(2,1)S(1)}, u32[]{:S(2)}, u32[]{:S(2)}) %all-to-all-start.10) | async-done | bytes 65568 | tf_op jit(solution)/shard_map/all_to_all | solution.py:23
  187.6 4.6 %all-to-all-start.12 = ((f32[64,1,1538]{2,1,0:T(1,128)}), f32[64,1,1538]{2,1,0:T(1,128)S(1)}, u32[]{:S(2)}, u32[]{:S(2)}) async-start(f32[64,1,1538]{2,1,0:T(1,128)} %all_to_all.69), calls=%async_computation.12 | async-start | bytes 851968 | tf_op jit(solution)/shard_map/all_to_all | solution.py:71
  192.3 25.1 %all-to-all-done.12 = f32[64,1,1538]{2,1,0:T(1,128)S(1)} async-done(((f32[64,1,1538]{2,1,0:T(1,128)}), f32[64,1,1538]{2,1,0:T(1,128)S(1)}, u32[]{:S(2)}, u32[]{:S(2)}) %all-to-all-start.12) | async-done | bytes 393760 | tf_op jit(solution)/shard_map/all_to_all | solution.py:71
  218.2 3.6 %all-to-all-start.9 = ((bf16[4,256,128]{1,2,0:T(8,128)(2,1)}), bf16[4,256,128]{1,2,0:T(8,128)(2,1)S(1)}, u32[]{:S(2)}, u32[]{:S(2)}) async-start(bf16[4,256,128]{1,2,0:T(8,128)(2,1)} %broadcast_in_dim.97), calls=%async_computation.9 | async-start | bytes 524288 | tf_op jit(solution)/shard_map/all_to_all | solution.py:23
  222.1 5.0 %all-to-all-done.9 = bf16[4,256,128]{1,2,0:T(8,128)(2,1)S(1)} async-done(((bf16[4,256,128]{1,2,0:T(8,128)(2,1)}), bf16[4,256,128]{1,2,0:T(8,128)(2,1)S(1)}, u32[]{:S(2)}, u32[]{:S(2)}) %all-to-all-start.9) | async-done | bytes 262176 | tf_op jit(solution)/shard_map/all_to_all | solution.py:23
  228.0 8.4 %all-to-all-start.13 = ((f32[64,1,1538]{2,1,0:T(1,128)}), f32[64,1,1538]{2,1,0:T(1,128)S(1)}, u32[]{:S(2)}, u32[]{:S(2)}) async-start(f32[64,1,1538]{2,1,0:T(1,128)} %broadcast_in_dim.99), calls=%async_computation.13 | async-start | bytes 851968 | tf_op jit(solution)/shard_map/all_to_all | solution.py:23
  238.2 22.0 %all-to-all-done.13 = f32[64,1,1538]{2,1,0:T(1,128)S(1)} async-done(((f32[64,1,1538]{2,1,0:T(1,128)}), f32[64,1,1538]{2,1,0:T(1,128)S(1)}, u32[]{:S(2)}, u32[]{:S(2)}) %all-to-all-start.13) | async-done | bytes 393760 | tf_op jit(solution)/shard_map/all_to_all | solution.py:23
  260.3 9.0 %all_to_all.93 = f32[2,64,1538]{2,1,0:T(8,128)S(1)} all-to-all(f32[2,64,1538]{2,1,0:T(8,128)S(1)} %broadcast_in_dim.100), channel_id=1, replica_groups=mesh['patch_0'=4,'patch_1'=16,'patch_2'=2,'chan'=4] {'patch_2'}, dimensions={0} | all-to-all | bytes 1574912 | tf_op jit(solution)/shard_map/all_to_all | solution.py:23
  (92 shorter events, 19.9 us)
Async XLA Ops:
  0.6 55.2 %copy-start = (bf16[512,512]{1,0:T(8,128)(2,1)S(1)}, bf16[512,512]{1,0:T(8,128)(2,1)}, u32[]{:S(2)}) copy-start(bf16[512,512]{1,0:T(8,128)(2,1)} %param.13) | copy-start | bytes 1572868
  1.5 0.7 copy-start.6
  5.8 20.5 %copy-start.5 = (bf16[256,128]{1,0:T(8,128)(2,1)S(1)}, bf16[256,128]{1,0:T(8,128)(2,1)}, u32[]{:S(2)}) copy-start(bf16[256,128]{1,0:T(8,128)(2,1)} %param.11) | copy-start | bytes 196612
  5.8 35.5 %all-to-all-start = ((s32[128,1,8]{2,1,0:T(1,128)}), s32[128,1,8]{2,1,0:T(1,128)S(1)}, u32[]{:S(2)}, u32[]{:S(2)}) async-start(s32[128,1,8]{2,1,0:T(1,128)} %bitcast.5), calls=%async_computation | async-start | bytes 131072 | tf_op jit(solution)/shard_map/all_to_all | solution.py:162
  42.0 4.3 %copy-start.9 = (s32[512]{0:T(512)S(1)}, s32[512]{0:T(512)}, u32[]{:S(2)}) copy-start(s32[512]{0:T(512)} %param.18) | copy-start | bytes 6148
  42.0 9.8 %all-to-all-start.1 = ((bf16[4,256,128]{1,2,0:T(8,128)(2,1)}), bf16[4,256,128]{1,2,0:T(8,128)(2,1)S(1)}, u32[]{:S(2)}, u32[]{:S(2)}) async-start(bf16[4,256,128]{1,2,0:T(8,128)(2,1)} %broadcast_in_dim.85), calls=%async_computation.1 | async-start | bytes 524288 | tf_op jit(solution)/shard_map/all_to_all | solution.py:23
  46.4 5.5 %copy-start.4 = (bf16[64,128]{1,0:T(8,128)(2,1)S(1)}, bf16[64,128]{1,0:T(8,128)(2,1)}, u32[]{:S(2)}) copy-start(bf16[64,128]{1,0:T(8,128)(2,1)} %param.12) | copy-start | bytes 49156
  52.5 7.7 %all-to-all-start.3 = ((bf16[4,64,128]{2,1,0:T(8,128)(2,1)}), bf16[4,64,128]{2,1,0:T(8,128)(2,1)S(1)}, u32[]{:S(2)}, u32[]{:S(2)}) async-start(bf16[4,64,128]{2,1,0:T(8,128)(2,1)} %broadcast_in_dim.87), calls=%async_computation.3 | async-start | bytes 131072 | tf_op jit(solution)/shard_map/all_to_all | solution.py:23
  59.8 10.3 %copy-start.3 = (bf16[512,512]{1,0:T(8,128)(2,1)S(1)}, bf16[512,512]{1,0:T(8,128)(2,1)}, u32[]{:S(2)}) copy-start(bf16[512,512]{1,0:T(8,128)(2,1)} %param.14) | copy-start | bytes 1572868
  60.2 31.7 %all-to-all-start.2 = ((bf16[128,8,128]{2,1,0:T(8,128)(2,1)}), bf16[128,8,128]{2,1,0:T(8,128)(2,1)S(1)}, u32[]{:S(2)}, u32[]{:S(2)}) async-start(bf16[128,8,128]{2,1,0:T(8,128)(2,1)} %bitcast.9), calls=%async_computation.2 | async-start | bytes 524288 | tf_op jit(solution)/shard_map/all_to_all | solution.py:155
  70.3 21.6 %copy-start.7 = (f32[128]{0:T(128)S(1)}, f32[128]{0:T(128)}, u32[]{:S(2)}) copy-start(f32[128]{0:T(128)} %param.16) | copy-start | bytes 1540
  73.1 32.4 %copy-start.2 = (bf16[512,512]{1,0:T(8,128)(2,1)S(1)}, bf16[512,512]{1,0:T(8,128)(2,1)}, u32[]{:S(2)}) copy-start(bf16[512,512]{1,0:T(8,128)(2,1)} %param.15) | copy-start | bytes 1572868
  105.7 6.7 %copy-start.1 = (bf16[64,128]{1,0:T(8,128)(2,1)S(1)}, bf16[64,128]{1,0:T(8,128)(2,1)}, u32[]{:S(2)}) copy-start(bf16[64,128]{1,0:T(8,128)(2,1)} %param.21) | copy-start | bytes 49156
  112.4 0.7 copy-start.8
  121.2 7.7 %all-to-all-start.7 = ((bf16[4,64,128]{2,1,0:T(8,128)(2,1)}), bf16[4,64,128]{2,1,0:T(8,128)(2,1)S(1)}, u32[]{:S(2)}, u32[]{:S(2)}) async-start(bf16[4,64,128]{2,1,0:T(8,128)(2,1)} %broadcast_in_dim.95), calls=%async_computation.7 | async-start | bytes 131072 | tf_op jit(solution)/shard_map/all_to_all | solution.py:23
  133.0 34.8 %all-to-all-start.8 = ((bf16[128,8,128]{2,1,0:T(8,128)(2,1)}), bf16[128,8,128]{2,1,0:T(8,128)(2,1)S(1)}, u32[]{:S(2)}, u32[]{:S(2)}) async-start(bf16[128,8,128]{2,1,0:T(8,128)(2,1)} %get-tuple-element.14), calls=%async_computation.8 | async-start | bytes 524288 | tf_op jit(solution)/shard_map/all_to_all | solution.py:209
  179.9 7.7 %all-to-all-start.10 = ((bf16[4,64,128]{2,1,0:T(8,128)(2,1)}), bf16[4,64,128]{2,1,0:T(8,128)(2,1)S(1)}, u32[]{:S(2)}, u32[]{:S(2)}) async-start(bf16[4,64,128]{2,1,0:T(8,128)(2,1)} %broadcast_in_dim.98), calls=%async_computation.10 | async-start | bytes 131072 | tf_op jit(solution)/shard_map/all_to_all | solution.py:23
  187.6 29.8 %all-to-all-start.12 = ((f32[64,1,1538]{2,1,0:T(1,128)}), f32[64,1,1538]{2,1,0:T(1,128)S(1)}, u32[]{:S(2)}, u32[]{:S(2)}) async-start(f32[64,1,1538]{2,1,0:T(1,128)} %all_to_all.69), calls=%async_computation.12 | async-start | bytes 851968 | tf_op jit(solution)/shard_map/all_to_all | solution.py:71
  218.2 8.9 %all-to-all-start.9 = ((bf16[4,256,128]{1,2,0:T(8,128)(2,1)}), bf16[4,256,128]{1,2,0:T(8,128)(2,1)S(1)}, u32[]{:S(2)}, u32[]{:S(2)}) async-start(bf16[4,256,128]{1,2,0:T(8,128)(2,1)} %broadcast_in_dim.97), calls=%async_computation.9 | async-start | bytes 524288 | tf_op jit(solution)/shard_map/all_to_all | solution.py:23
  228.0 32.1 %all-to-all-start.13 = ((f32[64,1,1538]{2,1,0:T(1,128)}), f32[64,1,1538]{2,1,0:T(1,128)S(1)}, u32[]{:S(2)}, u32[]{:S(2)}) async-start(f32[64,1,1538]{2,1,0:T(1,128)} %broadcast_in_dim.99), calls=%async_computation.13 | async-start | bytes 851968 | tf_op jit(solution)/shard_map/all_to_all | solution.py:23
where the time goes:
time: 274 us; the launch traced here: 273 us
  waiting for transfers between devices  115 us (42%)
  starting transfers between devices  72.8 us (27%)
  blocking collectives  35.5 us (13%)
  local copies, waits for them, and re-layouts  25.4 us (9%)
  other arithmetic  20.3 us (7%)
  matrix products  3.33 us (1%)
    all_to_all x6, waiting for transfers between devices, from_everyone(): return lax.all_to_all(copies, axis, split_axis=0, concat_axis=0, tiled=True)  40.5 us
    all_to_all x4, blocking collectives, from_everyone(): return lax.all_to_all(copies, axis, split_axis=0, concat_axis=0, tiled=True)  29.3 us
    all_to_all x6, starting transfers between devices, from_everyone(): return lax.all_to_all(copies, axis, split_axis=0, concat_axis=0, tiled=True)  26.2 us
    all_to_all x1, waiting for transfers between devices, sum_by_axis(): lax.all_to_all(nearer, far, split_axis=0, concat_axis=0, tiled=True)  25.1 us
    all_to_all x1, starting transfers between devices, on_device(): lax.all_to_all(targets.reshape(patches, capacity), PATCH, split_axis=0, c...  20.5 us
    all_to_all x1, waiting for transfers between devices, on_device(): lax.all_to_all(outgoing.reshape(patches, capacity, slice_width), PATCH, s...  18.8 us
    all_to_all x1, waiting for transfers between devices, on_device(): lax.all_to_all(grad_pre.reshape(patches, capacity, slice_width), PATCH, s...  15.4 us
    all_to_all x1, waiting for transfers between devices, on_device(): lax.all_to_all(targets.reshape(patches, capacity), PATCH, split_axis=0, c...  14.9 us
  transfers between devices with their start and end apart: 10, of which 10 were waited for; matrix products, arithmetic and copies ran while one was open for 6% of the time, Pallas kernels for 0%

commit v1 on v0

v1 whole, which is shorter than its diff:
```python
import jax
import jax.numpy as jnp
from jax import lax
from jax.experimental import pallas as pl
from jax.sharding import Mesh
from jax.sharding import PartitionSpec as P

FAR = ("x", "z")
PATCH = ("x", "z", "c")
BF = jnp.bfloat16
F32 = jnp.float32

NORM_EPS = 1e-05
LANES = 128
CAP = 8
CHANS = 4
GRID = 256
MESH = 64
EDGES = 512
PATCHES = 128
LATENT = CHANS * LANES
SLOTS = PATCHES * CAP
HALF = CAP // 2 * LANES
COT_AT = GRID
MESH_AT = COT_AT + MESH
GAIN_AT = MESH_AT + MESH
PACK = GAIN_AT + 16
FARS = 64
WEIGHT_BLOCKS = LATENT // FARS
HALF_BLOCKS = 3 * WEIGHT_BLOCKS // 2
PARAM_COLS = (HALF_BLOCKS + 2) * LANES


def dot(a, b, dims=((1,), (0,))):
    return lax.dot_general(a, b, (dims, ((), ())), preferred_element_type=F32)


def two_parts(v):
    high = v.astype(BF)
    return high, (v - high.astype(F32)).astype(BF)


def iota(shape, dim):
    return lax.broadcasted_iota(jnp.int32, shape, dim)


def cols(j):
    return slice(j * LANES, (j + 1) * LANES)


def call(kernel, outs, args, flops):
    shapes = tuple(jax.ShapeDtypeStruct(s, d) for s, d in outs)
    return pl.pallas_call(
        kernel,
        out_shape=shapes,
        cost_estimate=pl.CostEstimate(flops=flops, bytes_accessed=1 << 20, transcendentals=0),
        name=kernel.__name__,
    )(*args)


def pack_kernel(grid, cot, mesh, gain, out):
    high, rest = two_parts(gain[...])
    left = gain[...] - high.astype(F32)
    low = left - rest.astype(F32)
    row = iota((16, LANES), 0)
    parts = jnp.where(
        row == 0,
        high.astype(F32),
        jnp.where(row == 1, rest.astype(F32), jnp.where(row == 2, low, 0.0)),
    )
    for j in range(CHANS):
        out[j, 0:GRID] = grid[...]
        out[j, COT_AT:MESH_AT] = cot[...]
        out[j, MESH_AT:GAIN_AT] = mesh[...]
        out[j, GAIN_AT:PACK] = parts.astype(BF)


def slot_kernel(patch_col, patch_row, source, node, pick, meta):
    before = iota((EDGES, EDGES), 0) < iota((EDGES, EDGES), 1)
    same = patch_col[...] == patch_row[...]
    rank = jnp.sum(jnp.where(same & before, 1.0, 0.0), axis=0, keepdims=True)
    slot = rank.astype(jnp.int32) * PATCHES + patch_row[...]
    here = jnp.where(iota((SLOTS, EDGES), 0) == slot, 1.0, 0.0).astype(BF)
    row = iota((8, EDGES), 0)
    facts = jnp.where(
        row == 0, source[...], jnp.where(row == 1, node[...], jnp.where(row == 2, 1, 0))
    )
    found = dot(here, facts.astype(F32).astype(BF), ((1,), (1,)))
    live = found[:, 2:3] > 0.5
    from_row = jnp.where(live, found[:, 0:1], -1.0).astype(jnp.int32)
    pick[...] = jnp.where(iota((SLOTS, GRID), 1) == from_row, 1.0, 0.0).astype(BF)
    to_node = jnp.where(live, found[:, 1:2], float(MESH))
    lane = iota((PATCHES, LANES), 1)
    listed = jnp.zeros((PATCHES, LANES), F32)
    for r in range(CAP):
        listed = jnp.where(lane == r, to_node[r * PATCHES : (r + 1) * PATCHES], listed)
    meta[...] = listed.astype(BF)


def slot_at(r):
    at = r // (CAP // 2) * (HALF + LANES) + r % (CAP // 2) * LANES
    return slice(at, at + LANES)


def send_kernel(packed, pick, meta, source_cols, dest_cols, out, mesh_proj):
    projected = jnp.zeros((GRID, LANES), F32)
    landed = jnp.zeros((MESH, LANES), F32)
    for j in range(CHANS):
        projected += dot(packed[j, 0:GRID], source_cols[cols(j)])
        landed += dot(packed[j, MESH_AT:GAIN_AT], dest_cols[cols(j)])
    mesh_proj[...] = landed
    projected = projected.astype(BF)
    for r in range(CAP):
        rows = pick[r * PATCHES : (r + 1) * PATCHES]
        out[:, slot_at(r)] = dot(rows, projected).astype(BF)
    out[:, HALF : HALF + LANES] = meta[...]
    out[:, 2 * HALF + LANES : 2 * HALF + 2 * LANES] = jnp.zeros((PATCHES, LANES), BF)


def message_kernel(arrived, mesh_proj, bias, summed, pre, chosen):
    high, low = two_parts(mesh_proj[...])
    both = jnp.concatenate([high, low], axis=1)
    total = jnp.zeros((MESH, 2 * LANES), F32)
    for r in range(CAP):
        at = slice(r * PATCHES, (r + 1) * PATCHES)
        node = arrived[:, HALF + r : HALF + r + 1].astype(F32).astype(jnp.int32)
        mine = jnp.where(iota((PATCHES, MESH), 1) == node, 1.0, 0.0).astype(BF)
        chosen[at] = mine
        there = dot(mine, both)
        value = (
            arrived[:, slot_at(r)].astype(F32)
            + (there[:, 0:LANES] + there[:, LANES : 2 * LANES])
            + bias[...]
        )
        pre[at] = value
        message = value * jax.nn.sigmoid(value)
        total += dot(mine, jnp.concatenate(two_parts(message), axis=1), ((0,), (0,)))
    done = (total[:, 0:LANES] + total[:, LANES : 2 * LANES]).astype(BF)
    for j in range(CHANS):
        summed[j] = done


def node_kernel(
    packed,
    summed,
    pre,
    chosen,
    w_out,
    out_cols,
    out_rows,
    mesh,
    cot,
    gain,
    updated,
    grads,
    node_grad,
    dest_part,
    out_part,
    bias_part,
    gain_part,
):
    mixed = jnp.zeros((MESH, LATENT), F32)
    own = jnp.zeros((MESH, LANES), F32)
    for j in range(CHANS):
        mixed += dot(summed[j], w_out[cols(j)])
        own += dot(summed[j], out_cols[cols(j)])
    mean = jnp.sum(mixed, axis=1, keepdims=True) / LATENT
    apart = mixed - mean
    inv = lax.rsqrt(jnp.sum(apart * apart, axis=1, keepdims=True) / LATENT + NORM_EPS)
    normed = apart * inv
    scaled, first, second = [], 0.0, 0.0
    for j in range(CHANS):
        parts = packed[j, GAIN_AT:PACK].astype(F32)
        whole = parts[0:1] + parts[1:2] + parts[2:3]
        part = packed[j, COT_AT:MESH_AT].astype(F32) * whole
        scaled.append(part)
        first += jnp.sum(part, axis=1, keepdims=True)
        second += jnp.sum(part * normed[:, cols(j)], axis=1, keepdims=True)
    first, second = first / LATENT, second / LATENT
    own_normed = (own - mean) * inv
    cotangent = cot[...].astype(F32)
    updated[...] = (mesh[...].astype(F32) + own_normed * gain[...]).astype(BF)
    gain_part[...] = jnp.sum(cotangent * own_normed, axis=0, keepdims=True)
    own_grad = ((cotangent * gain[...] - first - own_normed * second) * inv).astype(BF)
    back = jnp.zeros((MESH, LANES), F32)
    for j in range(CHANS):
        out_part[cols(j)] = dot(summed[j], own_grad, ((0,), (0,))).astype(BF)
        part = ((scaled[j] - first - normed[:, cols(j)] * second) * inv).astype(BF)
        back += dot(part, out_rows[:, cols(j)], ((1,), (1,)))
    both = jnp.concatenate(two_parts(back), axis=1)
    bias = jnp.zeros((1, LANES), F32)
    total = jnp.zeros((MESH, LANES), F32)
    for r in range(CAP):
        at = slice(r * PATCHES, (r + 1) * PATCHES)
        mine = chosen[at]
        there = dot(mine, both)
        value = pre[at]
        gate = jax.nn.sigmoid(value)
        slope = gate * (1.0 + value * (1.0 - gate))
        grad = ((there[:, 0:LANES] + there[:, LANES : 2 * LANES]) * slope).astype(BF)
        grads[:, cols(r)] = grad
        bias += jnp.sum(grad.astype(F32), axis=0, keepdims=True)
        total += dot(mine, grad, ((0,), (0,)))
    bias_part[...] = bias
    total = total.astype(BF)
    node_grad[...] = total
    for j in range(CHANS):
        dest_part[cols(j)] = dot(packed[j, MESH_AT:GAIN_AT], total, ((0,), (0,))).astype(BF)


def grid_kernel(
    returned, pick, packed, node_grad, dest_part, out_part, bias_part, gain_part, out, params
):
    total = jnp.zeros((GRID, LANES), F32)
    for r in range(CAP):
        rows = pick[r * PATCHES : (r + 1) * PATCHES]
        total += dot(rows, returned[:, cols(r)], ((0,), (0,)))
    total = total.astype(BF)
    for j in range(CHANS):
        out[j, 0:GRID] = total
        out[j, GRID : GRID + MESH] = node_grad[...]
    blocks = []
    for j in range(CHANS):
        part = dot(packed[j, 0:GRID], total, ((0,), (0,))).astype(BF)
        blocks += [part[0:FARS], part[FARS : 2 * FARS]]
    for whole in (dest_part, out_part):
        blocks += [whole[b * FARS : (b + 1) * FARS] for b in range(WEIGHT_BLOCKS)]
    for b, block in enumerate(blocks):
        params[b // HALF_BLOCKS, :, cols(b % HALF_BLOCKS)] = block
    head = iota((FARS, LANES), 0) == 0
    for half, small in enumerate((bias_part, gain_part)):
        for k, part in enumerate(two_parts(small[...])):
            spread = jnp.where(head, part.astype(F32), 0.0)
            params[half, :, cols(HALF_BLOCKS + k)] = spread.astype(BF)


def back_kernel(gathered, source_rows, dest_rows, cot, grad_grid, grad_mesh):
    on_grid = jnp.zeros((GRID, LANES), F32)
    on_mesh = cot[...].astype(F32)
    for j in range(CHANS):
        on_grid += dot(gathered[j, 0:GRID], source_rows[:, cols(j)], ((1,), (1,)))
        on_mesh += dot(gathered[j, GRID : GRID + MESH], dest_rows[:, cols(j)], ((1,), (1,)))
    grad_grid[...] = on_grid.astype(BF)
    grad_mesh[...] = on_mesh.astype(BF)


def pair_kernel(params, out):
    total = params[0].astype(F32) + params[1].astype(F32)
    small = total[:, cols(HALF_BLOCKS)] + total[:, cols(HALF_BLOCKS + 1)]
    out[:, 0 : HALF_BLOCKS * LANES] = total[:, 0 : HALF_BLOCKS * LANES].astype(BF)
    for k, part in enumerate(two_parts(small)):
        out[:, cols(HALF_BLOCKS + k)] = part


def unpack_kernel(params, source, dest, out, bias, gain):
    for b in range(3 * WEIGHT_BLOCKS):
        block = params[b // HALF_BLOCKS, :, cols(b % HALF_BLOCKS)].astype(F32)
        at = b % WEIGHT_BLOCKS * FARS
        (source, dest, out)[b // WEIGHT_BLOCKS][at : at + FARS] = block
    for half, small in enumerate((bias, gain)):
        high = params[half, 0:1, cols(HALF_BLOCKS)].astype(F32)
        small[...] = high + params[half, 0:1, cols(HALF_BLOCKS + 1)].astype(F32)


def gather_stage(st):
    args = (st["grid_latent"], st["cotangent"], st["mesh_latent"], st["norm_gain"][None])
    (st["sent"],) = call(pack_kernel, [((CHANS, PACK, LANES), BF)], args, 1 << 20)
    return st


def send_stage(st):
    offset = st["chan"] * LANES
    st["packed"] = st["got"]
    for name in ("source", "dest", "out"):
        whole = st["w_" + name]
        st[name + "_cols"] = lax.dynamic_slice_in_dim(whole, offset, LANES, 1)
        st[name + "_rows"] = lax.dynamic_slice_in_dim(whole, offset, LANES, 0)
    patch = st["edge_patch"]
    args = (patch, patch.reshape(1, EDGES), st["edge_source"][None], st["edge_node"][None])
    outs = [((SLOTS, GRID), BF), ((PATCHES, LANES), BF)]
    st["pick"], meta = call(slot_kernel, outs, args, 1 << 27)
    args = (st["packed"], st["pick"], meta, st["source_cols"], st["dest_cols"])
    outs = [((PATCHES, 2 * HALF + 2 * LANES), BF), ((MESH, LANES), F32)]
    sent, st["mesh_proj"] = call(send_kernel, outs, args, 1 << 28)
    st["sent"] = sent.reshape(PATCHES, 2, HALF + LANES)
    return st


def message_stage(st):
    arrived = st["got"].reshape(PATCHES, 2 * HALF + 2 * LANES)
    outs = [((CHANS, MESH, LANES), BF), ((SLOTS, LANES), F32), ((SLOTS, MESH), BF)]
    args = (arrived, st["mesh_proj"], st["edge_bias"][None])
    st["sent"], st["pre"], st["chosen"] = call(message_kernel, outs, args, 1 << 27)
    return st


def node_stage(st):
    args = [st["packed"], st["got"], st["pre"], st["chosen"], st["w_out"], st["out_cols"]]
    args += [st["out_rows"], st["mesh_latent"], st["cotangent"], st["norm_gain"][None]]
    outs = [((MESH, LANES), BF), ((PATCHES, 2 * HALF), BF), ((MESH, LANES), BF)]
    outs += [((LATENT, LANES), BF)] * 2 + [((1, LANES), F32)] * 2
    st["updated"], grads, *st["partial"] = call(node_kernel, outs, args, 1 << 28)
    st["sent"] = grads.reshape(PATCHES, 2, HALF)
    return st


def grid_stage(st):
    returned = st["got"].reshape(PATCHES, 2 * HALF)
    outs = [((CHANS, GRID + MESH, LANES), BF), ((2, FARS, PARAM_COLS), BF)]
    args = (returned, st["pick"], st["packed"], *st["partial"])
    st["sent"], st["params"] = call(grid_kernel, outs, args, 1 << 28)
    return st


def back_stage(st):
    args = (st["got"], st["source_rows"], st["dest_rows"], st["cotangent"])
    outs = [((GRID, LANES), BF), ((MESH, LANES), BF)]
    st["grad_grid"], st["grad_mesh"] = call(back_kernel, outs, args, 1 << 26)
    st["sent"] = st["params"]
    return st


def far_stage(st):
    (sent,) = call(pair_kernel, [((FARS, PARAM_COLS), BF)], (st["got"],), 1 << 18)
    st["sent"] = sent.reshape(FARS, 2, PARAM_COLS // 2)
    return st


def sum_stage(st):
    total = jnp.sum(st["got"].astype(F32), axis=0)
    at = PARAM_COLS // 2 - 2 * LANES
    small = total[1:2, at : at + LANES] + total[1:2, at + LANES :]
    high = lax.reduce_precision(small, 8, 7)
    last = jnp.concatenate([total[1:2, :at], high, small - high], axis=1)
    total = jnp.concatenate([total[0:1], last], axis=0).astype(BF)
    st["sent"] = jnp.broadcast_to(total, (FARS, 2, PARAM_COLS // 2))
    return st


def near_stage(st):
    whole = st["got"].reshape(FARS, PARAM_COLS)
    st["sent"] = jnp.broadcast_to(whole, (2, FARS, PARAM_COLS))
    return st


def last_stage(st):
    outs = [((LATENT, LANES), F32)] * 3 + [((1, LANES), F32)] * 2
    *weights, bias, gain = call(unpack_kernel, outs, (st["got"],), 1 << 18)
    st["params"] = (*weights, bias.reshape(LANES), gain.reshape(LANES))
    return st


STAGES = (
    (gather_stage, "y"),
    (send_stage, PATCH),
    (message_stage, "y"),
    (node_stage, PATCH),
    (grid_stage, "y"),
    (back_stage, "c"),
    (far_stage, FAR),
    (sum_stage, FAR),
    (near_stage, "c"),
    (last_stage, None),
)

NAMES = (
    "grid_latent",
    "mesh_latent",
    "w_source",
    "w_dest",
    "w_out",
    "edge_bias",
    "norm_gain",
    "edge_source",
    "edge_patch",
    "edge_node",
    "cotangent",
)


def on_device(*args):
    st = dict(zip(NAMES, args))
    st["chan"] = lax.axis_index("y")
    for stage, axes in STAGES:
        st = stage(st)
        if axes is not None:
            st["got"] = lax.all_to_all(st["sent"], axes, 0, 0, tiled=True)
    return (st["updated"], st["grad_grid"], st["grad_mesh"], *st["params"])


def solution(mesh):
    torus = Mesh(mesh.devices.reshape(4, 16, 2, mesh.shape["chan"]), ("x", "z", "c", "y"))
    by_patch = P(PATCH, "y")
    return jax.shard_map(
        on_device,
        mesh=torus,
        in_specs=(by_patch, by_patch, P(), P(), P(), P("y"), P("y"))
        + (P(PATCH), P(PATCH, None), P(PATCH), by_patch),
        out_specs=(by_patch,) * 3 + (P(None, "y"),) * 3 + (P("y"),) * 2,
        check_vma=False,
    )
```

time: 274 us -> 195 us (0.71)
  waiting for transfers between devices: 115 us -> 50.3 us
  blocking collectives: 35.5 us -> 68 us
  starting transfers between devices: 72.8 us -> 41.5 us
  Pallas kernels: 0 us -> 21.7 us
  other arithmetic: 20.3 us -> 0.25 us
  local copies, waits for them, and re-layouts: 25.4 us -> 11.5 us
  matrix products: 3.33 us -> 0 us
    all_to_all x10 -> x5, waiting for transfers between devices: 115 us -> 50.3 us  [on_device(): st['got'] = lax.all_to_all(st['sent'], axes, 0, 0, tiled=True)]
    all_to_all x5 -> x4, blocking collectives: 35.5 us -> 68 us  [on_device(): st['got'] = lax.all_to_all(st['sent'], axes, 0, 0, tiled=True)]
    all_to_all x10 -> x5, starting transfers between devices: 72.8 us -> 41.5 us  [on_device(): st['got'] = lax.all_to_all(st['sent'], axes, 0, 0, tiled=True)]
    pallas_call x0 -> x9, Pallas kernels: none -> 21.7 us  [call(): pl.pallas_call(kernel, out_shape=shapes, cost_estimate=pl.CostEstimate(fl...]
    scatter-add x3 -> x0, other arithmetic: 16.5 us -> none  [the longest x1 6.78 us: on_device(): jax.ops.segment_sum(grad_edges, safe_node, num_segments=mesh_count)]
    scatter x2 -> x0, local copies, waits for them, and re-layouts: 6.27 us -> none  [the longest x1 3.67 us: on_device(): outgoing = empty_rows.at[slot_index].set(projected[edge_source])]
    gather x2 -> x0, local copies, waits for them, and re-layouts: 5.63 us -> none  [the longest x1 2.81 us: on_device(): grad_summed[safe_node] * silu_slope]
    reshape x0 -> x3, local copies, waits for them, and re-layouts: none -> 3.98 us  [the longest x1 1.84 us: send_stage(): st['sent'] = sent.reshape(PATCHES, 2, HALF + LANES)]
  transfers between devices with their start and end apart: 10 -> 5, of which waited for: 10 -> 5; matrix products, arithmetic and copies ran while one was open for 6% -> 2% of each run, Pallas kernels for 0% -> 2%
where the time goes in v1:
time: 195 us; the launch traced here: 194 us
  blocking collectives  68 us (35%)
  waiting for transfers between devices  50.3 us (26%)
  starting transfers between devices  41.5 us (21%)
  Pallas kernels  21.7 us (11%)
  local copies, waits for them, and re-layouts  11.5 us (6%)
    all_to_all x4, blocking collectives, on_device(): st['got'] = lax.all_to_all(st['sent'], axes, 0, 0, tiled=True)  68 us
    all_to_all x5, waiting for transfers between devices, on_device(): st['got'] = lax.all_to_all(st['sent'], axes, 0, 0, tiled=True)  50.3 us
    all_to_all x5, starting transfers between devices, on_device(): st['got'] = lax.all_to_all(st['sent'], axes, 0, 0, tiled=True)  41.5 us
    pallas_call x9, Pallas kernels, call(): pl.pallas_call(kernel, out_shape=shapes, cost_estimate=pl.CostEstimate(fl...  21.7 us
  transfers between devices with their start and end apart: 5, of which 5 were waited for; matrix products, arithmetic and copies ran while one was open for 2% of the time, Pallas kernels for 2%

profile of v1, /device:TPU:1, one launch (start us, length us, event | category | flops | bytes accessed | tf_op | source)
XLA Modules:
  0.0 193.8 jit_solution(17990885977462327157)
XLA Ops:
  0.6 1.7 pack_kernel.1
  2.3 5.1 %all-to-all-start = ((bf16[4,400,128]{2,1,0:T(8,128)(2,1)}), bf16[4,400,128]{2,1,0:T(8,128)(2,1)S(1)}, u32[]{:S(2)}, u32[]{:S(2)}) async-start(bf16[4,400,128]{2,1,0:T(8,128)(2,1)} %pack_kernel.1), calls=%async_computation | async-start | bytes 819200 | tf_op jit(solution)/shard_map/all_to_all | solution.py:387
  7.5 0.9 copy.19.patch_col
  8.3 2.6 %slot_kernel.1 = (bf16[1024,256]{1,0:T(8,128)(2,1)}, bf16[128,128]{1,0:T(8,128)(2,1)}) custom-call(s32[512,1]{1,0:T(8,128)} %copy.19.patch_col, s32[1,512]{1,0:T(1,128)} %bitcast.21, s32[1,512]{1,0:T(1,128)} %bitcast.24, s32[1,512]{1,0:T(1,128)} %bitcast.25), custom_call_target="tpu_custom_call" | custom-call | flops 134217728 | bytes 1048576 | tf_op jit(solution)/shard_map/slot_kernel/pallas_call | solution.py:53
  10.9 0.7 constant_dynamic-slice_fusion.4
  11.7 2.1 %all-to-all-done.packed = bf16[4,400,128]{2,1,0:T(8,128)(2,1)S(1)} async-done(((bf16[4,400,128]{2,1,0:T(8,128)(2,1)}), bf16[4,400,128]{2,1,0:T(8,128)(2,1)S(1)}, u32[]{:S(2)}, u32[]{:S(2)}) %all-to-all-start) | async-done | bytes 409632 | tf_op jit(solution)/shard_map/all_to_all | solution.py:387
  13.8 0.8 copy-done
  14.6 2.6 %send_kernel.1 = (bf16[128,1280]{1,0:T(8,128)(2,1)}, f32[64,128]{1,0:T(8,128)}) custom-call(bf16[4,400,128]{2,1,0:T(8,128)(2,1)} %copy-done, bf16[1024,256]{1,0:T(8,128)(2,1)} %get-tuple-element.31.pick, bf16[128,128]{1,0:T(8,128)(2,1)} %get-tuple-element.32.meta, bf16[512,128]{1,0:T(8,128)(2,1)} %get-tuple-element.59.source_cols, ...), custom_call_target="tpu_custom_call" | custom-call | flops 268435456 | bytes 1048576 | tf_op jit(solution)/shard_map/send_kernel/pallas_call | solution.py:53
  17.1 1.8 reshape.44
  18.9 21.8 %all-to-all-start.1 = ((bf16[128,2,640]{2,1,0:T(2,128)(2,1)}), bf16[128,2,640]{2,1,0:T(2,128)(2,1)S(1)}, u32[]{:S(2)}, u32[]{:S(2)}) async-start(bf16[128,2,640]{2,1,0:T(2,128)(2,1)} %reshape.44), calls=%async_computation.1 | async-start | bytes 655360 | tf_op jit(solution)/shard_map/all_to_all | solution.py:387
  41.4 24.7 %all-to-all-done.1 = bf16[128,2,640]{2,1,0:T(2,128)(2,1)S(1)} async-done(((bf16[128,2,640]{2,1,0:T(2,128)(2,1)}), bf16[128,2,640]{2,1,0:T(2,128)(2,1)S(1)}, u32[]{:S(2)}, u32[]{:S(2)}) %all-to-all-start.1) | async-done | bytes 327712 | tf_op jit(solution)/shard_map/all_to_all | solution.py:387
  66.1 0.8 copy.20
  66.9 2.4 %message_kernel.1 = (bf16[4,64,128]{2,1,0:T(8,128)(2,1)}, f32[1024,128]{1,0:T(8,128)}, bf16[1024,64]{1,0:T(8,128)(2,1)}) custom-call(bf16[128,1280]{1,0:T(8,128)(2,1)} %bitcast.19, f32[64,128]{1,0:T(8,128)} %get-tuple-element.34.mesh_proj, f32[1,128]{1,0:T(1,128)} %bitcast.26), custom_call_target="tpu_custom_call" | custom-call | flops 134217728 | bytes 1048576 | tf_op jit(solution)/shard_map/message_kernel/pallas_call | solution.py:53
  69.3 3.3 %all-to-all-start.2 = ((bf16[4,64,128]{2,1,0:T(8,128)(2,1)}), bf16[4,64,128]{2,1,0:T(8,128)(2,1)S(1)}, u32[]{:S(2)}, u32[]{:S(2)}) async-start(bf16[4,64,128]{2,1,0:T(8,128)(2,1)} %get-tuple-element.35), calls=%async_computation.2 | async-start | bytes 131072 | tf_op jit(solution)/shard_map/all_to_all | solution.py:387
  73.2 3.8 %all-to-all-done.2.summed = bf16[4,64,128]{2,1,0:T(8,128)(2,1)S(1)} async-done(((bf16[4,64,128]{2,1,0:T(8,128)(2,1)}), bf16[4,64,128]{2,1,0:T(8,128)(2,1)S(1)}, u32[]{:S(2)}, u32[]{:S(2)}) %all-to-all-start.2) | async-done | bytes 65568 | tf_op jit(solution)/shard_map/all_to_all | solution.py:387
  77.6 4.0 %node_kernel.1 = (bf16[64,128]{1,0:T(8,128)(2,1)}, bf16[128,1024]{1,0:T(8,128)(2,1)}, bf16[64,128]{1,0:T(8,128)(2,1)}, bf16[512,128]{1,0:T(8,128)(2,1)}, bf16[51...) custom-call(bf16[4,400,128]{2,1,0:T(8,128)(2,1)} %copy-done, bf16[4,64,128]{2,1,0:T(8,128)(2,1)} %copy-done.3, ...), custom_call_target="tpu_custom_call" | custom-call | flops 268435456 | bytes 1048576 | tf_op jit(solution)/shard_map/node_kernel/pallas_call | solution.py:53
  81.6 1.1 reshape.46
  82.8 30.0 %all_to_all.45 = bf16[128,2,512]{2,1,0:T(2,128)(2,1)S(1)} all-to-all(bf16[128,2,512]{2,1,0:T(2,128)(2,1)S(1)} %reshape.46), channel_id=1, replica_groups=mesh['x'=4,'z'=16,'c'=2,'y'=4] {'x','z','c'}, dimensions={0} | all-to-all | bytes 524288 | tf_op jit(solution)/shard_map/all_to_all | solution.py:387
  112.7 0.7 copy.21
  113.5 2.8 %grid_kernel.1 = (bf16[4,320,128]{2,1,0:T(8,128)(2,1)}, bf16[2,64,1792]{2,1,0:T(8,128)(2,1)}) custom-call(bf16[128,1024]{1,0:T(8,128)(2,1)} %bitcast.15, bf16[1024,256]{1,0:T(8,128)(2,1)} %get-tuple-element.31.pick, bf16[4,400,128]{2,1,0:T(8,128)(2,1)} %copy-done, bf16[64,128]{1,0:T(8,128)(2,1)} %get-tuple-element.40.node_grad, ...), custom_call_target="tpu_custom_call" | custom-call | flops 268435456 | bytes 1048576 | tf_op jit(solution)/shard_map/grid_kernel/pallas_call | solution.py:53
  116.3 7.8 %all_to_all.46.params = bf16[2,64,1792]{2,1,0:T(8,128)(2,1)} all-to-all(bf16[2,64,1792]{2,1,0:T(8,128)(2,1)} %get-tuple-element.48), channel_id=1, replica_groups=mesh['x'=4,'z'=16,'c'=2,'y'=4] {'c'}, dimensions={0} | all-to-all | bytes 917504 | tf_op jit(solution)/shard_map/all_to_all | solution.py:387
  124.1 1.8 pair_kernel.1
  125.9 1.0 reshape.48
  126.9 21.9 %all_to_all.47 = bf16[64,2,896]{2,1,0:T(2,128)(2,1)S(1)} all-to-all(bf16[64,2,896]{2,1,0:T(2,128)(2,1)S(1)} %reshape.48), channel_id=1, replica_groups=mesh['x'=4,'z'=16,'c'=2,'y'=4] {'x','z'}, dimensions={0} | all-to-all | bytes 458752 | tf_op jit(solution)/shard_map/all_to_all | solution.py:387
  148.8 3.5 %all-to-all-start.4 = ((bf16[4,320,128]{2,1,0:T(8,128)(2,1)}), bf16[4,320,128]{2,1,0:T(8,128)(2,1)S(1)}, u32[]{:S(2)}, u32[]{:S(2)}) async-start(bf16[4,320,128]{2,1,0:T(8,128)(2,1)} %get-tuple-element.45), calls=%async_computation.4 | async-start | bytes 655360 | tf_op jit(solution)/shard_map/all_to_all | solution.py:387
  152.6 5.6 %all-to-all-done.4.gathered = bf16[4,320,128]{2,1,0:T(8,128)(2,1)S(1)} async-done(((bf16[4,320,128]{2,1,0:T(8,128)(2,1)}), bf16[4,320,128]{2,1,0:T(8,128)(2,1)S(1)}, u32[]{:S(2)}, u32[]{:S(2)}) %all-to-all-start.4) | async-done | bytes 327712 | tf_op jit(solution)/shard_map/all_to_all | solution.py:387
  158.1 0.8 broadcast_in_dim.23
  159.0 7.8 %all-to-all-start.7 = ((bf16[64,2,896]{2,1,0:T(2,128)(2,1)}), bf16[64,2,896]{2,1,0:T(2,128)(2,1)S(1)}, u32[]{:S(2)}, u32[]{:S(2)}) async-start(bf16[64,2,896]{2,1,0:T(2,128)(2,1)} %broadcast_in_dim.23), calls=%async_computation.7 | async-start | bytes 458752 | tf_op jit(solution)/shard_map/all_to_all | solution.py:387
  167.5 2.0 %back_kernel.1 = (bf16[256,128]{1,0:T(8,128)(2,1)}, bf16[64,128]{1,0:T(8,128)(2,1)}) custom-call(bf16[4,320,128]{2,1,0:T(8,128)(2,1)} %copy-done.1, bf16[128,512]{1,0:T(8,128)(2,1)} %get-tuple-element.57.source_rows, bf16[128,512]{1,0:T(8,128)(2,1)} %get-tuple-element.56.dest_rows, bf16[64,128]{1,0:T(8,128)(2,1)} %cot.5), custom_call_target="tpu_custom_call" | custom-call | flops 67108864 | bytes 1048576 | tf_op jit(solution)/shard_map/back_kernel/pallas_call | solution.py:53
  169.5 14.1 %all-to-all-done.7 = bf16[64,2,896]{2,1,0:T(2,128)(2,1)S(1)} async-done(((bf16[64,2,896]{2,1,0:T(2,128)(2,1)}), bf16[64,2,896]{2,1,0:T(2,128)(2,1)S(1)}, u32[]{:S(2)}, u32[]{:S(2)}) %all-to-all-start.7) | async-done | bytes 229408 | tf_op jit(solution)/shard_map/all_to_all | solution.py:387
  183.7 8.2 %all_to_all.48.params = bf16[2,64,1792]{2,1,0:T(8,128)(2,1)} all-to-all(bf16[2,64,1792]{2,1,0:T(8,128)(2,1)S(1)} %broadcast_in_dim.24), channel_id=1, replica_groups=mesh['x'=4,'z'=16,'c'=2,'y'=4] {'c'}, dimensions={0} | all-to-all | bytes 917504 | tf_op jit(solution)/shard_map/all_to_all | solution.py:387
  191.9 1.9 unpack_kernel.1
  (23 shorter events, 3.0 us)
Async XLA Ops:
  2.3 5.1 %copy-start.6 = (s32[512,1]{0,1:T(1,128)S(1)}, s32[512,1]{0,1:T(1,128)}, u32[]{:S(2)}) copy-start(s32[512,1]{0,1:T(1,128)} %param.19) | copy-start | bytes 6148
  2.3 8.6 %copy-start.5 = (bf16[512,512]{1,0:T(8,128)(2,1)S(1)}, bf16[512,512]{1,0:T(8,128)(2,1)}, u32[]{:S(2)}) copy-start(bf16[512,512]{1,0:T(8,128)(2,1)} %param.13) | copy-start | bytes 1572868
  2.3 11.5 %all-to-all-start = ((bf16[4,400,128]{2,1,0:T(8,128)(2,1)}), bf16[4,400,128]{2,1,0:T(8,128)(2,1)S(1)}, u32[]{:S(2)}, u32[]{:S(2)}) async-start(bf16[4,400,128]{2,1,0:T(8,128)(2,1)} %pack_kernel.1), calls=%async_computation | async-start | bytes 819200 | tf_op jit(solution)/shard_map/all_to_all | solution.py:387
  7.5 3.5 %copy-start.4 = (bf16[512,512]{1,0:T(8,128)(2,1)S(1)}, bf16[512,512]{1,0:T(8,128)(2,1)}, u32[]{:S(2)}) copy-start(bf16[512,512]{1,0:T(8,128)(2,1)} %param.14) | copy-start | bytes 1572868
  13.8 0.8 copy-start
  17.1 23.6 %copy-start.2 = (bf16[512,512]{1,0:T(8,128)(2,1)S(1)}, bf16[512,512]{1,0:T(8,128)(2,1)}, u32[]{:S(2)}) copy-start(bf16[512,512]{1,0:T(8,128)(2,1)} %w_out.1) | copy-start | bytes 1572868
  18.9 47.1 %all-to-all-start.1 = ((bf16[128,2,640]{2,1,0:T(2,128)(2,1)}), bf16[128,2,640]{2,1,0:T(2,128)(2,1)S(1)}, u32[]{:S(2)}, u32[]{:S(2)}) async-start(bf16[128,2,640]{2,1,0:T(2,128)(2,1)} %reshape.44), calls=%async_computation.1 | async-start | bytes 655360 | tf_op jit(solution)/shard_map/all_to_all | solution.py:387
  69.3 7.7 %all-to-all-start.2 = ((bf16[4,64,128]{2,1,0:T(8,128)(2,1)}), bf16[4,64,128]{2,1,0:T(8,128)(2,1)S(1)}, u32[]{:S(2)}, u32[]{:S(2)}) async-start(bf16[4,64,128]{2,1,0:T(8,128)(2,1)} %get-tuple-element.35), calls=%async_computation.2 | async-start | bytes 131072 | tf_op jit(solution)/shard_map/all_to_all | solution.py:387
  77.0 0.6 copy-start.3
  148.8 9.3 %all-to-all-start.4 = ((bf16[4,320,128]{2,1,0:T(8,128)(2,1)}), bf16[4,320,128]{2,1,0:T(8,128)(2,1)S(1)}, u32[]{:S(2)}, u32[]{:S(2)}) async-start(bf16[4,320,128]{2,1,0:T(8,128)(2,1)} %get-tuple-element.45), calls=%async_computation.4 | async-start | bytes 655360 | tf_op jit(solution)/shard_map/all_to_all | solution.py:387
  158.1 0.8 copy-start.1
  159.0 24.7 %all-to-all-start.7 = ((bf16[64,2,896]{2,1,0:T(2,128)(2,1)}), bf16[64,2,896]{2,1,0:T(2,128)(2,1)S(1)}, u32[]{:S(2)}, u32[]{:S(2)}) async-start(bf16[64,2,896]{2,1,0:T(2,128)(2,1)} %broadcast_in_dim.23), calls=%async_computation.7 | async-start | bytes 458752 | tf_op jit(solution)/shard_map/all_to_all | solution.py:387

commit v2 on v1

--- a/solution.py
+++ b/solution.py
@@ -2,10 +2,12 @@
 import jax.numpy as jnp
 from jax import lax
 from jax.experimental import pallas as pl
+from jax.experimental.pallas import tpu as pltpu
 from jax.sharding import Mesh
 from jax.sharding import PartitionSpec as P
 
-FAR = ("x", "z")
+
+NEAR = ("x", "c")
 PATCH = ("x", "z", "c")
 BF = jnp.bfloat16
 F32 = jnp.float32
@@ -25,10 +27,12 @@
 MESH_AT = COT_AT + MESH
 GAIN_AT = MESH_AT + MESH
 PACK = GAIN_AT + 16
-FARS = 64
+NEARS = 8
+FARS = 16
 WEIGHT_BLOCKS = LATENT // FARS
-HALF_BLOCKS = 3 * WEIGHT_BLOCKS // 2
-PARAM_COLS = (HALF_BLOCKS + 2) * LANES
+OWN_BLOCKS = 3 * WEIGHT_BLOCKS // NEARS
+PARAM_COLS = (OWN_BLOCKS + 2) * LANES
+VMEM_BYTES = 20 << 20
 
 
 def dot(a, b, dims=((1,), (0,))):
@@ -48,13 +52,14 @@
     return slice(j * LANES, (j + 1) * LANES)
 
 
-def call(kernel, outs, args, flops):
+def call(kernel, outs, args, flops, **more):
     shapes = tuple(jax.ShapeDtypeStruct(s, d) for s, d in outs)
     return pl.pallas_call(
         kernel,
         out_shape=shapes,
+        compiler_params=pltpu.CompilerParams(vmem_limit_bytes=VMEM_BYTES),
+        **more,
         cost_estimate=pl.CostEstimate(flops=flops, bytes_accessed=1 << 20, transcendentals=0),
-        name=kernel.__name__,
     )(*args)
 
 
@@ -216,50 +221,56 @@
         rows = pick[r * PATCHES : (r + 1) * PATCHES]
         total += dot(rows, returned[:, cols(r)], ((0,), (0,)))
     total = total.astype(BF)
-    for j in range(CHANS):
-        out[j, 0:GRID] = total
-        out[j, GRID : GRID + MESH] = node_grad[...]
+    out[0:GRID] = total
+    out[GRID : GRID + MESH] = node_grad[...]
     blocks = []
     for j in range(CHANS):
         part = dot(packed[j, 0:GRID], total, ((0,), (0,))).astype(BF)
-        blocks += [part[0:FARS], part[FARS : 2 * FARS]]
+        blocks += [part[b * FARS : (b + 1) * FARS] for b in range(LANES // FARS)]
     for whole in (dest_part, out_part):
         blocks += [whole[b * FARS : (b + 1) * FARS] for b in range(WEIGHT_BLOCKS)]
     for b, block in enumerate(blocks):
-        params[b // HALF_BLOCKS, :, cols(b % HALF_BLOCKS)] = block
+        params[b // OWN_BLOCKS, :, cols(b % OWN_BLOCKS)] = block
     head = iota((FARS, LANES), 0) == 0
-    for half, small in enumerate((bias_part, gain_part)):
-        for k, part in enumerate(two_parts(small[...])):
+    small = [bias_part[...], gain_part[...]] + [jnp.zeros((1, LANES), F32)] * (NEARS - 2)
+    for g in range(NEARS):
+        for k, part in enumerate(two_parts(small[g])):
             spread = jnp.where(head, part.astype(F32), 0.0)
-            params[half, :, cols(HALF_BLOCKS + k)] = spread.astype(BF)
-
-
-def back_kernel(gathered, source_rows, dest_rows, cot, grad_grid, grad_mesh):
+            params[g, :, cols(OWN_BLOCKS + k)] = spread.astype(BF)
+
+
+def back_kernel(
+    chan, own, last, middle, following, source_rows, dest_rows, cot, grad_grid, grad_mesh
+):
     on_grid = jnp.zeros((GRID, LANES), F32)
     on_mesh = cot[...].astype(F32)
-    for j in range(CHANS):
-        on_grid += dot(gathered[j, 0:GRID], source_rows[:, cols(j)], ((1,), (1,)))
-        on_mesh += dot(gathered[j, GRID : GRID + MESH], dest_rows[:, cols(j)], ((1,), (1,)))
+    for k, block in enumerate((own, last, middle, following)):
+        at = pl.multiple_of(lax.rem(chan[0] + CHANS - k, CHANS) * LANES, LANES)
+        there = pl.ds(at, LANES)
+        on_grid += dot(block[0:GRID], source_rows[:, there], ((1,), (1,)))
+        on_mesh += dot(block[GRID : GRID + MESH], dest_rows[:, there], ((1,), (1,)))
     grad_grid[...] = on_grid.astype(BF)
     grad_mesh[...] = on_mesh.astype(BF)
 
 
-def pair_kernel(params, out):
-    total = params[0].astype(F32) + params[1].astype(F32)
-    small = total[:, cols(HALF_BLOCKS)] + total[:, cols(HALF_BLOCKS + 1)]
-    out[:, 0 : HALF_BLOCKS * LANES] = total[:, 0 : HALF_BLOCKS * LANES].astype(BF)
+def near_sum_kernel(params, out):
+    total = params[0].astype(F32)
+    for g in range(1, NEARS):
+        total += params[g].astype(F32)
+    small = total[:, cols(OWN_BLOCKS)] + total[:, cols(OWN_BLOCKS + 1)]
+    out[:, 0 : OWN_BLOCKS * LANES] = total[:, 0 : OWN_BLOCKS * LANES].astype(BF)
     for k, part in enumerate(two_parts(small)):
-        out[:, cols(HALF_BLOCKS + k)] = part
+        out[:, cols(OWN_BLOCKS + k)] = part
 
 
 def unpack_kernel(params, source, dest, out, bias, gain):
     for b in range(3 * WEIGHT_BLOCKS):
-        block = params[b // HALF_BLOCKS, :, cols(b % HALF_BLOCKS)].astype(F32)
+        block = params[b // OWN_BLOCKS, :, cols(b % OWN_BLOCKS)].astype(F32)
         at = b % WEIGHT_BLOCKS * FARS
         (source, dest, out)[b // WEIGHT_BLOCKS][at : at + FARS] = block
-    for half, small in enumerate((bias, gain)):
-        high = params[half, 0:1, cols(HALF_BLOCKS)].astype(F32)
-        small[...] = high + params[half, 0:1, cols(HALF_BLOCKS + 1)].astype(F32)
+    for g, small in enumerate((bias, gain)):
+        high = params[g, 0:1, cols(OWN_BLOCKS)].astype(F32)
+        small[...] = high + params[g, 0:1, cols(OWN_BLOCKS + 1)].astype(F32)
 
 
 def gather_stage(st):
@@ -306,22 +317,23 @@
 
 def grid_stage(st):
     returned = st["got"].reshape(PATCHES, 2 * HALF)
-    outs = [((CHANS, GRID + MESH, LANES), BF), ((2, FARS, PARAM_COLS), BF)]
+    outs = [((GRID + MESH, LANES), BF), ((NEARS, FARS, PARAM_COLS), BF)]
     args = (returned, st["pick"], st["packed"], *st["partial"])
     st["sent"], st["params"] = call(grid_kernel, outs, args, 1 << 28)
     return st
 
 
 def back_stage(st):
-    args = (st["got"], st["source_rows"], st["dest_rows"], st["cotangent"])
+    args = (st["chan"][None], *st["got"], st["source_rows"], st["dest_rows"], st["cotangent"])
     outs = [((GRID, LANES), BF), ((MESH, LANES), BF)]
-    st["grad_grid"], st["grad_mesh"] = call(back_kernel, outs, args, 1 << 26)
+    specs = [pl.BlockSpec(memory_space=pltpu.SMEM)] + [pl.BlockSpec()] * (len(args) - 1)
+    st["grad_grid"], st["grad_mesh"] = call(back_kernel, outs, args, 1 << 26, in_specs=specs)
     st["sent"] = st["params"]
     return st
 
 
 def far_stage(st):
-    (sent,) = call(pair_kernel, [((FARS, PARAM_COLS), BF)], (st["got"],), 1 << 18)
+    (sent,) = call(near_sum_kernel, [((FARS, PARAM_COLS), BF)], (st["got"],), 1 << 18)
     st["sent"] = sent.reshape(FARS, 2, PARAM_COLS // 2)
     return st
 
@@ -339,7 +351,7 @@
 
 def near_stage(st):
     whole = st["got"].reshape(FARS, PARAM_COLS)
-    st["sent"] = jnp.broadcast_to(whole, (2, FARS, PARAM_COLS))
+    st["sent"] = jnp.broadcast_to(whole, (NEARS, FARS, PARAM_COLS))
     return st
 
 
@@ -355,11 +367,11 @@
     (send_stage, PATCH),
     (message_stage, "y"),
     (node_stage, PATCH),
-    (grid_stage, "y"),
-    (back_stage, "c"),
-    (far_stage, FAR),
-    (sum_stage, FAR),
-    (near_stage, "c"),
+    (grid_stage, "shifts"),
+    (back_stage, NEAR),
+    (far_stage, "z"),
+    (sum_stage, "z"),
+    (near_stage, NEAR),
     (last_stage, None),
 )
 
@@ -378,12 +390,18 @@
 )
 
 
+def shifted(x, by):
+    return lax.ppermute(x, "y", [(i, (i + by) % CHANS) for i in range(CHANS)])
+
+
 def on_device(*args):
     st = dict(zip(NAMES, args))
     st["chan"] = lax.axis_index("y")
     for stage, axes in STAGES:
         st = stage(st)
-        if axes is not None:
+        if axes == "shifts":
+            st["got"] = [st["sent"]] + [shifted(st["sent"], k) for k in range(1, CHANS)]
+        elif axes is not None:
             st["got"] = lax.all_to_all(st["sent"], axes, 0, 0, tiled=True)
     return (st["updated"], st["grad_grid"], st["grad_mesh"], *st["params"])
 

time: 195 us -> 171 us (0.88)
  waiting for transfers between devices: 50.3 us -> 34.2 us
  Pallas kernels: 21.7 us -> 8.27 us
  blocking collectives: 68 us -> 71.9 us
  starting transfers between devices: 41.5 us -> 45.3 us
  local copies, waits for them, and re-layouts: 11.5 us -> 9.05 us
    all_to_all x5 -> x4, waiting for transfers between devices: 50.3 us -> 32.7 us  [on_device(): st['got'] = lax.all_to_all(st['sent'], axes, 0, 0, tiled=True)]
    pallas_call x9, Pallas kernels: 21.7 us -> 8.27 us  [call(): pl.pallas_call(kernel, out_shape=shapes, compiler_params=pltpu.CompilerPa...]
    ppermute x0 -> x3, starting transfers between devices: none -> 8.5 us  [shifted(): return lax.ppermute(x, 'y', [(i, (i + by) % CHANS) for i in range(CHANS)])]
    all_to_all x5 -> x4, starting transfers between devices: 41.5 us -> 36.8 us  [on_device(): st['got'] = lax.all_to_all(st['sent'], axes, 0, 0, tiled=True)]
    all_to_all x4, blocking collectives: 68 us -> 71.9 us  [on_device(): st['got'] = lax.all_to_all(st['sent'], axes, 0, 0, tiled=True)]
    unnamed x18 -> x26, local copies, waits for them, and re-layouts: 3.81 us -> 5.17 us
  transfers between devices with their start and end apart: 5 -> 7, of which waited for: 5 -> 4; matrix products, arithmetic and copies ran while one was open for 2% -> 1% of each run, Pallas kernels for 2% -> 1%
where the time goes in v2:
time: 171 us; the launch traced here: 170 us
  blocking collectives  71.9 us (42%)
  starting transfers between devices  45.3 us (26%)
  waiting for transfers between devices  34.2 us (20%)
  local copies, waits for them, and re-layouts  9.05 us (5%)
  Pallas kernels  8.27 us (5%)
    all_to_all x4, blocking collectives, on_device(): st['got'] = lax.all_to_all(st['sent'], axes, 0, 0, tiled=True)  71.9 us
    all_to_all x4, starting transfers between devices, on_device(): st['got'] = lax.all_to_all(st['sent'], axes, 0, 0, tiled=True)  36.8 us
    all_to_all x4, waiting for transfers between devices, on_device(): st['got'] = lax.all_to_all(st['sent'], axes, 0, 0, tiled=True)  32.7 us
    ppermute x3, starting transfers between devices, shifted(): return lax.ppermute(x, 'y', [(i, (i + by) % CHANS) for i in range(CHANS)])  8.5 us
    pallas_call x9, Pallas kernels, call(): pl.pallas_call(kernel, out_shape=shapes, compiler_params=pltpu.CompilerPa...  8.27 us
    unnamed x26, local copies, waits for them, and re-layouts  5.17 us
  transfers between devices with their start and end apart: 7, of which 4 were waited for; matrix products, arithmetic and copies ran while one was open for 1% of the time, Pallas kernels for 1%

profile of v2, /device:TPU:1, one launch (start us, length us, event | category | flops | bytes accessed | tf_op | source)
XLA Modules:
  0.0 169.7 jit_solution(16140743741899530881)
XLA Ops:
  0.6 0.6 copy-done.7
  1.3 0.7 copy-done.1
  2.0 0.7 copy-done.3
  2.7 0.8 copy-done.5
  3.6 0.8 shard_map.170
  4.4 5.0 %all-to-all-start = ((bf16[4,400,128]{2,1,0:T(8,128)(2,1)}), bf16[4,400,128]{2,1,0:T(8,128)(2,1)S(1)}, u32[]{:S(2)}, u32[]{:S(2)}) async-start(bf16[4,400,128]{2,1,0:T(8,128)(2,1)} %shard_map.170), calls=%async_computation | async-start | bytes 819200 | tf_op jit(solution)/shard_map/all_to_all | solution.py:405
  9.4 0.7 copy-done.6
  10.9 0.8 shard_map.171
  11.7 1.0 constant_dynamic-slice_fusion.4
  12.7 3.0 %all-to-all-done.packed = bf16[4,400,128]{2,1,0:T(8,128)(2,1)S(1)} async-done(((bf16[4,400,128]{2,1,0:T(8,128)(2,1)}), bf16[4,400,128]{2,1,0:T(8,128)(2,1)S(1)}, u32[]{:S(2)}, u32[]{:S(2)}) %all-to-all-start) | async-done | bytes 409632 | tf_op jit(solution)/shard_map/all_to_all | solution.py:405
  16.3 0.8 reshape.44
  17.1 21.8 %all-to-all-start.1 = ((bf16[128,2,640]{2,1,0:T(2,128)(2,1)}), bf16[128,2,640]{2,1,0:T(2,128)(2,1)S(1)}, u32[]{:S(2)}, u32[]{:S(2)}) async-start(bf16[128,2,640]{2,1,0:T(2,128)(2,1)} %reshape.44), calls=%async_computation.1 | async-start | bytes 655360 | tf_op jit(solution)/shard_map/all_to_all | solution.py:405
  38.9 25.3 %all-to-all-done.1 = bf16[128,2,640]{2,1,0:T(2,128)(2,1)S(1)} async-done(((bf16[128,2,640]{2,1,0:T(2,128)(2,1)}), bf16[128,2,640]{2,1,0:T(2,128)(2,1)S(1)}, u32[]{:S(2)}, u32[]{:S(2)}) %all-to-all-start.1) | async-done | bytes 327712 | tf_op jit(solution)/shard_map/all_to_all | solution.py:405
  64.3 0.6 copy-done.10
  65.0 1.3 shard_map.173
  66.3 3.3 %all-to-all-start.2 = ((bf16[4,64,128]{2,1,0:T(8,128)(2,1)}), bf16[4,64,128]{2,1,0:T(8,128)(2,1)S(1)}, u32[]{:S(2)}, u32[]{:S(2)}) async-start(bf16[4,64,128]{2,1,0:T(8,128)(2,1)} %get-tuple-element.35), calls=%async_computation.2 | async-start | bytes 131072 | tf_op jit(solution)/shard_map/all_to_all | solution.py:405
  69.7 4.4 %all-to-all-done.2.summed = bf16[4,64,128]{2,1,0:T(8,128)(2,1)S(1)} async-done(((bf16[4,64,128]{2,1,0:T(8,128)(2,1)}), bf16[4,64,128]{2,1,0:T(8,128)(2,1)S(1)}, u32[]{:S(2)}, u32[]{:S(2)}) %all-to-all-start.2) | async-done | bytes 65568 | tf_op jit(solution)/shard_map/all_to_all | solution.py:405
  74.0 2.2 %shard_map.174 = (bf16[64,128]{1,0:T(8,128)(2,1)}, bf16[128,1024]{1,0:T(8,128)(2,1)S(1)}, bf16[64,128]{1,0:T(8,128)(2,1)S(1)}, bf16[512,128]{1,0:T(8,128)(2,1)S(...) custom-call(bf16[4,400,128]{2,1,0:T(8,128)(2,1)S(1)} %all-to-all-done.packed, ...), custom_call_target="tpu_custom_call" | custom-call | flops 268435456 | bytes 1048576 | tf_op jit(solution)/shard_map/pallas_call | solution.py:57
  76.4 30.0 %all_to_all.40 = bf16[128,2,512]{2,1,0:T(2,128)(2,1)S(1)} all-to-all(bf16[128,2,512]{2,1,0:T(2,128)(2,1)S(1)} %reshape.46), channel_id=1, replica_groups=mesh['x'=4,'z'=16,'c'=2,'y'=4] {'x','z','c'}, dimensions={0} | all-to-all | bytes 524288 | tf_op jit(solution)/shard_map/all_to_all | solution.py:405
  106.4 0.6 shard_map.175
  107.1 13.6 %all_to_all.41.params = bf16[8,16,1792]{2,1,0:T(8,128)(2,1)S(1)} all-to-all(bf16[8,16,1792]{2,1,0:T(8,128)(2,1)S(1)} %get-tuple-element.48), channel_id=1, replica_groups=mesh['x'=4,'z'=16,'c'=2,'y'=4] {'x','c'}, dimensions={0} | all-to-all | bytes 917504 | tf_op jit(solution)/shard_map/all_to_all | solution.py:405
  120.8 14.2 %all_to_all.42 = bf16[16,2,896]{2,1,0:T(2,128)(2,1)S(1)} all-to-all(bf16[16,2,896]{2,1,0:T(2,128)(2,1)S(1)} %reshape.48), channel_id=1, replica_groups=mesh['x'=4,'z'=16,'c'=2,'y'=4] {'z'}, dimensions={0} | all-to-all | bytes 114688 | tf_op jit(solution)/shard_map/all_to_all | solution.py:405
  135.2 14.1 %all_to_all.43 = bf16[16,2,896]{2,1,0:T(2,128)(2,1)S(1)} all-to-all(bf16[16,2,896]{2,1,0:T(2,128)(2,1)S(1)} %broadcast_in_dim.27), channel_id=1, replica_groups=mesh['x'=4,'z'=16,'c'=2,'y'=4] {'z'}, dimensions={0} | all-to-all | bytes 114688 | tf_op jit(solution)/shard_map/all_to_all | solution.py:405
  149.3 0.8 broadcast_in_dim.28
  150.1 6.7 %all-to-all-start.7 = ((bf16[8,16,1792]{2,1,0:T(8,128)(2,1)}), bf16[8,16,1792]{2,1,0:T(8,128)(2,1)S(1)}, u32[]{:S(2)}, u32[]{:S(2)}) async-start(bf16[8,16,1792]{2,1,0:T(8,128)(2,1)} %broadcast_in_dim.28), calls=%async_computation.7 | async-start | bytes 917504 | tf_op jit(solution)/shard_map/all_to_all | solution.py:405
  156.8 2.2 %collective-permute-start = (bf16[320,128]{1,0:T(8,128)(2,1)S(1)}, bf16[320,128]{1,0:T(8,128)(2,1)S(1)}, u32[]{:S(2)}, u32[]{:S(2)}) collective-permute-start(bf16[320,128]{1,0:T(8,128)(2,1)S(1)} %get-tuple-element.45.own), channel_id=1, source_target_pairs={{0,1},{1,2},{2,3},{3,0},{4,5},{5,6},{6,7},{7,4},{8,9},{9,10},{10,1... | collective-permute-start | bytes 245768 | tf_op jit(solution)/shard_map/ppermute | solution.py:394
  159.0 3.7 %collective-permute-start.1 = (bf16[320,128]{1,0:T(8,128)(2,1)S(1)}, bf16[320,128]{1,0:T(8,128)(2,1)S(1)}, u32[]{:S(2)}, u32[]{:S(2)}) collective-permute-start(bf16[320,128]{1,0:T(8,128)(2,1)S(1)} %get-tuple-element.45.own), channel_id=1, source_target_pairs={{0,2},{1,3},{2,0},{3,1},{4,6},{5,7},{6,4},{7,5},{8,10},{9,11},{10,... | collective-permute-start | bytes 245768 | tf_op jit(solution)/shard_map/ppermute | solution.py:394
  162.7 2.6 %collective-permute-start.2 = (bf16[320,128]{1,0:T(8,128)(2,1)S(1)}, bf16[320,128]{1,0:T(8,128)(2,1)S(1)}, u32[]{:S(2)}, u32[]{:S(2)}) collective-permute-start(bf16[320,128]{1,0:T(8,128)(2,1)S(1)} %get-tuple-element.45.own), channel_id=1, source_target_pairs={{0,3},{1,0},{2,1},{3,2},{4,7},{5,4},{6,5},{7,6},{8,11},{9,8},{10,9... | collective-permute-start | bytes 245768 | tf_op jit(solution)/shard_map/ppermute | solution.py:394
  165.3 1.0 constant_dynamic-slice_fusion
  166.3 1.5 collective-permute-done.2.following
  167.9 0.9 shard_map.176
  168.8 0.9 shard_map.178
  (35 shorter events, 2.0 us)
Async XLA Ops:
  0.6 0.7 copy-start.7
  1.3 0.7 copy-start.1
  2.0 0.7 copy-start.3
  2.7 0.8 copy-start.5
  4.4 11.3 %all-to-all-start = ((bf16[4,400,128]{2,1,0:T(8,128)(2,1)}), bf16[4,400,128]{2,1,0:T(8,128)(2,1)S(1)}, u32[]{:S(2)}, u32[]{:S(2)}) async-start(bf16[4,400,128]{2,1,0:T(8,128)(2,1)} %shard_map.170), calls=%async_computation | async-start | bytes 819200 | tf_op jit(solution)/shard_map/all_to_all | solution.py:405
  9.4 0.7 copy-start.6
  10.1 0.7 copy-start.9
  10.2 0.7 copy-start.8
  16.3 22.6 %copy-start = (bf16[512,512]{1,0:T(8,128)(2,1)S(1)}, bf16[512,512]{1,0:T(8,128)(2,1)}, u32[]{:S(2)}) copy-start(bf16[512,512]{1,0:T(8,128)(2,1)} %w_out.1) | copy-start | bytes 1572868
  17.1 47.2 %all-to-all-start.1 = ((bf16[128,2,640]{2,1,0:T(2,128)(2,1)}), bf16[128,2,640]{2,1,0:T(2,128)(2,1)S(1)}, u32[]{:S(2)}, u32[]{:S(2)}) async-start(bf16[128,2,640]{2,1,0:T(2,128)(2,1)} %reshape.44), calls=%async_computation.1 | async-start | bytes 655360 | tf_op jit(solution)/shard_map/all_to_all | solution.py:405
  64.3 0.7 copy-start.10
  66.3 7.7 %all-to-all-start.2 = ((bf16[4,64,128]{2,1,0:T(8,128)(2,1)}), bf16[4,64,128]{2,1,0:T(8,128)(2,1)S(1)}, u32[]{:S(2)}, u32[]{:S(2)}) async-start(bf16[4,64,128]{2,1,0:T(8,128)(2,1)} %get-tuple-element.35), calls=%async_computation.2 | async-start | bytes 131072 | tf_op jit(solution)/shard_map/all_to_all | solution.py:405
  69.6 4.4 %copy-start.2 = (bf16[64,128]{1,0:T(8,128)(2,1)S(1)}, bf16[64,128]{1,0:T(8,128)(2,1)}, u32[]{:S(2)}) copy-start(bf16[64,128]{1,0:T(8,128)(2,1)} %cot.5) | copy-start | bytes 49156
  69.6 4.4 %copy-start.4 = (bf16[64,128]{1,0:T(8,128)(2,1)S(1)}, bf16[64,128]{1,0:T(8,128)(2,1)}, u32[]{:S(2)}) copy-start(bf16[64,128]{1,0:T(8,128)(2,1)} %mesh.3) | copy-start | bytes 49156
  150.1 18.7 %all-to-all-start.7 = ((bf16[8,16,1792]{2,1,0:T(8,128)(2,1)}), bf16[8,16,1792]{2,1,0:T(8,128)(2,1)S(1)}, u32[]{:S(2)}, u32[]{:S(2)}) async-start(bf16[8,16,1792]{2,1,0:T(8,128)(2,1)} %broadcast_in_dim.28), calls=%async_computation.7 | async-start | bytes 917504 | tf_op jit(solution)/shard_map/all_to_all | solution.py:405
  156.8 9.5 %collective-permute-start = (bf16[320,128]{1,0:T(8,128)(2,1)S(1)}, bf16[320,128]{1,0:T(8,128)(2,1)S(1)}, u32[]{:S(2)}, u32[]{:S(2)}) collective-permute-start(bf16[320,128]{1,0:T(8,128)(2,1)S(1)} %get-tuple-element.45.own), channel_id=1, source_target_pairs={{0,1},{1,2},{2,3},{3,0},{4,5},{5,6},{6,7},{7,4},{8,9},{9,10},{10,1... | collective-permute-start | bytes 245768 | tf_op jit(solution)/shard_map/ppermute | solution.py:394
  159.0 7.3 %collective-permute-start.1 = (bf16[320,128]{1,0:T(8,128)(2,1)S(1)}, bf16[320,128]{1,0:T(8,128)(2,1)S(1)}, u32[]{:S(2)}, u32[]{:S(2)}) collective-permute-start(bf16[320,128]{1,0:T(8,128)(2,1)S(1)} %get-tuple-element.45.own), channel_id=1, source_target_pairs={{0,2},{1,3},{2,0},{3,1},{4,6},{5,7},{6,4},{7,5},{8,10},{9,11},{10,... | collective-permute-start | bytes 245768 | tf_op jit(solution)/shard_map/ppermute | solution.py:394
  162.7 5.2 %collective-permute-start.2 = (bf16[320,128]{1,0:T(8,128)(2,1)S(1)}, bf16[320,128]{1,0:T(8,128)(2,1)S(1)}, u32[]{:S(2)}, u32[]{:S(2)}) collective-permute-start(bf16[320,128]{1,0:T(8,128)(2,1)S(1)} %get-tuple-element.45.own), channel_id=1, source_target_pairs={{0,3},{1,0},{2,1},{3,2},{4,7},{5,4},{6,5},{7,6},{8,11},{9,8},{10,9... | collective-permute-start | bytes 245768 | tf_op jit(solution)/shard_map/ppermute | solution.py:394

commit v3 on v2

--- a/solution.py
+++ b/solution.py
@@ -33,6 +33,7 @@
 OWN_BLOCKS = 3 * WEIGHT_BLOCKS // NEARS
 PARAM_COLS = (OWN_BLOCKS + 2) * LANES
 VMEM_BYTES = 20 << 20
+ALL_VMEM = 60 << 20
 
 
 def dot(a, b, dims=((1,), (0,))):
@@ -52,12 +53,12 @@
     return slice(j * LANES, (j + 1) * LANES)
 
 
-def call(kernel, outs, args, flops, **more):
+def call(kernel, outs, args, flops, vmem=VMEM_BYTES, **more):
     shapes = tuple(jax.ShapeDtypeStruct(s, d) for s, d in outs)
     return pl.pallas_call(
         kernel,
         out_shape=shapes,
-        compiler_params=pltpu.CompilerParams(vmem_limit_bytes=VMEM_BYTES),
+        compiler_params=pltpu.CompilerParams(vmem_limit_bytes=vmem),
         **more,
         cost_estimate=pl.CostEstimate(flops=flops, bytes_accessed=1 << 20, transcendentals=0),
     )(*args)
@@ -80,7 +81,11 @@
         out[j, GAIN_AT:PACK] = parts.astype(BF)
 
 
-def slot_kernel(patch_col, patch_row, source, node, pick, meta):
+def slot_kernel(
+    patch_col, patch_row, source, node, bias, gain, pick, meta, bias_out, gain_out
+):
+    bias_out[...] = bias[...]
+    gain_out[...] = gain[...]
     before = iota((EDGES, EDGES), 0) < iota((EDGES, EDGES), 1)
     same = patch_col[...] == patch_row[...]
     rank = jnp.sum(jnp.where(same & before, 1.0, 0.0), axis=0, keepdims=True)
@@ -239,16 +244,22 @@
             params[g, :, cols(OWN_BLOCKS + k)] = spread.astype(BF)
 
 
-def back_kernel(
-    chan, own, last, middle, following, source_rows, dest_rows, cot, grad_grid, grad_mesh
-):
+def join_kernel(own, other, out):
+    out[0, 0:GRID] = own[0:GRID]
+    out[0, GRID : GRID + MESH] = own[GRID : GRID + MESH]
+    out[1, 0:GRID] = other[0:GRID]
+    out[1, GRID : GRID + MESH] = other[GRID : GRID + MESH]
+
+
+def back_kernel(chan, near, far, source_rows, dest_rows, cot, grad_grid, grad_mesh):
     on_grid = jnp.zeros((GRID, LANES), F32)
     on_mesh = cot[...].astype(F32)
-    for k, block in enumerate((own, last, middle, following)):
-        at = pl.multiple_of(lax.rem(chan[0] + CHANS - k, CHANS) * LANES, LANES)
+    for k in range(CHANS):
+        block = (near, far)[k // 2]
+        at = pl.multiple_of(lax.bitwise_xor(chan[0], jnp.int32(k)) * LANES, LANES)
         there = pl.ds(at, LANES)
-        on_grid += dot(block[0:GRID], source_rows[:, there], ((1,), (1,)))
-        on_mesh += dot(block[GRID : GRID + MESH], dest_rows[:, there], ((1,), (1,)))
+        on_grid += dot(block[k % 2, 0:GRID], source_rows[:, there], ((1,), (1,)))
+        on_mesh += dot(block[k % 2, GRID : GRID + MESH], dest_rows[:, there], ((1,), (1,)))
     grad_grid[...] = on_grid.astype(BF)
     grad_mesh[...] = on_mesh.astype(BF)
 
@@ -275,7 +286,8 @@
 
 def gather_stage(st):
     args = (st["grid_latent"], st["cotangent"], st["mesh_latent"], st["norm_gain"][None])
-    (st["sent"],) = call(pack_kernel, [((CHANS, PACK, LANES), BF)], args, 1 << 20)
+    outs = [((CHANS, PACK, LANES), BF)]
+    (st["sent"],) = call(pack_kernel, outs, args, 1 << 20, ALL_VMEM)
     return st
 
 
@@ -287,9 +299,10 @@
         st[name + "_cols"] = lax.dynamic_slice_in_dim(whole, offset, LANES, 1)
         st[name + "_rows"] = lax.dynamic_slice_in_dim(whole, offset, LANES, 0)
     patch = st["edge_patch"]
-    args = (patch, patch.reshape(1, EDGES), st["edge_source"][None], st["edge_node"][None])
-    outs = [((SLOTS, GRID), BF), ((PATCHES, LANES), BF)]
-    st["pick"], meta = call(slot_kernel, outs, args, 1 << 27)
+    args = [patch, patch.reshape(1, EDGES), st["edge_source"][None], st["edge_node"][None]]
+    args += [st["edge_bias"][None], st["norm_gain"][None]]
+    outs = [((SLOTS, GRID), BF), ((PATCHES, LANES), BF)] + [((1, LANES), F32)] * 2
+    st["pick"], meta, st["bias"], st["gain"] = call(slot_kernel, outs, args, 1 << 27)
     args = (st["packed"], st["pick"], meta, st["source_cols"], st["dest_cols"])
     outs = [((PATCHES, 2 * HALF + 2 * LANES), BF), ((MESH, LANES), F32)]
     sent, st["mesh_proj"] = call(send_kernel, outs, args, 1 << 28)
@@ -300,14 +313,14 @@
 def message_stage(st):
     arrived = st["got"].reshape(PATCHES, 2 * HALF + 2 * LANES)
     outs = [((CHANS, MESH, LANES), BF), ((SLOTS, LANES), F32), ((SLOTS, MESH), BF)]
-    args = (arrived, st["mesh_proj"], st["edge_bias"][None])
+    args = (arrived, st["mesh_proj"], st["bias"])
     st["sent"], st["pre"], st["chosen"] = call(message_kernel, outs, args, 1 << 27)
     return st
 
 
 def node_stage(st):
     args = [st["packed"], st["got"], st["pre"], st["chosen"], st["w_out"], st["out_cols"]]
-    args += [st["out_rows"], st["mesh_latent"], st["cotangent"], st["norm_gain"][None]]
+    args += [st["out_rows"], st["mesh_latent"], st["cotangent"], st["gain"]]
     outs = [((MESH, LANES), BF), ((PATCHES, 2 * HALF), BF), ((MESH, LANES), BF)]
     outs += [((LATENT, LANES), BF)] * 2 + [((1, LANES), F32)] * 2
     st["updated"], grads, *st["partial"] = call(node_kernel, outs, args, 1 << 28)
@@ -323,8 +336,16 @@
     return st
 
 
+def join_stage(st):
+    outs = [((2, GRID + MESH, LANES), BF)]
+    (st["near"],) = call(join_kernel, outs, (st["sent"], st["got"]), 1 << 18)
+    st["sent"] = st["near"]
+    return st
+
+
 def back_stage(st):
-    args = (st["chan"][None], *st["got"], st["source_rows"], st["dest_rows"], st["cotangent"])
+    args = (st["chan"][None], st["near"], st["got"])
+    args += (st["source_rows"], st["dest_rows"], st["cotangent"])
     outs = [((GRID, LANES), BF), ((MESH, LANES), BF)]
     specs = [pl.BlockSpec(memory_space=pltpu.SMEM)] + [pl.BlockSpec()] * (len(args) - 1)
     st["grad_grid"], st["grad_mesh"] = call(back_kernel, outs, args, 1 << 26, in_specs=specs)
@@ -367,7 +388,8 @@
     (send_stage, PATCH),
     (message_stage, "y"),
     (node_stage, PATCH),
-    (grid_stage, "shifts"),
+    (grid_stage, 1),
+    (join_stage, 2),
     (back_stage, NEAR),
     (far_stage, "z"),
     (sum_stage, "z"),
@@ -390,17 +412,13 @@
 )
 
 
-def shifted(x, by):
-    return lax.ppermute(x, "y", [(i, (i + by) % CHANS) for i in range(CHANS)])
-
-
 def on_device(*args):
     st = dict(zip(NAMES, args))
     st["chan"] = lax.axis_index("y")
     for stage, axes in STAGES:
         st = stage(st)
-        if axes == "shifts":
-            st["got"] = [st["sent"]] + [shifted(st["sent"], k) for k in range(1, CHANS)]
+        if axes in (1, 2):
+            st["got"] = lax.ppermute(st["sent"], "y", [(i, i ^ axes) for i in range(CHANS)])
         elif axes is not None:
             st["got"] = lax.all_to_all(st["sent"], axes, 0, 0, tiled=True)
     return (st["updated"], st["grad_grid"], st["grad_mesh"], *st["params"])

time: 171 us -> 171 us (level)
  waiting for transfers between devices: 34.2 us -> 40.8 us
  starting transfers between devices: 45.3 us -> 41.6 us
  local copies, waits for them, and re-layouts: 9.05 us -> 5.47 us
    ppermute x3 -> x2, waiting for transfers between devices: 1.55 us -> 8.11 us  [on_device(): lax.ppermute(st['sent'], 'y', [(i, i ^ axes) for i in range(CHANS)])]
    ppermute x3 -> x2, starting transfers between devices: 8.5 us -> 4.82 us  [on_device(): lax.ppermute(st['sent'], 'y', [(i, i ^ axes) for i in range(CHANS)])]
    unnamed x26 -> x20, local copies, waits for them, and re-layouts: 5.17 us -> 1.59 us
    pallas_call x9 -> x10, Pallas kernels: 8.27 us -> 9.13 us  [call(): pl.pallas_call(kernel, out_shape=shapes, compiler_params=pltpu.CompilerPa...]
  transfers between devices with their start and end apart: 7 -> 6, of which waited for: 4 -> 5; matrix products, arithmetic and copies ran while one was open for 1% -> 1% of each run, Pallas kernels for 1% -> 1%
where the time goes in v3:
time: 171 us; the launch traced here: 170 us
  blocking collectives  71.9 us (42%)
  starting transfers between devices  41.6 us (24%)
  waiting for transfers between devices  40.8 us (24%)
  Pallas kernels  9.13 us (5%)
  local copies, waits for them, and re-layouts  5.47 us (3%)
    all_to_all x4, blocking collectives, on_device(): st['got'] = lax.all_to_all(st['sent'], axes, 0, 0, tiled=True)  71.9 us
    all_to_all x4, starting transfers between devices, on_device(): st['got'] = lax.all_to_all(st['sent'], axes, 0, 0, tiled=True)  36.8 us
    all_to_all x4, waiting for transfers between devices, on_device(): st['got'] = lax.all_to_all(st['sent'], axes, 0, 0, tiled=True)  32.7 us
    pallas_call x10, Pallas kernels, call(): pl.pallas_call(kernel, out_shape=shapes, compiler_params=pltpu.CompilerPa...  9.13 us
    ppermute x2, waiting for transfers between devices, on_device(): lax.ppermute(st['sent'], 'y', [(i, i ^ axes) for i in range(CHANS)])  8.11 us
    ppermute x2, starting transfers between devices, on_device(): lax.ppermute(st['sent'], 'y', [(i, i ^ axes) for i in range(CHANS)])  4.82 us
  transfers between devices with their start and end apart: 6, of which 5 were waited for; matrix products, arithmetic and copies ran while one was open for 1% of the time, Pallas kernels for 1%

profile of v3, /device:TPU:1, one launch (start us, length us, event | category | flops | bytes accessed | tf_op | source)
XLA Modules:
  0.0 169.8 jit_solution(1596187481461606616)
XLA Ops:
  0.6 1.7 shard_map.170
  2.3 5.0 %all-to-all-start = ((bf16[4,400,128]{2,1,0:T(8,128)(2,1)}), bf16[4,400,128]{2,1,0:T(8,128)(2,1)S(1)}, u32[]{:S(2)}, u32[]{:S(2)}) async-start(bf16[4,400,128]{2,1,0:T(8,128)(2,1)} %shard_map.170), calls=%async_computation | async-start | bytes 819200 | tf_op jit(solution)/shard_map/all_to_all | solution.py:423
  7.3 0.7 copy-done.3
  8.0 0.1 copy.19.patch_col
  8.2 0.5 copy-done.6
  8.7 0.2 copy-done.5
  8.8 0.8 shard_map.171
  9.6 1.0 constant_dynamic-slice_fusion.4
  10.6 3.0 %all-to-all-done.packed = bf16[4,400,128]{2,1,0:T(8,128)(2,1)S(1)} async-done(((bf16[4,400,128]{2,1,0:T(8,128)(2,1)}), bf16[4,400,128]{2,1,0:T(8,128)(2,1)S(1)}, u32[]{:S(2)}, u32[]{:S(2)}) %all-to-all-start) | async-done | bytes 409632 | tf_op jit(solution)/shard_map/all_to_all | solution.py:423
  13.6 0.6 shard_map.172
  14.2 0.8 reshape.44
  15.0 21.8 %all-to-all-start.1 = ((bf16[128,2,640]{2,1,0:T(2,128)(2,1)}), bf16[128,2,640]{2,1,0:T(2,128)(2,1)S(1)}, u32[]{:S(2)}, u32[]{:S(2)}) async-start(bf16[128,2,640]{2,1,0:T(2,128)(2,1)} %reshape.44), calls=%async_computation.1 | async-start | bytes 655360 | tf_op jit(solution)/shard_map/all_to_all | solution.py:423
  36.8 25.3 %all-to-all-done.1 = bf16[128,2,640]{2,1,0:T(2,128)(2,1)S(1)} async-done(((bf16[128,2,640]{2,1,0:T(2,128)(2,1)}), bf16[128,2,640]{2,1,0:T(2,128)(2,1)S(1)}, u32[]{:S(2)}, u32[]{:S(2)}) %all-to-all-start.1) | async-done | bytes 327712 | tf_op jit(solution)/shard_map/all_to_all | solution.py:423
  62.2 1.3 shard_map.173
  63.6 3.3 %all-to-all-start.2 = ((bf16[4,64,128]{2,1,0:T(8,128)(2,1)}), bf16[4,64,128]{2,1,0:T(8,128)(2,1)S(1)}, u32[]{:S(2)}, u32[]{:S(2)}) async-start(bf16[4,64,128]{2,1,0:T(8,128)(2,1)} %get-tuple-element.38), calls=%async_computation.2 | async-start | bytes 131072 | tf_op jit(solution)/shard_map/all_to_all | solution.py:423
  66.9 4.4 %all-to-all-done.2.summed = bf16[4,64,128]{2,1,0:T(8,128)(2,1)S(1)} async-done(((bf16[4,64,128]{2,1,0:T(8,128)(2,1)}), bf16[4,64,128]{2,1,0:T(8,128)(2,1)S(1)}, u32[]{:S(2)}, u32[]{:S(2)}) %all-to-all-start.2) | async-done | bytes 65568 | tf_op jit(solution)/shard_map/all_to_all | solution.py:423
  71.3 2.2 %shard_map.174 = (bf16[64,128]{1,0:T(8,128)(2,1)}, bf16[128,1024]{1,0:T(8,128)(2,1)S(1)}, bf16[64,128]{1,0:T(8,128)(2,1)S(1)}, bf16[512,128]{1,0:T(8,128)(2,1)S(...) custom-call(bf16[4,400,128]{2,1,0:T(8,128)(2,1)S(1)} %all-to-all-done.packed, ...), custom_call_target="tpu_custom_call" | custom-call | flops 268435456 | bytes 1048576 | tf_op jit(solution)/shard_map/pallas_call | solution.py:58
  73.5 0.2 reshape.46
  73.6 30.0 %all_to_all.40 = bf16[128,2,512]{2,1,0:T(2,128)(2,1)S(1)} all-to-all(bf16[128,2,512]{2,1,0:T(2,128)(2,1)S(1)} %reshape.46), channel_id=1, replica_groups=mesh['x'=4,'z'=16,'c'=2,'y'=4] {'x','z','c'}, dimensions={0} | all-to-all | bytes 524288 | tf_op jit(solution)/shard_map/all_to_all | solution.py:423
  103.7 0.6 shard_map.175
  104.3 13.6 %all_to_all.41.params = bf16[8,16,1792]{2,1,0:T(8,128)(2,1)S(1)} all-to-all(bf16[8,16,1792]{2,1,0:T(8,128)(2,1)S(1)} %get-tuple-element.52), channel_id=1, replica_groups=mesh['x'=4,'z'=16,'c'=2,'y'=4] {'x','c'}, dimensions={0} | all-to-all | bytes 917504 | tf_op jit(solution)/shard_map/all_to_all | solution.py:423
  118.0 14.2 %all_to_all.42 = bf16[16,2,896]{2,1,0:T(2,128)(2,1)S(1)} all-to-all(bf16[16,2,896]{2,1,0:T(2,128)(2,1)S(1)} %reshape.48), channel_id=1, replica_groups=mesh['x'=4,'z'=16,'c'=2,'y'=4] {'z'}, dimensions={0} | all-to-all | bytes 114688 | tf_op jit(solution)/shard_map/all_to_all | solution.py:423
  132.4 14.1 %all_to_all.43 = bf16[16,2,896]{2,1,0:T(2,128)(2,1)S(1)} all-to-all(bf16[16,2,896]{2,1,0:T(2,128)(2,1)S(1)} %broadcast_in_dim.27), channel_id=1, replica_groups=mesh['x'=4,'z'=16,'c'=2,'y'=4] {'z'}, dimensions={0} | all-to-all | bytes 114688 | tf_op jit(solution)/shard_map/all_to_all | solution.py:423
  146.5 0.8 broadcast_in_dim.28
  147.3 6.7 %all-to-all-start.7 = ((bf16[8,16,1792]{2,1,0:T(8,128)(2,1)}), bf16[8,16,1792]{2,1,0:T(8,128)(2,1)S(1)}, u32[]{:S(2)}, u32[]{:S(2)}) async-start(bf16[8,16,1792]{2,1,0:T(8,128)(2,1)} %broadcast_in_dim.28), calls=%async_computation.7 | async-start | bytes 917504 | tf_op jit(solution)/shard_map/all_to_all | solution.py:423
  154.0 2.2 %collective-permute-start = (bf16[320,128]{1,0:T(8,128)(2,1)S(1)}, bf16[320,128]{1,0:T(8,128)(2,1)S(1)}, u32[]{:S(2)}, u32[]{:S(2)}) collective-permute-start(bf16[320,128]{1,0:T(8,128)(2,1)S(1)} %get-tuple-element.49.own), channel_id=1, source_target_pairs={{0,1},{1,0},{2,3},{3,2},{4,5},{5,4},{6,7},{7,6},{8,9},{9,8},{10,11... | collective-permute-start | bytes 245768 | tf_op jit(solution)/shard_map/ppermute | solution.py:421
  156.2 3.6 %collective-permute-done.other = bf16[320,128]{1,0:T(8,128)(2,1)S(1)} collective-permute-done((bf16[320,128]{1,0:T(8,128)(2,1)S(1)}, bf16[320,128]{1,0:T(8,128)(2,1)S(1)}, u32[]{:S(2)}, u32[]{:S(2)}) %collective-permute-start) | collective-permute-done | bytes 81952 | tf_op jit(solution)/shard_map/ppermute | solution.py:421
  159.8 2.6 %collective-permute-start.1 = (bf16[2,320,128]{2,1,0:T(8,128)(2,1)S(1)}, bf16[2,320,128]{2,1,0:T(8,128)(2,1)S(1)}, u32[]{:S(2)}, u32[]{:S(2)}) collective-permute-start(bf16[2,320,128]{2,1,0:T(8,128)(2,1)S(1)} %shard_map.176.near), channel_id=1, source_target_pairs={{0,2},{1,3},{2,0},{3,1},{4,6},{5,7},{6,4},{7,5},{8,10},{9,11},{10,... | collective-permute-start | bytes 491528 | tf_op jit(solution)/shard_map/ppermute | solution.py:421
  162.5 1.0 constant_dynamic-slice_fusion
  163.4 4.5 %collective-permute-done.1.far = bf16[2,320,128]{2,1,0:T(8,128)(2,1)S(1)} collective-permute-done((bf16[2,320,128]{2,1,0:T(8,128)(2,1)S(1)}, bf16[2,320,128]{2,1,0:T(8,128)(2,1)S(1)}, u32[]{:S(2)}, u32[]{:S(2)}) %collective-permute-start.1) | collective-permute-done | bytes 163872 | tf_op jit(solution)/shard_map/ppermute | solution.py:421
  168.0 0.9 shard_map.177
  168.9 0.9 shard_map.179
  (28 shorter events, 0.4 us)
Async XLA Ops:
  2.3 11.3 %all-to-all-start = ((bf16[4,400,128]{2,1,0:T(8,128)(2,1)}), bf16[4,400,128]{2,1,0:T(8,128)(2,1)S(1)}, u32[]{:S(2)}, u32[]{:S(2)}) async-start(bf16[4,400,128]{2,1,0:T(8,128)(2,1)} %shard_map.170), calls=%async_computation | async-start | bytes 819200 | tf_op jit(solution)/shard_map/all_to_all | solution.py:423
  7.3 0.7 copy-start.3
  8.0 0.7 copy-start.6
  8.1 0.7 copy-start.5
  8.2 0.7 copy-start.4
  8.2 0.7 copy-start.7
  14.2 22.6 %copy-start = (bf16[512,512]{1,0:T(8,128)(2,1)S(1)}, bf16[512,512]{1,0:T(8,128)(2,1)}, u32[]{:S(2)}) copy-start(bf16[512,512]{1,0:T(8,128)(2,1)} %w_out.1) | copy-start | bytes 1572868
  15.0 47.1 %all-to-all-start.1 = ((bf16[128,2,640]{2,1,0:T(2,128)(2,1)}), bf16[128,2,640]{2,1,0:T(2,128)(2,1)S(1)}, u32[]{:S(2)}, u32[]{:S(2)}) async-start(bf16[128,2,640]{2,1,0:T(2,128)(2,1)} %reshape.44), calls=%async_computation.1 | async-start | bytes 655360 | tf_op jit(solution)/shard_map/all_to_all | solution.py:423
  63.6 7.7 %all-to-all-start.2 = ((bf16[4,64,128]{2,1,0:T(8,128)(2,1)}), bf16[4,64,128]{2,1,0:T(8,128)(2,1)S(1)}, u32[]{:S(2)}, u32[]{:S(2)}) async-start(bf16[4,64,128]{2,1,0:T(8,128)(2,1)} %get-tuple-element.38), calls=%async_computation.2 | async-start | bytes 131072 | tf_op jit(solution)/shard_map/all_to_all | solution.py:423
  66.8 4.4 %copy-start.1 = (bf16[64,128]{1,0:T(8,128)(2,1)S(1)}, bf16[64,128]{1,0:T(8,128)(2,1)}, u32[]{:S(2)}) copy-start(bf16[64,128]{1,0:T(8,128)(2,1)} %cot.5) | copy-start | bytes 49156
  66.9 4.4 %copy-start.2 = (bf16[64,128]{1,0:T(8,128)(2,1)S(1)}, bf16[64,128]{1,0:T(8,128)(2,1)}, u32[]{:S(2)}) copy-start(bf16[64,128]{1,0:T(8,128)(2,1)} %mesh.3) | copy-start | bytes 49156
  147.3 21.6 %all-to-all-start.7 = ((bf16[8,16,1792]{2,1,0:T(8,128)(2,1)}), bf16[8,16,1792]{2,1,0:T(8,128)(2,1)S(1)}, u32[]{:S(2)}, u32[]{:S(2)}) async-start(bf16[8,16,1792]{2,1,0:T(8,128)(2,1)} %broadcast_in_dim.28), calls=%async_computation.7 | async-start | bytes 917504 | tf_op jit(solution)/shard_map/all_to_all | solution.py:423
  154.0 5.8 %collective-permute-start = (bf16[320,128]{1,0:T(8,128)(2,1)S(1)}, bf16[320,128]{1,0:T(8,128)(2,1)S(1)}, u32[]{:S(2)}, u32[]{:S(2)}) collective-permute-start(bf16[320,128]{1,0:T(8,128)(2,1)S(1)} %get-tuple-element.49.own), channel_id=1, source_target_pairs={{0,1},{1,0},{2,3},{3,2},{4,5},{5,4},{6,7},{7,6},{8,9},{9,8},{10,11... | collective-permute-start | bytes 245768 | tf_op jit(solution)/shard_map/ppermute | solution.py:421
  159.8 8.2 %collective-permute-start.1 = (bf16[2,320,128]{2,1,0:T(8,128)(2,1)S(1)}, bf16[2,320,128]{2,1,0:T(8,128)(2,1)S(1)}, u32[]{:S(2)}, u32[]{:S(2)}) collective-permute-start(bf16[2,320,128]{2,1,0:T(8,128)(2,1)S(1)} %shard_map.176.near), channel_id=1, source_target_pairs={{0,2},{1,3},{2,0},{3,1},{4,6},{5,7},{6,4},{7,5},{8,10},{9,11},{10,... | collective-permute-start | bytes 491528 | tf_op jit(solution)/shard_map/ppermute | solution.py:421

commit v4 on v3

--- a/solution.py
+++ b/solution.py
@@ -7,8 +7,8 @@
 from jax.sharding import PartitionSpec as P
 
 
-NEAR = ("x", "c")
-PATCH = ("x", "z", "c")
+NEAR = ("x", "zl", "c")
+PATCH = ("x", "zh", "zl", "c")
 BF = jnp.bfloat16
 F32 = jnp.float32
 
@@ -27,11 +27,11 @@
 MESH_AT = COT_AT + MESH
 GAIN_AT = MESH_AT + MESH
 PACK = GAIN_AT + 16
-NEARS = 8
-FARS = 16
-WEIGHT_BLOCKS = LATENT // FARS
-OWN_BLOCKS = 3 * WEIGHT_BLOCKS // NEARS
-PARAM_COLS = (OWN_BLOCKS + 2) * LANES
+NEARS = 16
+FARS = 8
+WEIGHT_ROWS = 3 * LATENT // NEARS
+OWN_ROWS = WEIGHT_ROWS + 8
+BLOCK = 32
 VMEM_BYTES = 20 << 20
 ALL_VMEM = 60 << 20
 
@@ -218,6 +218,18 @@
         dest_part[cols(j)] = dot(packed[j, MESH_AT:GAIN_AT], total, ((0,), (0,))).astype(BF)
 
 
+def place(row):
+    at = row % WEIGHT_ROWS
+    return row // WEIGHT_ROWS, slice(at, at + BLOCK)
+
+
+def small_rows(v):
+    high, low = two_parts(v)
+    row = iota((OWN_ROWS - WEIGHT_ROWS, LANES), 0)
+    rows = jnp.where(row == 0, high.astype(F32), jnp.where(row == 1, low.astype(F32), 0.0))
+    return rows.astype(BF)
+
+
 def grid_kernel(
     returned, pick, packed, node_grad, dest_part, out_part, bias_part, gain_part, out, params
 ):
@@ -228,20 +240,18 @@
     total = total.astype(BF)
     out[0:GRID] = total
     out[GRID : GRID + MESH] = node_grad[...]
-    blocks = []
     for j in range(CHANS):
         part = dot(packed[j, 0:GRID], total, ((0,), (0,))).astype(BF)
-        blocks += [part[b * FARS : (b + 1) * FARS] for b in range(LANES // FARS)]
-    for whole in (dest_part, out_part):
-        blocks += [whole[b * FARS : (b + 1) * FARS] for b in range(WEIGHT_BLOCKS)]
-    for b, block in enumerate(blocks):
-        params[b // OWN_BLOCKS, :, cols(b % OWN_BLOCKS)] = block
-    head = iota((FARS, LANES), 0) == 0
+        for at in range(0, LANES, BLOCK):
+            g, own = place(j * LANES + at)
+            params[g, own] = part[at : at + BLOCK]
+    for k, whole in enumerate((dest_part, out_part)):
+        for at in range(0, LATENT, BLOCK):
+            g, own = place((k + 1) * LATENT + at)
+            params[g, own] = whole[at : at + BLOCK]
     small = [bias_part[...], gain_part[...]] + [jnp.zeros((1, LANES), F32)] * (NEARS - 2)
     for g in range(NEARS):
-        for k, part in enumerate(two_parts(small[g])):
-            spread = jnp.where(head, part.astype(F32), 0.0)
-            params[g, :, cols(OWN_BLOCKS + k)] = spread.astype(BF)
+        params[g, WEIGHT_ROWS:OWN_ROWS] = small_rows(small[g])
 
 
 def join_kernel(own, other, out):
@@ -264,24 +274,26 @@
     grad_mesh[...] = on_mesh.astype(BF)
 
 
-def near_sum_kernel(params, out):
-    total = params[0].astype(F32)
-    for g in range(1, NEARS):
-        total += params[g].astype(F32)
-    small = total[:, cols(OWN_BLOCKS)] + total[:, cols(OWN_BLOCKS + 1)]
-    out[:, 0 : OWN_BLOCKS * LANES] = total[:, 0 : OWN_BLOCKS * LANES].astype(BF)
-    for k, part in enumerate(two_parts(small)):
-        out[:, cols(OWN_BLOCKS + k)] = part
+def sum_kernel(parts, out):
+    total = parts[0].astype(F32)
+    for g in range(1, parts.shape[0]):
+        total += parts[g].astype(F32)
+    weights = total[0:WEIGHT_ROWS].astype(BF)
+    small = total[WEIGHT_ROWS : WEIGHT_ROWS + 1] + total[WEIGHT_ROWS + 1 : WEIGHT_ROWS + 2]
+    rows = small_rows(small)
+    for g in range(out.shape[0]):
+        out[g, 0:WEIGHT_ROWS] = weights
+        out[g, WEIGHT_ROWS:OWN_ROWS] = rows
 
 
 def unpack_kernel(params, source, dest, out, bias, gain):
-    for b in range(3 * WEIGHT_BLOCKS):
-        block = params[b // OWN_BLOCKS, :, cols(b % OWN_BLOCKS)].astype(F32)
-        at = b % WEIGHT_BLOCKS * FARS
-        (source, dest, out)[b // WEIGHT_BLOCKS][at : at + FARS] = block
+    for k, whole in enumerate((source, dest, out)):
+        for at in range(0, LATENT, BLOCK):
+            g, own = place(k * LATENT + at)
+            whole[at : at + BLOCK] = params[g, own].astype(F32)
     for g, small in enumerate((bias, gain)):
-        high = params[g, 0:1, cols(OWN_BLOCKS)].astype(F32)
-        small[...] = high + params[g, 0:1, cols(OWN_BLOCKS + 1)].astype(F32)
+        rows = params[g, WEIGHT_ROWS:OWN_ROWS].astype(F32)
+        small[...] = rows[0:1] + rows[1:2]
 
 
 def gather_stage(st):
@@ -330,7 +342,7 @@
 
 def grid_stage(st):
     returned = st["got"].reshape(PATCHES, 2 * HALF)
-    outs = [((GRID + MESH, LANES), BF), ((NEARS, FARS, PARAM_COLS), BF)]
+    outs = [((GRID + MESH, LANES), BF), ((NEARS, OWN_ROWS, LANES), BF)]
     args = (returned, st["pick"], st["packed"], *st["partial"])
     st["sent"], st["params"] = call(grid_kernel, outs, args, 1 << 28)
     return st
@@ -354,25 +366,14 @@
 
 
 def far_stage(st):
-    (sent,) = call(near_sum_kernel, [((FARS, PARAM_COLS), BF)], (st["got"],), 1 << 18)
-    st["sent"] = sent.reshape(FARS, 2, PARAM_COLS // 2)
-    return st
-
-
-def sum_stage(st):
-    total = jnp.sum(st["got"].astype(F32), axis=0)
-    at = PARAM_COLS // 2 - 2 * LANES
-    small = total[1:2, at : at + LANES] + total[1:2, at + LANES :]
-    high = lax.reduce_precision(small, 8, 7)
-    last = jnp.concatenate([total[1:2, :at], high, small - high], axis=1)
-    total = jnp.concatenate([total[0:1], last], axis=0).astype(BF)
-    st["sent"] = jnp.broadcast_to(total, (FARS, 2, PARAM_COLS // 2))
+    outs = [((FARS, OWN_ROWS, LANES), BF)]
+    (st["sent"],) = call(sum_kernel, outs, (st["got"],), 1 << 20)
     return st
 
 
 def near_stage(st):
-    whole = st["got"].reshape(FARS, PARAM_COLS)
-    st["sent"] = jnp.broadcast_to(whole, (NEARS, FARS, PARAM_COLS))
+    outs = [((NEARS, OWN_ROWS, LANES), BF)]
+    (st["sent"],) = call(sum_kernel, outs, (st["got"],), 1 << 20)
     return st
 
 
@@ -391,8 +392,7 @@
     (grid_stage, 1),
     (join_stage, 2),
     (back_stage, NEAR),
-    (far_stage, "z"),
-    (sum_stage, "z"),
+    (far_stage, "zh"),
     (near_stage, NEAR),
     (last_stage, None),
 )
@@ -425,7 +425,7 @@
 
 
 def solution(mesh):
-    torus = Mesh(mesh.devices.reshape(4, 16, 2, mesh.shape["chan"]), ("x", "z", "c", "y"))
+    torus = Mesh(mesh.devices.reshape(4, FARS, 2, 2, CHANS), PATCH + ("y",))
     by_patch = P(PATCH, "y")
     return jax.shard_map(
         on_device,

time: 171 us -> 162 us (0.947)
  blocking collectives: 71.9 us -> 62.7 us
    all_to_all x4 -> x3, blocking collectives: 71.9 us -> 62.7 us  [on_device(): st['got'] = lax.all_to_all(st['sent'], axes, 0, 0, tiled=True)]
    pallas_call x10 -> x11, Pallas kernels: 9.13 us -> 9.95 us  [call(): pl.pallas_call(kernel, out_shape=shapes, compiler_params=pltpu.CompilerPa...]
where the time goes in v4:
time: 162 us; the launch traced here: 161 us
  blocking collectives  62.7 us (39%)
  starting transfers between devices  42.5 us (26%)
  waiting for transfers between devices  40.6 us (25%)
  Pallas kernels  9.95 us (6%)
  local copies, waits for them, and re-layouts  4.6 us (3%)
    all_to_all x3, blocking collectives, on_device(): st['got'] = lax.all_to_all(st['sent'], axes, 0, 0, tiled=True)  62.7 us
    all_to_all x4, starting transfers between devices, on_device(): st['got'] = lax.all_to_all(st['sent'], axes, 0, 0, tiled=True)  37.7 us
    all_to_all x4, waiting for transfers between devices, on_device(): st['got'] = lax.all_to_all(st['sent'], axes, 0, 0, tiled=True)  32.7 us
    pallas_call x11, Pallas kernels, call(): pl.pallas_call(kernel, out_shape=shapes, compiler_params=pltpu.CompilerPa...  9.95 us
    ppermute x2, waiting for transfers between devices, on_device(): lax.ppermute(st['sent'], 'y', [(i, i ^ axes) for i in range(CHANS)])  7.9 us
    ppermute x2, starting transfers between devices, on_device(): lax.ppermute(st['sent'], 'y', [(i, i ^ axes) for i in range(CHANS)])  4.81 us
  transfers between devices with their start and end apart: 6, of which 5 were waited for; matrix products, arithmetic and copies ran while one was open for 1% of the time, Pallas kernels for 1%

profile of v4, /device:TPU:1, one launch (start us, length us, event | category | flops | bytes accessed | tf_op | source)
XLA Modules:
  0.0 161.2 jit_solution(14337211707751403290)
XLA Ops:
  0.6 1.7 %shard_map.170 = bf16[4,400,128]{2,1,0:T(8,128)(2,1)} custom-call(bf16[256,128]{1,0:T(8,128)(2,1)} %grid.1, bf16[64,128]{1,0:T(8,128)(2,1)} %cot.5, bf16[64,128]{1,0:T(8,128)(2,1)} %mesh.3, f32[1,128]{1,0:T(1,128)} %bitcast.15), custom_call_target="tpu_custom_call" | custom-call | flops 1048576 | bytes 1048576 | tf_op jit(solution)/shard_map/pallas_call | solution.py:58
  2.3 5.0 %all-to-all-start = ((bf16[4,400,128]{2,1,0:T(8,128)(2,1)}), bf16[4,400,128]{2,1,0:T(8,128)(2,1)S(1)}, u32[]{:S(2)}, u32[]{:S(2)}) async-start(bf16[4,400,128]{2,1,0:T(8,128)(2,1)} %shard_map.170), calls=%async_computation | async-start | bytes 819200 | tf_op jit(solution)/shard_map/all_to_all | solution.py:423
  7.3 0.7 copy-done.3
  8.0 0.1 copy.19.patch_col
  8.2 0.5 copy-done.6
  8.7 0.2 copy-done.5
  8.8 0.8 shard_map.171
  9.6 1.0 constant_dynamic-slice_fusion.4
  10.6 3.0 %all-to-all-done.packed = bf16[4,400,128]{2,1,0:T(8,128)(2,1)S(1)} async-done(((bf16[4,400,128]{2,1,0:T(8,128)(2,1)}), bf16[4,400,128]{2,1,0:T(8,128)(2,1)S(1)}, u32[]{:S(2)}, u32[]{:S(2)}) %all-to-all-start) | async-done | bytes 409632 | tf_op jit(solution)/shard_map/all_to_all | solution.py:423
  13.6 0.6 shard_map.172
  14.2 0.8 reshape.38
  15.0 21.8 %all-to-all-start.1 = ((bf16[128,2,640]{2,1,0:T(2,128)(2,1)}), bf16[128,2,640]{2,1,0:T(2,128)(2,1)S(1)}, u32[]{:S(2)}, u32[]{:S(2)}) async-start(bf16[128,2,640]{2,1,0:T(2,128)(2,1)} %reshape.38), calls=%async_computation.1 | async-start | bytes 655360 | tf_op jit(solution)/shard_map/all_to_all | solution.py:423
  36.9 25.3 %all-to-all-done.1 = bf16[128,2,640]{2,1,0:T(2,128)(2,1)S(1)} async-done(((bf16[128,2,640]{2,1,0:T(2,128)(2,1)}), bf16[128,2,640]{2,1,0:T(2,128)(2,1)S(1)}, u32[]{:S(2)}, u32[]{:S(2)}) %all-to-all-start.1) | async-done | bytes 327712 | tf_op jit(solution)/shard_map/all_to_all | solution.py:423
  62.2 1.3 shard_map.173
  63.6 3.3 %all-to-all-start.2 = ((bf16[4,64,128]{2,1,0:T(8,128)(2,1)}), bf16[4,64,128]{2,1,0:T(8,128)(2,1)S(1)}, u32[]{:S(2)}, u32[]{:S(2)}) async-start(bf16[4,64,128]{2,1,0:T(8,128)(2,1)} %get-tuple-element.38), calls=%async_computation.2 | async-start | bytes 131072 | tf_op jit(solution)/shard_map/all_to_all | solution.py:423
  66.9 4.4 %all-to-all-done.2.summed = bf16[4,64,128]{2,1,0:T(8,128)(2,1)S(1)} async-done(((bf16[4,64,128]{2,1,0:T(8,128)(2,1)}), bf16[4,64,128]{2,1,0:T(8,128)(2,1)S(1)}, u32[]{:S(2)}, u32[]{:S(2)}) %all-to-all-start.2) | async-done | bytes 65568 | tf_op jit(solution)/shard_map/all_to_all | solution.py:423
  71.3 2.2 %shard_map.174 = (bf16[64,128]{1,0:T(8,128)(2,1)}, bf16[128,1024]{1,0:T(8,128)(2,1)S(1)}, bf16[64,128]{1,0:T(8,128)(2,1)S(1)}, bf16[512,128]{1,0:T(8,128)(2,1)S(...) custom-call(bf16[4,400,128]{2,1,0:T(8,128)(2,1)S(1)} %all-to-all-done.packed, ...), custom_call_target="tpu_custom_call" | custom-call | flops 268435456 | bytes 1048576 | tf_op jit(solution)/shard_map/pallas_call | solution.py:58
  73.5 0.2 reshape.40
  73.7 30.0 %all_to_all.35 = bf16[128,2,512]{2,1,0:T(2,128)(2,1)S(1)} all-to-all(bf16[128,2,512]{2,1,0:T(2,128)(2,1)S(1)} %reshape.40), channel_id=1, replica_groups=mesh['x'=4,'zh'=8,'zl'=2,'c'=2,'y'=4] {'x','zh','zl','c'}, dimensions={0} | all-to-all | bytes 524288 | tf_op jit(solution)/shard_map/all_to_all | solution.py:423
  103.7 0.6 shard_map.175
  104.3 13.8 %all_to_all.36.parts = bf16[16,104,128]{2,1,0:T(8,128)(2,1)S(1)} all-to-all(bf16[16,104,128]{2,1,0:T(8,128)(2,1)S(1)} %get-tuple-element.52), channel_id=1, replica_groups=mesh['x'=4,'zh'=8,'zl'=2,'c'=2,'y'=4] {'x','zl','c'}, dimensions={0} | all-to-all | bytes 851968 | tf_op jit(solution)/shard_map/all_to_all | solution.py:423
  118.1 0.1 shard_map.178
  118.2 18.9 %all_to_all.37.parts = bf16[8,104,128]{2,1,0:T(8,128)(2,1)S(1)} all-to-all(bf16[8,104,128]{2,1,0:T(8,128)(2,1)S(1)} %shard_map.178), channel_id=1, replica_groups=mesh['x'=4,'zh'=8,'zl'=2,'c'=2,'y'=4] {'zh'}, dimensions={0} | all-to-all | bytes 425984 | tf_op jit(solution)/shard_map/all_to_all | solution.py:423
  137.1 0.8 shard_map.179
  137.9 7.6 %all-to-all-start.6 = ((bf16[16,104,128]{2,1,0:T(8,128)(2,1)}), bf16[16,104,128]{2,1,0:T(8,128)(2,1)S(1)}, u32[]{:S(2)}, u32[]{:S(2)}) async-start(bf16[16,104,128]{2,1,0:T(8,128)(2,1)} %shard_map.179), calls=%async_computation.6 | async-start | bytes 851968 | tf_op jit(solution)/shard_map/all_to_all | solution.py:423
  145.6 2.2 %collective-permute-start = (bf16[320,128]{1,0:T(8,128)(2,1)S(1)}, bf16[320,128]{1,0:T(8,128)(2,1)S(1)}, u32[]{:S(2)}, u32[]{:S(2)}) collective-permute-start(bf16[320,128]{1,0:T(8,128)(2,1)S(1)} %get-tuple-element.49.own), channel_id=1, source_target_pairs={{0,1},{1,0},{2,3},{3,2},{4,5},{5,4},{6,7},{7,6},{8,9},{9,8},{10,11... | collective-permute-start | bytes 245768 | tf_op jit(solution)/shard_map/ppermute | solution.py:421
  147.8 3.5 %collective-permute-done.other = bf16[320,128]{1,0:T(8,128)(2,1)S(1)} collective-permute-done((bf16[320,128]{1,0:T(8,128)(2,1)S(1)}, bf16[320,128]{1,0:T(8,128)(2,1)S(1)}, u32[]{:S(2)}, u32[]{:S(2)}) %collective-permute-start) | collective-permute-done | bytes 81952 | tf_op jit(solution)/shard_map/ppermute | solution.py:421
  151.3 2.6 %collective-permute-start.1 = (bf16[2,320,128]{2,1,0:T(8,128)(2,1)S(1)}, bf16[2,320,128]{2,1,0:T(8,128)(2,1)S(1)}, u32[]{:S(2)}, u32[]{:S(2)}) collective-permute-start(bf16[2,320,128]{2,1,0:T(8,128)(2,1)S(1)} %shard_map.176.near), channel_id=1, source_target_pairs={{0,2},{1,3},{2,0},{3,1},{4,6},{5,7},{6,4},{7,5},{8,10},{9,11},{10,... | collective-permute-start | bytes 491528 | tf_op jit(solution)/shard_map/ppermute | solution.py:421
  153.9 1.0 constant_dynamic-slice_fusion
  154.9 4.4 %collective-permute-done.1.far = bf16[2,320,128]{2,1,0:T(8,128)(2,1)S(1)} collective-permute-done((bf16[2,320,128]{2,1,0:T(8,128)(2,1)S(1)}, bf16[2,320,128]{2,1,0:T(8,128)(2,1)S(1)}, u32[]{:S(2)}, u32[]{:S(2)}) %collective-permute-start.1) | collective-permute-done | bytes 163872 | tf_op jit(solution)/shard_map/ppermute | solution.py:421
  159.3 0.9 shard_map.177
  160.3 0.9 shard_map.180
  (19 shorter events, 0.2 us)
Async XLA Ops:
  2.3 11.3 %all-to-all-start = ((bf16[4,400,128]{2,1,0:T(8,128)(2,1)}), bf16[4,400,128]{2,1,0:T(8,128)(2,1)S(1)}, u32[]{:S(2)}, u32[]{:S(2)}) async-start(bf16[4,400,128]{2,1,0:T(8,128)(2,1)} %shard_map.170), calls=%async_computation | async-start | bytes 819200 | tf_op jit(solution)/shard_map/all_to_all | solution.py:423
  7.3 0.7 copy-start.3
  8.0 0.7 copy-start.6
  8.1 0.7 copy-start.5
  8.1 0.7 copy-start.4
  8.2 0.7 copy-start.7
  14.2 22.6 %copy-start = (bf16[512,512]{1,0:T(8,128)(2,1)S(1)}, bf16[512,512]{1,0:T(8,128)(2,1)}, u32[]{:S(2)}) copy-start(bf16[512,512]{1,0:T(8,128)(2,1)} %w_out.1) | copy-start | bytes 1572868
  15.0 47.1 %all-to-all-start.1 = ((bf16[128,2,640]{2,1,0:T(2,128)(2,1)}), bf16[128,2,640]{2,1,0:T(2,128)(2,1)S(1)}, u32[]{:S(2)}, u32[]{:S(2)}) async-start(bf16[128,2,640]{2,1,0:T(2,128)(2,1)} %reshape.38), calls=%async_computation.1 | async-start | bytes 655360 | tf_op jit(solution)/shard_map/all_to_all | solution.py:423
  63.6 7.7 %all-to-all-start.2 = ((bf16[4,64,128]{2,1,0:T(8,128)(2,1)}), bf16[4,64,128]{2,1,0:T(8,128)(2,1)S(1)}, u32[]{:S(2)}, u32[]{:S(2)}) async-start(bf16[4,64,128]{2,1,0:T(8,128)(2,1)} %get-tuple-element.38), calls=%async_computation.2 | async-start | bytes 131072 | tf_op jit(solution)/shard_map/all_to_all | solution.py:423
  66.9 4.4 %copy-start.1 = (bf16[64,128]{1,0:T(8,128)(2,1)S(1)}, bf16[64,128]{1,0:T(8,128)(2,1)}, u32[]{:S(2)}) copy-start(bf16[64,128]{1,0:T(8,128)(2,1)} %cot.5) | copy-start | bytes 49156
  66.9 4.4 %copy-start.2 = (bf16[64,128]{1,0:T(8,128)(2,1)S(1)}, bf16[64,128]{1,0:T(8,128)(2,1)}, u32[]{:S(2)}) copy-start(bf16[64,128]{1,0:T(8,128)(2,1)} %mesh.3) | copy-start | bytes 49156
  137.9 22.3 %all-to-all-start.6 = ((bf16[16,104,128]{2,1,0:T(8,128)(2,1)}), bf16[16,104,128]{2,1,0:T(8,128)(2,1)S(1)}, u32[]{:S(2)}, u32[]{:S(2)}) async-start(bf16[16,104,128]{2,1,0:T(8,128)(2,1)} %shard_map.179), calls=%async_computation.6 | async-start | bytes 851968 | tf_op jit(solution)/shard_map/all_to_all | solution.py:423
  145.6 5.6 %collective-permute-start = (bf16[320,128]{1,0:T(8,128)(2,1)S(1)}, bf16[320,128]{1,0:T(8,128)(2,1)S(1)}, u32[]{:S(2)}, u32[]{:S(2)}) collective-permute-start(bf16[320,128]{1,0:T(8,128)(2,1)S(1)} %get-tuple-element.49.own), channel_id=1, source_target_pairs={{0,1},{1,0},{2,3},{3,2},{4,5},{5,4},{6,7},{7,6},{8,9},{9,8},{10,11... | collective-permute-start | bytes 245768 | tf_op jit(solution)/shard_map/ppermute | solution.py:421
  151.3 8.1 %collective-permute-start.1 = (bf16[2,320,128]{2,1,0:T(8,128)(2,1)S(1)}, bf16[2,320,128]{2,1,0:T(8,128)(2,1)S(1)}, u32[]{:S(2)}, u32[]{:S(2)}) collective-permute-start(bf16[2,320,128]{2,1,0:T(8,128)(2,1)S(1)} %shard_map.176.near), channel_id=1, source_target_pairs={{0,2},{1,3},{2,0},{3,1},{4,6},{5,7},{6,4},{7,5},{8,10},{9,11},{10,... | collective-permute-start | bytes 491528 | tf_op jit(solution)/shard_map/ppermute | solution.py:421

commit v5 on v4

--- a/solution.py
+++ b/solution.py
@@ -64,6 +64,10 @@
     )(*args)
 
 
+def scalar_first(args):
+    return [pl.BlockSpec(memory_space=pltpu.SMEM)] + [pl.BlockSpec()] * (len(args) - 1)
+
+
 def pack_kernel(grid, cot, mesh, gain, out):
     high, rest = two_parts(gain[...])
     left = gain[...] - high.astype(F32)
@@ -81,11 +85,13 @@
         out[j, GAIN_AT:PACK] = parts.astype(BF)
 
 
-def slot_kernel(
-    patch_col, patch_row, source, node, bias, gain, pick, meta, bias_out, gain_out
-):
-    bias_out[...] = bias[...]
-    gain_out[...] = gain[...]
+def slot_kernel(chan, patch_col, patch_row, source, node, *rest):
+    kept, (pick, meta, out_cols, out_rows, *copies) = rest[: len(KEPT)], rest[len(KEPT) :]
+    for held, copy in zip(kept, copies):
+        copy[...] = held[...]
+    own = pl.ds(pl.multiple_of(chan[0] * LANES, LANES), LANES)
+    out_cols[...] = kept[0][:, own]
+    out_rows[...] = kept[0][own, :]
     before = iota((EDGES, EDGES), 0) < iota((EDGES, EDGES), 1)
     same = patch_col[...] == patch_row[...]
     rank = jnp.sum(jnp.where(same & before, 1.0, 0.0), axis=0, keepdims=True)
@@ -296,6 +302,9 @@
         small[...] = rows[0:1] + rows[1:2]
 
 
+KEPT = ("w_out", "edge_bias", "norm_gain", "mesh_latent", "cotangent")
+
+
 def gather_stage(st):
     args = (st["grid_latent"], st["cotangent"], st["mesh_latent"], st["norm_gain"][None])
     outs = [((CHANS, PACK, LANES), BF)]
@@ -306,15 +315,19 @@
 def send_stage(st):
     offset = st["chan"] * LANES
     st["packed"] = st["got"]
-    for name in ("source", "dest", "out"):
+    for name in ("source", "dest"):
         whole = st["w_" + name]
         st[name + "_cols"] = lax.dynamic_slice_in_dim(whole, offset, LANES, 1)
         st[name + "_rows"] = lax.dynamic_slice_in_dim(whole, offset, LANES, 0)
     patch = st["edge_patch"]
     args = [patch, patch.reshape(1, EDGES), st["edge_source"][None], st["edge_node"][None]]
-    args += [st["edge_bias"][None], st["norm_gain"][None]]
-    outs = [((SLOTS, GRID), BF), ((PATCHES, LANES), BF)] + [((1, LANES), F32)] * 2
-    st["pick"], meta, st["bias"], st["gain"] = call(slot_kernel, outs, args, 1 << 27)
+    kept = [st[name].reshape(-1, st[name].shape[-1]) for name in KEPT]
+    outs = [((SLOTS, GRID), BF), ((PATCHES, LANES), BF), ((LATENT, LANES), BF)]
+    outs += [((LANES, LATENT), BF)] + [(v.shape, v.dtype) for v in kept]
+    args = [st["chan"][None]] + args + kept
+    results = call(slot_kernel, outs, args, 1 << 27, in_specs=scalar_first(args))
+    st["pick"], meta, st["out_cols"], st["out_rows"], *copies = results
+    st["kept"] = dict(zip(KEPT, copies))
     args = (st["packed"], st["pick"], meta, st["source_cols"], st["dest_cols"])
     outs = [((PATCHES, 2 * HALF + 2 * LANES), BF), ((MESH, LANES), F32)]
     sent, st["mesh_proj"] = call(send_kernel, outs, args, 1 << 28)
@@ -325,14 +338,15 @@
 def message_stage(st):
     arrived = st["got"].reshape(PATCHES, 2 * HALF + 2 * LANES)
     outs = [((CHANS, MESH, LANES), BF), ((SLOTS, LANES), F32), ((SLOTS, MESH), BF)]
-    args = (arrived, st["mesh_proj"], st["bias"])
+    args = (arrived, st["mesh_proj"], st["kept"]["edge_bias"])
     st["sent"], st["pre"], st["chosen"] = call(message_kernel, outs, args, 1 << 27)
     return st
 
 
 def node_stage(st):
-    args = [st["packed"], st["got"], st["pre"], st["chosen"], st["w_out"], st["out_cols"]]
-    args += [st["out_rows"], st["mesh_latent"], st["cotangent"], st["gain"]]
+    kept = st["kept"]
+    args = [st["packed"], st["got"], st["pre"], st["chosen"], kept["w_out"], st["out_cols"]]
+    args += [st["out_rows"], kept["mesh_latent"], kept["cotangent"], kept["norm_gain"]]
     outs = [((MESH, LANES), BF), ((PATCHES, 2 * HALF), BF), ((MESH, LANES), BF)]
     outs += [((LATENT, LANES), BF)] * 2 + [((1, LANES), F32)] * 2
     st["updated"], grads, *st["partial"] = call(node_kernel, outs, args, 1 << 28)
@@ -357,9 +371,9 @@
 
 def back_stage(st):
     args = (st["chan"][None], st["near"], st["got"])
-    args += (st["source_rows"], st["dest_rows"], st["cotangent"])
+    args += (st["source_rows"], st["dest_rows"], st["kept"]["cotangent"])
     outs = [((GRID, LANES), BF), ((MESH, LANES), BF)]
-    specs = [pl.BlockSpec(memory_space=pltpu.SMEM)] + [pl.BlockSpec()] * (len(args) - 1)
+    specs = scalar_first(args)
     st["grad_grid"], st["grad_mesh"] = call(back_kernel, outs, args, 1 << 26, in_specs=specs)
     st["sent"] = st["params"]
     return st

time: 162 us -> 160 us (0.988)
  blocking collectives: 62.7 us -> 116 us
  waiting for transfers between devices: 40.6 us -> 10.9 us
  starting transfers between devices: 42.5 us -> 17.6 us
    all_to_all x3 -> x5, blocking collectives: 62.7 us -> 116 us  [on_device(): st['got'] = lax.all_to_all(st['sent'], axes, 0, 0, tiled=True)]
    all_to_all x4 -> x2, waiting for transfers between devices: 32.7 us -> 2.97 us  [on_device(): st['got'] = lax.all_to_all(st['sent'], axes, 0, 0, tiled=True)]
    all_to_all x4 -> x2, starting transfers between devices: 37.7 us -> 12.8 us  [on_device(): st['got'] = lax.all_to_all(st['sent'], axes, 0, 0, tiled=True)]
  transfers between devices with their start and end apart: 6 -> 4, of which waited for: 5 -> 3; matrix products, arithmetic and copies ran while one was open for 1% -> 1% of each run, Pallas kernels for 1% -> 1%
where the time goes in v5:
time: 160 us; the launch traced here: 159 us
  blocking collectives  116 us (72%)
  starting transfers between devices  17.6 us (11%)
  waiting for transfers between devices  10.9 us (7%)
  Pallas kernels  9.38 us (6%)
  local copies, waits for them, and re-layouts  3.73 us (2%)
    all_to_all x5, blocking collectives, on_device(): st['got'] = lax.all_to_all(st['sent'], axes, 0, 0, tiled=True)  116 us
    all_to_all x2, starting transfers between devices, on_device(): st['got'] = lax.all_to_all(st['sent'], axes, 0, 0, tiled=True)  12.8 us
    pallas_call x11, Pallas kernels, call(): pl.pallas_call(kernel, out_shape=shapes, compiler_params=pltpu.CompilerPa...  9.38 us
    ppermute x2, waiting for transfers between devices, on_device(): lax.ppermute(st['sent'], 'y', [(i, i ^ axes) for i in range(CHANS)])  7.94 us
    ppermute x2, starting transfers between devices, on_device(): lax.ppermute(st['sent'], 'y', [(i, i ^ axes) for i in range(CHANS)])  4.82 us
  transfers between devices with their start and end apart: 4, of which 3 were waited for; matrix products, arithmetic and copies ran while one was open for 1% of the time, Pallas kernels for 1%

profile of v5, /device:TPU:1, one launch (start us, length us, event | category | flops | bytes accessed | tf_op | source)
XLA Modules:
  0.0 158.9 jit_solution(5421484253078882435)
XLA Ops:
  0.6 1.7 %shard_map.170 = bf16[4,400,128]{2,1,0:T(8,128)(2,1)} custom-call(bf16[256,128]{1,0:T(8,128)(2,1)} %grid.1, bf16[64,128]{1,0:T(8,128)(2,1)} %rest_4_.1, bf16[64,128]{1,0:T(8,128)(2,1)} %rest_3_.1, f32[1,128]{1,0:T(1,128)} %bitcast.17), custom_call_target="tpu_custom_call" | custom-call | flops 1048576 | bytes 1048576 | tf_op jit(solution)/shard_map/pallas_call | solution.py:58
  2.4 5.1 %all-to-all-start = ((bf16[4,400,128]{2,1,0:T(8,128)(2,1)}), bf16[4,400,128]{2,1,0:T(8,128)(2,1)S(1)}, u32[]{:S(2)}, u32[]{:S(2)}) async-start(bf16[4,400,128]{2,1,0:T(8,128)(2,1)} %shard_map.170), calls=%async_computation | async-start | bytes 819200 | tf_op jit(solution)/shard_map/all_to_all | solution.py:437
  7.5 0.7 copy-done.3
  8.2 0.1 copy.19.patch_col
  8.3 0.0 copy-start.1
  8.4 0.0 copy-start.6
  8.4 0.5 copy-done.2
  8.9 0.2 copy-done.1
  9.1 0.8 shard_map.171
  9.9 0.9 constant_dynamic-slice_fusion.2
  10.9 3.0 %all-to-all-done.packed = bf16[4,400,128]{2,1,0:T(8,128)(2,1)S(1)} async-done(((bf16[4,400,128]{2,1,0:T(8,128)(2,1)}), bf16[4,400,128]{2,1,0:T(8,128)(2,1)S(1)}, u32[]{:S(2)}, u32[]{:S(2)}) %all-to-all-start) | async-done | bytes 409632 | tf_op jit(solution)/shard_map/all_to_all | solution.py:437
  13.8 0.6 shard_map.172
  14.4 0.1 reshape.43
  14.5 46.9 %all_to_all.35 = bf16[128,2,640]{2,1,0:T(2,128)(2,1)S(1)} all-to-all(bf16[128,2,640]{2,1,0:T(2,128)(2,1)S(1)} %reshape.43), channel_id=1, replica_groups=mesh['x'=4,'zh'=8,'zl'=2,'c'=2,'y'=4] {'x','zh','zl','c'}, dimensions={0} | all-to-all | bytes 655360 | tf_op jit(solution)/shard_map/all_to_all | solution.py:437
  61.5 0.7 shard_map.173
  62.2 6.8 %all_to_all.36.summed = bf16[4,64,128]{2,1,0:T(8,128)(2,1)S(1)} all-to-all(bf16[4,64,128]{2,1,0:T(8,128)(2,1)S(1)} %get-tuple-element.43), channel_id=1, replica_groups=mesh['x'=4,'zh'=8,'zl'=2,'c'=2,'y'=4] {'y'}, dimensions={0} | all-to-all | bytes 131072 | tf_op jit(solution)/shard_map/all_to_all | solution.py:437
  69.0 2.2 %shard_map.174 = (bf16[64,128]{1,0:T(8,128)(2,1)}, bf16[128,1024]{1,0:T(8,128)(2,1)S(1)}, bf16[64,128]{1,0:T(8,128)(2,1)S(1)}, bf16[512,128]{1,0:T(8,128)(2,1)S(...) custom-call(bf16[4,400,128]{2,1,0:T(8,128)(2,1)S(1)} %all-to-all-done.packed, ...), custom_call_target="tpu_custom_call" | custom-call | flops 268435456 | bytes 1048576 | tf_op jit(solution)/shard_map/pallas_call | solution.py:58
  71.2 0.2 reshape.45
  71.4 30.0 %all_to_all.37 = bf16[128,2,512]{2,1,0:T(2,128)(2,1)S(1)} all-to-all(bf16[128,2,512]{2,1,0:T(2,128)(2,1)S(1)} %reshape.45), channel_id=1, replica_groups=mesh['x'=4,'zh'=8,'zl'=2,'c'=2,'y'=4] {'x','zh','zl','c'}, dimensions={0} | all-to-all | bytes 524288 | tf_op jit(solution)/shard_map/all_to_all | solution.py:437
  101.4 0.6 shard_map.175
  102.1 13.8 %all_to_all.38.parts = bf16[16,104,128]{2,1,0:T(8,128)(2,1)S(1)} all-to-all(bf16[16,104,128]{2,1,0:T(8,128)(2,1)S(1)} %get-tuple-element.62), channel_id=1, replica_groups=mesh['x'=4,'zh'=8,'zl'=2,'c'=2,'y'=4] {'x','zl','c'}, dimensions={0} | all-to-all | bytes 851968 | tf_op jit(solution)/shard_map/all_to_all | solution.py:437
  115.8 0.1 shard_map.178
  115.9 18.9 %all_to_all.39.parts = bf16[8,104,128]{2,1,0:T(8,128)(2,1)S(1)} all-to-all(bf16[8,104,128]{2,1,0:T(8,128)(2,1)S(1)} %shard_map.178), channel_id=1, replica_groups=mesh['x'=4,'zh'=8,'zl'=2,'c'=2,'y'=4] {'zh'}, dimensions={0} | all-to-all | bytes 425984 | tf_op jit(solution)/shard_map/all_to_all | solution.py:437
  134.9 0.8 shard_map.179
  135.7 7.6 %all-to-all-start.6 = ((bf16[16,104,128]{2,1,0:T(8,128)(2,1)}), bf16[16,104,128]{2,1,0:T(8,128)(2,1)S(1)}, u32[]{:S(2)}, u32[]{:S(2)}) async-start(bf16[16,104,128]{2,1,0:T(8,128)(2,1)} %shard_map.179), calls=%async_computation.6 | async-start | bytes 851968 | tf_op jit(solution)/shard_map/all_to_all | solution.py:437
  143.3 2.2 %collective-permute-start = (bf16[320,128]{1,0:T(8,128)(2,1)S(1)}, bf16[320,128]{1,0:T(8,128)(2,1)S(1)}, u32[]{:S(2)}, u32[]{:S(2)}) collective-permute-start(bf16[320,128]{1,0:T(8,128)(2,1)S(1)} %get-tuple-element.59.own), channel_id=1, source_target_pairs={{0,1},{1,0},{2,3},{3,2},{4,5},{5,4},{6,7},{7,6},{8,9},{9,8},{10,11... | collective-permute-start | bytes 245768 | tf_op jit(solution)/shard_map/ppermute | solution.py:435
  145.5 3.5 %collective-permute-done.other = bf16[320,128]{1,0:T(8,128)(2,1)S(1)} collective-permute-done((bf16[320,128]{1,0:T(8,128)(2,1)S(1)}, bf16[320,128]{1,0:T(8,128)(2,1)S(1)}, u32[]{:S(2)}, u32[]{:S(2)}) %collective-permute-start) | collective-permute-done | bytes 81952 | tf_op jit(solution)/shard_map/ppermute | solution.py:435
  149.0 2.6 %collective-permute-start.1 = (bf16[2,320,128]{2,1,0:T(8,128)(2,1)S(1)}, bf16[2,320,128]{2,1,0:T(8,128)(2,1)S(1)}, u32[]{:S(2)}, u32[]{:S(2)}) collective-permute-start(bf16[2,320,128]{2,1,0:T(8,128)(2,1)S(1)} %shard_map.176.near), channel_id=1, source_target_pairs={{0,2},{1,3},{2,0},{3,1},{4,6},{5,7},{6,4},{7,5},{8,10},{9,11},{10,... | collective-permute-start | bytes 491528 | tf_op jit(solution)/shard_map/ppermute | solution.py:435
  151.6 0.9 constant_dynamic-slice_fusion
  152.5 4.5 %collective-permute-done.1.far = bf16[2,320,128]{2,1,0:T(8,128)(2,1)S(1)} collective-permute-done((bf16[2,320,128]{2,1,0:T(8,128)(2,1)S(1)}, bf16[2,320,128]{2,1,0:T(8,128)(2,1)S(1)}, u32[]{:S(2)}, u32[]{:S(2)}) %collective-permute-start.1) | collective-permute-done | bytes 163872 | tf_op jit(solution)/shard_map/ppermute | solution.py:435
  157.0 0.9 shard_map.177
  158.0 0.9 shard_map.180
  (17 shorter events, 0.1 us)
Async XLA Ops:
  0.6 9.3 %copy-start.8 = (bf16[512,512]{1,0:T(8,128)(2,1)S(1)}, bf16[512,512]{1,0:T(8,128)(2,1)}, u32[]{:S(2)}) copy-start(bf16[512,512]{1,0:T(8,128)(2,1)} %param.14) | copy-start | bytes 1572868
  2.4 6.0 %copy-start = (bf16[512,512]{1,0:T(8,128)(2,1)S(1)}, bf16[512,512]{1,0:T(8,128)(2,1)}, u32[]{:S(2)}) copy-start(bf16[512,512]{1,0:T(8,128)(2,1)} %rest_0_.1) | copy-start | bytes 1572868
  2.4 11.5 %all-to-all-start = ((bf16[4,400,128]{2,1,0:T(8,128)(2,1)}), bf16[4,400,128]{2,1,0:T(8,128)(2,1)S(1)}, u32[]{:S(2)}, u32[]{:S(2)}) async-start(bf16[4,400,128]{2,1,0:T(8,128)(2,1)} %shard_map.170), calls=%async_computation | async-start | bytes 819200 | tf_op jit(solution)/shard_map/all_to_all | solution.py:437
  7.5 0.7 copy-start.3
  8.2 0.7 copy-start.2
  8.2 0.7 copy-start.4
  8.2 0.7 copy-start.5
  8.3 0.7 copy-start.1
  8.4 0.7 copy-start.6
  8.4 0.7 copy-start.7
  135.7 22.3 %all-to-all-start.6 = ((bf16[16,104,128]{2,1,0:T(8,128)(2,1)}), bf16[16,104,128]{2,1,0:T(8,128)(2,1)S(1)}, u32[]{:S(2)}, u32[]{:S(2)}) async-start(bf16[16,104,128]{2,1,0:T(8,128)(2,1)} %shard_map.179), calls=%async_computation.6 | async-start | bytes 851968 | tf_op jit(solution)/shard_map/all_to_all | solution.py:437
  143.3 5.6 %collective-permute-start = (bf16[320,128]{1,0:T(8,128)(2,1)S(1)}, bf16[320,128]{1,0:T(8,128)(2,1)S(1)}, u32[]{:S(2)}, u32[]{:S(2)}) collective-permute-start(bf16[320,128]{1,0:T(8,128)(2,1)S(1)} %get-tuple-element.59.own), channel_id=1, source_target_pairs={{0,1},{1,0},{2,3},{3,2},{4,5},{5,4},{6,7},{7,6},{8,9},{9,8},{10,11... | collective-permute-start | bytes 245768 | tf_op jit(solution)/shard_map/ppermute | solution.py:435
  149.0 8.1 %collective-permute-start.1 = (bf16[2,320,128]{2,1,0:T(8,128)(2,1)S(1)}, bf16[2,320,128]{2,1,0:T(8,128)(2,1)S(1)}, u32[]{:S(2)}, u32[]{:S(2)}) collective-permute-start(bf16[2,320,128]{2,1,0:T(8,128)(2,1)S(1)} %shard_map.176.near), channel_id=1, source_target_pairs={{0,2},{1,3},{2,0},{3,1},{4,6},{5,7},{6,4},{7,5},{8,10},{9,11},{10,... | collective-permute-start | bytes 491528 | tf_op jit(solution)/shard_map/ppermute | solution.py:435

commit v6 on v5

--- a/solution.py
+++ b/solution.py
@@ -47,6 +47,10 @@
 
 def iota(shape, dim):
     return lax.broadcasted_iota(jnp.int32, shape, dim)
+
+
+def joined(blocks):
+    return jnp.concatenate(blocks, axis=1)
 
 
 def cols(j):
@@ -175,53 +179,38 @@
     bias_part,
     gain_part,
 ):
-    mixed = jnp.zeros((MESH, LATENT), F32)
-    own = jnp.zeros((MESH, LANES), F32)
-    for j in range(CHANS):
-        mixed += dot(summed[j], w_out[cols(j)])
-        own += dot(summed[j], out_cols[cols(j)])
+    whole = joined([summed[j] for j in range(CHANS)])
+    mixed = dot(whole, w_out[...])
+    own = dot(whole, out_cols[...])
     mean = jnp.sum(mixed, axis=1, keepdims=True) / LATENT
     apart = mixed - mean
     inv = lax.rsqrt(jnp.sum(apart * apart, axis=1, keepdims=True) / LATENT + NORM_EPS)
     normed = apart * inv
-    scaled, first, second = [], 0.0, 0.0
-    for j in range(CHANS):
-        parts = packed[j, GAIN_AT:PACK].astype(F32)
-        whole = parts[0:1] + parts[1:2] + parts[2:3]
-        part = packed[j, COT_AT:MESH_AT].astype(F32) * whole
-        scaled.append(part)
-        first += jnp.sum(part, axis=1, keepdims=True)
-        second += jnp.sum(part * normed[:, cols(j)], axis=1, keepdims=True)
-    first, second = first / LATENT, second / LATENT
+    parts = joined([packed[j, GAIN_AT:PACK] for j in range(CHANS)]).astype(F32)
+    scaled = joined([packed[j, COT_AT:MESH_AT] for j in range(CHANS)]).astype(F32)
+    scaled = scaled * (parts[0:1] + parts[1:2] + parts[2:3])
+    first = jnp.sum(scaled, axis=1, keepdims=True) / LATENT
+    second = jnp.sum(scaled * normed, axis=1, keepdims=True) / LATENT
+    part = ((scaled - first - normed * second) * inv).astype(BF)
+    back = dot(part, out_rows[...], ((1,), (1,)))
+    there = dot(chosen[...], joined(two_parts(back)))
+    value = pre[...]
+    gate = jax.nn.sigmoid(value)
+    slope = gate * (1.0 + value * (1.0 - gate))
+    grad = ((there[:, 0:LANES] + there[:, LANES : 2 * LANES]) * slope).astype(BF)
+    for r in range(CAP):
+        grads[:, cols(r)] = grad[r * PATCHES : (r + 1) * PATCHES]
+    bias_part[...] = jnp.sum(grad.astype(F32), axis=0, keepdims=True)
+    total = dot(chosen[...], grad, ((0,), (0,))).astype(BF)
+    node_grad[...] = total
+    nodes = joined([packed[j, MESH_AT:GAIN_AT] for j in range(CHANS)])
+    dest_part[...] = dot(nodes, total, ((0,), (0,))).astype(BF)
     own_normed = (own - mean) * inv
     cotangent = cot[...].astype(F32)
     updated[...] = (mesh[...].astype(F32) + own_normed * gain[...]).astype(BF)
     gain_part[...] = jnp.sum(cotangent * own_normed, axis=0, keepdims=True)
     own_grad = ((cotangent * gain[...] - first - own_normed * second) * inv).astype(BF)
-    back = jnp.zeros((MESH, LANES), F32)
-    for j in range(CHANS):
-        out_part[cols(j)] = dot(summed[j], own_grad, ((0,), (0,))).astype(BF)
-        part = ((scaled[j] - first - normed[:, cols(j)] * second) * inv).astype(BF)
-        back += dot(part, out_rows[:, cols(j)], ((1,), (1,)))
-    both = jnp.concatenate(two_parts(back), axis=1)
-    bias = jnp.zeros((1, LANES), F32)
-    total = jnp.zeros((MESH, LANES), F32)
-    for r in range(CAP):
-        at = slice(r * PATCHES, (r + 1) * PATCHES)
-        mine = chosen[at]
-        there = dot(mine, both)
-        value = pre[at]
-        gate = jax.nn.sigmoid(value)
-        slope = gate * (1.0 + value * (1.0 - gate))
-        grad = ((there[:, 0:LANES] + there[:, LANES : 2 * LANES]) * slope).astype(BF)
-        grads[:, cols(r)] = grad
-        bias += jnp.sum(grad.astype(F32), axis=0, keepdims=True)
-        total += dot(mine, grad, ((0,), (0,)))
-    bias_part[...] = bias
-    total = total.astype(BF)
-    node_grad[...] = total
-    for j in range(CHANS):
-        dest_part[cols(j)] = dot(packed[j, MESH_AT:GAIN_AT], total, ((0,), (0,))).astype(BF)
+    out_part[...] = dot(whole, own_grad, ((0,), (0,))).astype(BF)
 
 
 def place(row):
@@ -272,7 +261,8 @@
     on_mesh = cot[...].astype(F32)
     for k in range(CHANS):
         block = (near, far)[k // 2]
-        at = pl.multiple_of(lax.bitwise_xor(chan[0], jnp.int32(k)) * LANES, LANES)
+        other = lax.bitwise_xor(chan[0], jnp.int32((0, 2, 1, 3)[k]))
+        at = pl.multiple_of(other * LANES, LANES)
         there = pl.ds(at, LANES)
         on_grid += dot(block[k % 2, 0:GRID], source_rows[:, there], ((1,), (1,)))
         on_mesh += dot(block[k % 2, GRID : GRID + MESH], dest_rows[:, there], ((1,), (1,)))
@@ -403,8 +393,8 @@
     (send_stage, PATCH),
     (message_stage, "y"),
     (node_stage, PATCH),
-    (grid_stage, 1),
-    (join_stage, 2),
+    (grid_stage, 2),
+    (join_stage, 1),
     (back_stage, NEAR),
     (far_stage, "zh"),
     (near_stage, NEAR),

time: 160 us -> 159 us (level)
  no operation moved by 1% of the time
where the time goes in v6:
time: 159 us; the launch traced here: 158 us
  blocking collectives  116 us (73%)
  starting transfers between devices  17.6 us (11%)
  waiting for transfers between devices  10.9 us (7%)
  Pallas kernels  8.81 us (6%)
  local copies, waits for them, and re-layouts  3.73 us (2%)
    all_to_all x5, blocking collectives, on_device(): st['got'] = lax.all_to_all(st['sent'], axes, 0, 0, tiled=True)  116 us
    all_to_all x2, starting transfers between devices, on_device(): st['got'] = lax.all_to_all(st['sent'], axes, 0, 0, tiled=True)  12.8 us
    pallas_call x11, Pallas kernels, call(): pl.pallas_call(kernel, out_shape=shapes, compiler_params=pltpu.CompilerPa...  8.81 us
    ppermute x2, waiting for transfers between devices, on_device(): lax.ppermute(st['sent'], 'y', [(i, i ^ axes) for i in range(CHANS)])  7.96 us
    ppermute x2, starting transfers between devices, on_device(): lax.ppermute(st['sent'], 'y', [(i, i ^ axes) for i in range(CHANS)])  4.81 us
  transfers between devices with their start and end apart: 4, of which 3 were waited for; matrix products, arithmetic and copies ran while one was open for 1% of the time, Pallas kernels for 1%

profile of v6, /device:TPU:1, one launch (start us, length us, event | category | flops | bytes accessed | tf_op | source)
XLA Modules:
  0.0 158.3 jit_solution(2884569358346080454)
XLA Ops:
  0.6 1.7 %shard_map.170 = bf16[4,400,128]{2,1,0:T(8,128)(2,1)} custom-call(bf16[256,128]{1,0:T(8,128)(2,1)} %grid.1, bf16[64,128]{1,0:T(8,128)(2,1)} %rest_4_.1, bf16[64,128]{1,0:T(8,128)(2,1)} %rest_3_.1, f32[1,128]{1,0:T(1,128)} %bitcast.17), custom_call_target="tpu_custom_call" | custom-call | flops 1048576 | bytes 1048576 | tf_op jit(solution)/shard_map/pallas_call | solution.py:62
  2.4 5.1 %all-to-all-start = ((bf16[4,400,128]{2,1,0:T(8,128)(2,1)}), bf16[4,400,128]{2,1,0:T(8,128)(2,1)S(1)}, u32[]{:S(2)}, u32[]{:S(2)}) async-start(bf16[4,400,128]{2,1,0:T(8,128)(2,1)} %shard_map.170), calls=%async_computation | async-start | bytes 819200 | tf_op jit(solution)/shard_map/all_to_all | solution.py:427
  7.5 0.7 copy-done.3
  8.2 0.1 copy.19.patch_col
  8.3 0.0 copy-start.1
  8.4 0.0 copy-start.6
  8.4 0.5 copy-done.2
  8.9 0.2 copy-done.1
  9.1 0.8 shard_map.171
  9.9 0.9 constant_dynamic-slice_fusion.2
  10.9 3.0 %all-to-all-done.packed = bf16[4,400,128]{2,1,0:T(8,128)(2,1)S(1)} async-done(((bf16[4,400,128]{2,1,0:T(8,128)(2,1)}), bf16[4,400,128]{2,1,0:T(8,128)(2,1)S(1)}, u32[]{:S(2)}, u32[]{:S(2)}) %all-to-all-start) | async-done | bytes 409632 | tf_op jit(solution)/shard_map/all_to_all | solution.py:427
  13.8 0.6 shard_map.172
  14.4 0.1 reshape.43
  14.5 46.9 %all_to_all.35 = bf16[128,2,640]{2,1,0:T(2,128)(2,1)S(1)} all-to-all(bf16[128,2,640]{2,1,0:T(2,128)(2,1)S(1)} %reshape.43), channel_id=1, replica_groups=mesh['x'=4,'zh'=8,'zl'=2,'c'=2,'y'=4] {'x','zh','zl','c'}, dimensions={0} | all-to-all | bytes 655360 | tf_op jit(solution)/shard_map/all_to_all | solution.py:427
  61.5 0.7 shard_map.173
  62.2 6.8 %all_to_all.36.summed = bf16[4,64,128]{2,1,0:T(8,128)(2,1)S(1)} all-to-all(bf16[4,64,128]{2,1,0:T(8,128)(2,1)S(1)} %get-tuple-element.43), channel_id=1, replica_groups=mesh['x'=4,'zh'=8,'zl'=2,'c'=2,'y'=4] {'y'}, dimensions={0} | all-to-all | bytes 131072 | tf_op jit(solution)/shard_map/all_to_all | solution.py:427
  69.0 1.6 %shard_map.174 = (bf16[64,128]{1,0:T(8,128)(2,1)}, bf16[128,1024]{1,0:T(8,128)(2,1)S(1)}, bf16[64,128]{1,0:T(8,128)(2,1)S(1)}, bf16[512,128]{1,0:T(8,128)(2,1)S(...) custom-call(bf16[4,400,128]{2,1,0:T(8,128)(2,1)S(1)} %all-to-all-done.packed, ...), custom_call_target="tpu_custom_call" | custom-call | flops 268435456 | bytes 1048576 | tf_op jit(solution)/shard_map/pallas_call | solution.py:62
  70.6 0.2 reshape.45
  70.8 30.0 %all_to_all.37 = bf16[128,2,512]{2,1,0:T(2,128)(2,1)S(1)} all-to-all(bf16[128,2,512]{2,1,0:T(2,128)(2,1)S(1)} %reshape.45), channel_id=1, replica_groups=mesh['x'=4,'zh'=8,'zl'=2,'c'=2,'y'=4] {'x','zh','zl','c'}, dimensions={0} | all-to-all | bytes 524288 | tf_op jit(solution)/shard_map/all_to_all | solution.py:427
  100.9 0.6 shard_map.175
  101.5 13.8 %all_to_all.38.parts = bf16[16,104,128]{2,1,0:T(8,128)(2,1)S(1)} all-to-all(bf16[16,104,128]{2,1,0:T(8,128)(2,1)S(1)} %get-tuple-element.62), channel_id=1, replica_groups=mesh['x'=4,'zh'=8,'zl'=2,'c'=2,'y'=4] {'x','zl','c'}, dimensions={0} | all-to-all | bytes 851968 | tf_op jit(solution)/shard_map/all_to_all | solution.py:427
  115.3 0.1 shard_map.178
  115.4 18.9 %all_to_all.39.parts = bf16[8,104,128]{2,1,0:T(8,128)(2,1)S(1)} all-to-all(bf16[8,104,128]{2,1,0:T(8,128)(2,1)S(1)} %shard_map.178), channel_id=1, replica_groups=mesh['x'=4,'zh'=8,'zl'=2,'c'=2,'y'=4] {'zh'}, dimensions={0} | all-to-all | bytes 425984 | tf_op jit(solution)/shard_map/all_to_all | solution.py:427
  134.3 0.8 shard_map.179
  135.1 7.6 %all-to-all-start.6 = ((bf16[16,104,128]{2,1,0:T(8,128)(2,1)}), bf16[16,104,128]{2,1,0:T(8,128)(2,1)S(1)}, u32[]{:S(2)}, u32[]{:S(2)}) async-start(bf16[16,104,128]{2,1,0:T(8,128)(2,1)} %shard_map.179), calls=%async_computation.6 | async-start | bytes 851968 | tf_op jit(solution)/shard_map/all_to_all | solution.py:427
  142.7 2.6 %collective-permute-start = (bf16[320,128]{1,0:T(8,128)(2,1)S(1)}, bf16[320,128]{1,0:T(8,128)(2,1)S(1)}, u32[]{:S(2)}, u32[]{:S(2)}) collective-permute-start(bf16[320,128]{1,0:T(8,128)(2,1)S(1)} %get-tuple-element.59.own), channel_id=1, source_target_pairs={{0,2},{1,3},{2,0},{3,1},{4,6},{5,7},{6,4},{7,5},{8,10},{9,11},{10,... | collective-permute-start | bytes 245768 | tf_op jit(solution)/shard_map/ppermute | solution.py:425
  145.4 4.5 %collective-permute-done.other = bf16[320,128]{1,0:T(8,128)(2,1)S(1)} collective-permute-done((bf16[320,128]{1,0:T(8,128)(2,1)S(1)}, bf16[320,128]{1,0:T(8,128)(2,1)S(1)}, u32[]{:S(2)}, u32[]{:S(2)}) %collective-permute-start) | collective-permute-done | bytes 81952 | tf_op jit(solution)/shard_map/ppermute | solution.py:425
  149.9 2.2 %collective-permute-start.1 = (bf16[2,320,128]{2,1,0:T(8,128)(2,1)S(1)}, bf16[2,320,128]{2,1,0:T(8,128)(2,1)S(1)}, u32[]{:S(2)}, u32[]{:S(2)}) collective-permute-start(bf16[2,320,128]{2,1,0:T(8,128)(2,1)S(1)} %shard_map.176.near), channel_id=1, source_target_pairs={{0,1},{1,0},{2,3},{3,2},{4,5},{5,4},{6,7},{7,6},{8,9},{9,8},{10,11... | collective-permute-start | bytes 491528 | tf_op jit(solution)/shard_map/ppermute | solution.py:425
  152.1 0.9 constant_dynamic-slice_fusion
  153.0 3.4 %collective-permute-done.1.far = bf16[2,320,128]{2,1,0:T(8,128)(2,1)S(1)} collective-permute-done((bf16[2,320,128]{2,1,0:T(8,128)(2,1)S(1)}, bf16[2,320,128]{2,1,0:T(8,128)(2,1)S(1)}, u32[]{:S(2)}, u32[]{:S(2)}) %collective-permute-start.1) | collective-permute-done | bytes 163872 | tf_op jit(solution)/shard_map/ppermute | solution.py:425
  156.5 0.9 shard_map.177
  157.4 0.9 shard_map.180
  (17 shorter events, 0.1 us)
Async XLA Ops:
  0.6 9.3 %copy-start.8 = (bf16[512,512]{1,0:T(8,128)(2,1)S(1)}, bf16[512,512]{1,0:T(8,128)(2,1)}, u32[]{:S(2)}) copy-start(bf16[512,512]{1,0:T(8,128)(2,1)} %param.14) | copy-start | bytes 1572868
  2.4 6.0 %copy-start = (bf16[512,512]{1,0:T(8,128)(2,1)S(1)}, bf16[512,512]{1,0:T(8,128)(2,1)}, u32[]{:S(2)}) copy-start(bf16[512,512]{1,0:T(8,128)(2,1)} %rest_0_.1) | copy-start | bytes 1572868
  2.4 11.5 %all-to-all-start = ((bf16[4,400,128]{2,1,0:T(8,128)(2,1)}), bf16[4,400,128]{2,1,0:T(8,128)(2,1)S(1)}, u32[]{:S(2)}, u32[]{:S(2)}) async-start(bf16[4,400,128]{2,1,0:T(8,128)(2,1)} %shard_map.170), calls=%async_computation | async-start | bytes 819200 | tf_op jit(solution)/shard_map/all_to_all | solution.py:427
  7.5 0.7 copy-start.3
  8.2 0.7 copy-start.2
  8.2 0.7 copy-start.4
  8.2 0.7 copy-start.5
  8.3 0.7 copy-start.1
  8.4 0.7 copy-start.6
  8.4 0.7 copy-start.7
  135.1 22.3 %all-to-all-start.6 = ((bf16[16,104,128]{2,1,0:T(8,128)(2,1)}), bf16[16,104,128]{2,1,0:T(8,128)(2,1)S(1)}, u32[]{:S(2)}, u32[]{:S(2)}) async-start(bf16[16,104,128]{2,1,0:T(8,128)(2,1)} %shard_map.179), calls=%async_computation.6 | async-start | bytes 851968 | tf_op jit(solution)/shard_map/all_to_all | solution.py:427
  142.7 7.2 %collective-permute-start = (bf16[320,128]{1,0:T(8,128)(2,1)S(1)}, bf16[320,128]{1,0:T(8,128)(2,1)S(1)}, u32[]{:S(2)}, u32[]{:S(2)}) collective-permute-start(bf16[320,128]{1,0:T(8,128)(2,1)S(1)} %get-tuple-element.59.own), channel_id=1, source_target_pairs={{0,2},{1,3},{2,0},{3,1},{4,6},{5,7},{6,4},{7,5},{8,10},{9,11},{10,... | collective-permute-start | bytes 245768 | tf_op jit(solution)/shard_map/ppermute | solution.py:425
  149.9 6.6 %collective-permute-start.1 = (bf16[2,320,128]{2,1,0:T(8,128)(2,1)S(1)}, bf16[2,320,128]{2,1,0:T(8,128)(2,1)S(1)}, u32[]{:S(2)}, u32[]{:S(2)}) collective-permute-start(bf16[2,320,128]{2,1,0:T(8,128)(2,1)S(1)} %shard_map.176.near), channel_id=1, source_target_pairs={{0,1},{1,0},{2,3},{3,2},{4,5},{5,4},{6,7},{7,6},{8,9},{9,8},{10,11... | collective-permute-start | bytes 491528 | tf_op jit(solution)/shard_map/ppermute | solution.py:425

commit v7 on v6

--- a/solution.py
+++ b/solution.py
@@ -261,7 +261,7 @@
     on_mesh = cot[...].astype(F32)
     for k in range(CHANS):
         block = (near, far)[k // 2]
-        other = lax.bitwise_xor(chan[0], jnp.int32((0, 2, 1, 3)[k]))
+        other = lax.bitwise_xor(chan[0], jnp.int32((0, 1, 3, 2)[k]))
         at = pl.multiple_of(other * LANES, LANES)
         there = pl.ds(at, LANES)
         on_grid += dot(block[k % 2, 0:GRID], source_rows[:, there], ((1,), (1,)))
@@ -393,8 +393,8 @@
     (send_stage, PATCH),
     (message_stage, "y"),
     (node_stage, PATCH),
-    (grid_stage, 2),
-    (join_stage, 1),
+    (grid_stage, 1),
+    (join_stage, 3),
     (back_stage, NEAR),
     (far_stage, "zh"),
     (near_stage, NEAR),
@@ -421,7 +421,7 @@
     st["chan"] = lax.axis_index("y")
     for stage, axes in STAGES:
         st = stage(st)
-        if axes in (1, 2):
+        if axes in (1, 3):
             st["got"] = lax.ppermute(st["sent"], "y", [(i, i ^ axes) for i in range(CHANS)])
         elif axes is not None:
             st["got"] = lax.all_to_all(st["sent"], axes, 0, 0, tiled=True)

time: 159 us -> 159 us (level)
  no operation moved by 1% of the time
where the time goes in v7:
time: 159 us; the launch traced here: 158 us
  blocking collectives  116 us (73%)
  starting transfers between devices  17.8 us (11%)
  waiting for transfers between devices  10.5 us (7%)
  Pallas kernels  8.82 us (6%)
  local copies, waits for them, and re-layouts  3.73 us (2%)
    all_to_all x5, blocking collectives, on_device(): st['got'] = lax.all_to_all(st['sent'], axes, 0, 0, tiled=True)  116 us
    all_to_all x2, starting transfers between devices, on_device(): st['got'] = lax.all_to_all(st['sent'], axes, 0, 0, tiled=True)  12.8 us
    pallas_call x11, Pallas kernels, call(): pl.pallas_call(kernel, out_shape=shapes, compiler_params=pltpu.CompilerPa...  8.82 us
    ppermute x2, waiting for transfers between devices, on_device(): lax.ppermute(st['sent'], 'y', [(i, i ^ axes) for i in range(CHANS)])  7.49 us
    ppermute x2, starting transfers between devices, on_device(): lax.ppermute(st['sent'], 'y', [(i, i ^ axes) for i in range(CHANS)])  4.98 us
  transfers between devices with their start and end apart: 4, of which 3 were waited for; matrix products, arithmetic and copies ran while one was open for 1% of the time, Pallas kernels for 1%

profile of v7, /device:TPU:1, one launch (start us, length us, event | category | flops | bytes accessed | tf_op | source)
XLA Modules:
  0.0 158.0 jit_solution(10657267812302981132)
XLA Ops:
  0.6 1.7 %shard_map.170 = bf16[4,400,128]{2,1,0:T(8,128)(2,1)} custom-call(bf16[256,128]{1,0:T(8,128)(2,1)} %grid.1, bf16[64,128]{1,0:T(8,128)(2,1)} %rest_4_.1, bf16[64,128]{1,0:T(8,128)(2,1)} %rest_3_.1, f32[1,128]{1,0:T(1,128)} %bitcast.17), custom_call_target="tpu_custom_call" | custom-call | flops 1048576 | bytes 1048576 | tf_op jit(solution)/shard_map/pallas_call | solution.py:62
  2.4 5.1 %all-to-all-start = ((bf16[4,400,128]{2,1,0:T(8,128)(2,1)}), bf16[4,400,128]{2,1,0:T(8,128)(2,1)S(1)}, u32[]{:S(2)}, u32[]{:S(2)}) async-start(bf16[4,400,128]{2,1,0:T(8,128)(2,1)} %shard_map.170), calls=%async_computation | async-start | bytes 819200 | tf_op jit(solution)/shard_map/all_to_all | solution.py:427
  7.5 0.7 copy-done.3
  8.2 0.1 copy.19.patch_col
  8.3 0.0 copy-start.1
  8.4 0.0 copy-start.6
  8.4 0.5 copy-done.2
  8.9 0.2 copy-done.1
  9.1 0.8 shard_map.171
  9.9 0.9 constant_dynamic-slice_fusion.2
  10.9 3.0 %all-to-all-done.packed = bf16[4,400,128]{2,1,0:T(8,128)(2,1)S(1)} async-done(((bf16[4,400,128]{2,1,0:T(8,128)(2,1)}), bf16[4,400,128]{2,1,0:T(8,128)(2,1)S(1)}, u32[]{:S(2)}, u32[]{:S(2)}) %all-to-all-start) | async-done | bytes 409632 | tf_op jit(solution)/shard_map/all_to_all | solution.py:427
  13.8 0.6 shard_map.172
  14.4 0.1 reshape.43
  14.5 46.9 %all_to_all.35 = bf16[128,2,640]{2,1,0:T(2,128)(2,1)S(1)} all-to-all(bf16[128,2,640]{2,1,0:T(2,128)(2,1)S(1)} %reshape.43), channel_id=1, replica_groups=mesh['x'=4,'zh'=8,'zl'=2,'c'=2,'y'=4] {'x','zh','zl','c'}, dimensions={0} | all-to-all | bytes 655360 | tf_op jit(solution)/shard_map/all_to_all | solution.py:427
  61.5 0.7 shard_map.173
  62.2 6.8 %all_to_all.36.summed = bf16[4,64,128]{2,1,0:T(8,128)(2,1)S(1)} all-to-all(bf16[4,64,128]{2,1,0:T(8,128)(2,1)S(1)} %get-tuple-element.43), channel_id=1, replica_groups=mesh['x'=4,'zh'=8,'zl'=2,'c'=2,'y'=4] {'y'}, dimensions={0} | all-to-all | bytes 131072 | tf_op jit(solution)/shard_map/all_to_all | solution.py:427
  69.0 1.6 %shard_map.174 = (bf16[64,128]{1,0:T(8,128)(2,1)}, bf16[128,1024]{1,0:T(8,128)(2,1)S(1)}, bf16[64,128]{1,0:T(8,128)(2,1)S(1)}, bf16[512,128]{1,0:T(8,128)(2,1)S(...) custom-call(bf16[4,400,128]{2,1,0:T(8,128)(2,1)S(1)} %all-to-all-done.packed, ...), custom_call_target="tpu_custom_call" | custom-call | flops 268435456 | bytes 1048576 | tf_op jit(solution)/shard_map/pallas_call | solution.py:62
  70.6 0.2 reshape.45
  70.8 30.0 %all_to_all.37 = bf16[128,2,512]{2,1,0:T(2,128)(2,1)S(1)} all-to-all(bf16[128,2,512]{2,1,0:T(2,128)(2,1)S(1)} %reshape.45), channel_id=1, replica_groups=mesh['x'=4,'zh'=8,'zl'=2,'c'=2,'y'=4] {'x','zh','zl','c'}, dimensions={0} | all-to-all | bytes 524288 | tf_op jit(solution)/shard_map/all_to_all | solution.py:427
  100.9 0.6 shard_map.175
  101.5 13.8 %all_to_all.38.parts = bf16[16,104,128]{2,1,0:T(8,128)(2,1)S(1)} all-to-all(bf16[16,104,128]{2,1,0:T(8,128)(2,1)S(1)} %get-tuple-element.62), channel_id=1, replica_groups=mesh['x'=4,'zh'=8,'zl'=2,'c'=2,'y'=4] {'x','zl','c'}, dimensions={0} | all-to-all | bytes 851968 | tf_op jit(solution)/shard_map/all_to_all | solution.py:427
  115.3 0.1 shard_map.178
  115.4 18.9 %all_to_all.39.parts = bf16[8,104,128]{2,1,0:T(8,128)(2,1)S(1)} all-to-all(bf16[8,104,128]{2,1,0:T(8,128)(2,1)S(1)} %shard_map.178), channel_id=1, replica_groups=mesh['x'=4,'zh'=8,'zl'=2,'c'=2,'y'=4] {'zh'}, dimensions={0} | all-to-all | bytes 425984 | tf_op jit(solution)/shard_map/all_to_all | solution.py:427
  134.3 0.8 shard_map.179
  135.1 7.6 %all-to-all-start.6 = ((bf16[16,104,128]{2,1,0:T(8,128)(2,1)}), bf16[16,104,128]{2,1,0:T(8,128)(2,1)S(1)}, u32[]{:S(2)}, u32[]{:S(2)}) async-start(bf16[16,104,128]{2,1,0:T(8,128)(2,1)} %shard_map.179), calls=%async_computation.6 | async-start | bytes 851968 | tf_op jit(solution)/shard_map/all_to_all | solution.py:427
  142.7 2.2 %collective-permute-start = (bf16[320,128]{1,0:T(8,128)(2,1)S(1)}, bf16[320,128]{1,0:T(8,128)(2,1)S(1)}, u32[]{:S(2)}, u32[]{:S(2)}) collective-permute-start(bf16[320,128]{1,0:T(8,128)(2,1)S(1)} %get-tuple-element.59.own), channel_id=1, source_target_pairs={{0,1},{1,0},{2,3},{3,2},{4,5},{5,4},{6,7},{7,6},{8,9},{9,8},{10,11... | collective-permute-start | bytes 245768 | tf_op jit(solution)/shard_map/ppermute | solution.py:425
  144.9 3.5 %collective-permute-done.other = bf16[320,128]{1,0:T(8,128)(2,1)S(1)} collective-permute-done((bf16[320,128]{1,0:T(8,128)(2,1)S(1)}, bf16[320,128]{1,0:T(8,128)(2,1)S(1)}, u32[]{:S(2)}, u32[]{:S(2)}) %collective-permute-start) | collective-permute-done | bytes 81952 | tf_op jit(solution)/shard_map/ppermute | solution.py:425
  148.4 2.8 %collective-permute-start.1 = (bf16[2,320,128]{2,1,0:T(8,128)(2,1)S(1)}, bf16[2,320,128]{2,1,0:T(8,128)(2,1)S(1)}, u32[]{:S(2)}, u32[]{:S(2)}) collective-permute-start(bf16[2,320,128]{2,1,0:T(8,128)(2,1)S(1)} %shard_map.176.near), channel_id=1, source_target_pairs={{0,3},{1,2},{2,1},{3,0},{4,7},{5,6},{6,5},{7,4},{8,11},{9,10},{10,... | collective-permute-start | bytes 491528 | tf_op jit(solution)/shard_map/ppermute | solution.py:425
  151.2 0.9 constant_dynamic-slice_fusion
  152.1 4.0 %collective-permute-done.1.far = bf16[2,320,128]{2,1,0:T(8,128)(2,1)S(1)} collective-permute-done((bf16[2,320,128]{2,1,0:T(8,128)(2,1)S(1)}, bf16[2,320,128]{2,1,0:T(8,128)(2,1)S(1)}, u32[]{:S(2)}, u32[]{:S(2)}) %collective-permute-start.1) | collective-permute-done | bytes 163872 | tf_op jit(solution)/shard_map/ppermute | solution.py:425
  156.2 0.9 shard_map.177
  157.1 0.9 shard_map.180
  (17 shorter events, 0.1 us)
Async XLA Ops:
  0.6 9.3 %copy-start.8 = (bf16[512,512]{1,0:T(8,128)(2,1)S(1)}, bf16[512,512]{1,0:T(8,128)(2,1)}, u32[]{:S(2)}) copy-start(bf16[512,512]{1,0:T(8,128)(2,1)} %param.14) | copy-start | bytes 1572868
  2.4 6.0 %copy-start = (bf16[512,512]{1,0:T(8,128)(2,1)S(1)}, bf16[512,512]{1,0:T(8,128)(2,1)}, u32[]{:S(2)}) copy-start(bf16[512,512]{1,0:T(8,128)(2,1)} %rest_0_.1) | copy-start | bytes 1572868
  2.4 11.5 %all-to-all-start = ((bf16[4,400,128]{2,1,0:T(8,128)(2,1)}), bf16[4,400,128]{2,1,0:T(8,128)(2,1)S(1)}, u32[]{:S(2)}, u32[]{:S(2)}) async-start(bf16[4,400,128]{2,1,0:T(8,128)(2,1)} %shard_map.170), calls=%async_computation | async-start | bytes 819200 | tf_op jit(solution)/shard_map/all_to_all | solution.py:427
  7.5 0.7 copy-start.3
  8.2 0.7 copy-start.2
  8.2 0.7 copy-start.4
  8.2 0.7 copy-start.5
  8.3 0.7 copy-start.1
  8.4 0.7 copy-start.6
  8.4 0.7 copy-start.7
  135.1 22.0 %all-to-all-start.6 = ((bf16[16,104,128]{2,1,0:T(8,128)(2,1)}), bf16[16,104,128]{2,1,0:T(8,128)(2,1)S(1)}, u32[]{:S(2)}, u32[]{:S(2)}) async-start(bf16[16,104,128]{2,1,0:T(8,128)(2,1)} %shard_map.179), calls=%async_computation.6 | async-start | bytes 851968 | tf_op jit(solution)/shard_map/all_to_all | solution.py:427
  142.7 5.6 %collective-permute-start = (bf16[320,128]{1,0:T(8,128)(2,1)S(1)}, bf16[320,128]{1,0:T(8,128)(2,1)S(1)}, u32[]{:S(2)}, u32[]{:S(2)}) collective-permute-start(bf16[320,128]{1,0:T(8,128)(2,1)S(1)} %get-tuple-element.59.own), channel_id=1, source_target_pairs={{0,1},{1,0},{2,3},{3,2},{4,5},{5,4},{6,7},{7,6},{8,9},{9,8},{10,11... | collective-permute-start | bytes 245768 | tf_op jit(solution)/shard_map/ppermute | solution.py:425
  148.4 7.8 %collective-permute-start.1 = (bf16[2,320,128]{2,1,0:T(8,128)(2,1)S(1)}, bf16[2,320,128]{2,1,0:T(8,128)(2,1)S(1)}, u32[]{:S(2)}, u32[]{:S(2)}) collective-permute-start(bf16[2,320,128]{2,1,0:T(8,128)(2,1)S(1)} %shard_map.176.near), channel_id=1, source_target_pairs={{0,3},{1,2},{2,1},{3,0},{4,7},{5,6},{6,5},{7,4},{8,11},{9,10},{10,... | collective-permute-start | bytes 491528 | tf_op jit(solution)/shard_map/ppermute | solution.py:425

commit v8 on v7

--- a/solution.py
+++ b/solution.py
@@ -9,6 +9,7 @@
 
 NEAR = ("x", "zl", "c")
 PATCH = ("x", "zh", "zl", "c")
+PEERS = ("zh", "zl", "c", "x")
 BF = jnp.bfloat16
 F32 = jnp.float32
 
@@ -99,7 +100,8 @@
     before = iota((EDGES, EDGES), 0) < iota((EDGES, EDGES), 1)
     same = patch_col[...] == patch_row[...]
     rank = jnp.sum(jnp.where(same & before, 1.0, 0.0), axis=0, keepdims=True)
-    slot = rank.astype(jnp.int32) * PATCHES + patch_row[...]
+    peer = lax.rem(patch_row[...], PATCHES // 4) * 4 + patch_row[...] // (PATCHES // 4)
+    slot = rank.astype(jnp.int32) * PATCHES + peer
     here = jnp.where(iota((SLOTS, EDGES), 0) == slot, 1.0, 0.0).astype(BF)
     row = iota((8, EDGES), 0)
     facts = jnp.where(
@@ -390,9 +392,9 @@
 
 STAGES = (
     (gather_stage, "y"),
-    (send_stage, PATCH),
+    (send_stage, PEERS),
     (message_stage, "y"),
-    (node_stage, PATCH),
+    (node_stage, PEERS),
     (grid_stage, 1),
     (join_stage, 3),
     (back_stage, NEAR),

time: 159 us -> 158 us (level)
  no operation moved by 1% of the time
where the time goes in v8:
time: 158 us; the launch traced here: 157 us
  blocking collectives  116 us (73%)
  starting transfers between devices  17.6 us (11%)
  waiting for transfers between devices  10.5 us (7%)
  Pallas kernels  8.82 us (6%)
  local copies, waits for them, and re-layouts  3.73 us (2%)
    all_to_all x5, blocking collectives, on_device(): st['got'] = lax.all_to_all(st['sent'], axes, 0, 0, tiled=True)  116 us
    all_to_all x2, starting transfers between devices, on_device(): st['got'] = lax.all_to_all(st['sent'], axes, 0, 0, tiled=True)  12.6 us
    pallas_call x11, Pallas kernels, call(): pl.pallas_call(kernel, out_shape=shapes, compiler_params=pltpu.CompilerPa...  8.82 us
    ppermute x2, waiting for transfers between devices, on_device(): lax.ppermute(st['sent'], 'y', [(i, i ^ axes) for i in range(CHANS)])  7.49 us
    ppermute x2, starting transfers between devices, on_device(): lax.ppermute(st['sent'], 'y', [(i, i ^ axes) for i in range(CHANS)])  4.98 us
  transfers between devices with their start and end apart: 4, of which 3 were waited for; matrix products, arithmetic and copies ran while one was open for 1% of the time, Pallas kernels for 1%

profile of v8, /device:TPU:1, one launch (start us, length us, event | category | flops | bytes accessed | tf_op | source)
XLA Modules:
  0.0 156.9 jit_solution(2301062684034162826)
XLA Ops:
  0.6 1.7 %shard_map.170 = bf16[4,400,128]{2,1,0:T(8,128)(2,1)} custom-call(bf16[256,128]{1,0:T(8,128)(2,1)} %grid.1, bf16[64,128]{1,0:T(8,128)(2,1)} %rest_4_.1, bf16[64,128]{1,0:T(8,128)(2,1)} %rest_3_.1, f32[1,128]{1,0:T(1,128)} %bitcast.17), custom_call_target="tpu_custom_call" | custom-call | flops 1048576 | bytes 1048576 | tf_op jit(solution)/shard_map/pallas_call | solution.py:63
  2.4 5.1 %all-to-all-start = ((bf16[4,400,128]{2,1,0:T(8,128)(2,1)}), bf16[4,400,128]{2,1,0:T(8,128)(2,1)S(1)}, u32[]{:S(2)}, u32[]{:S(2)}) async-start(bf16[4,400,128]{2,1,0:T(8,128)(2,1)} %shard_map.170), calls=%async_computation | async-start | bytes 819200 | tf_op jit(solution)/shard_map/all_to_all | solution.py:429
  7.5 0.7 copy-done.3
  8.2 0.1 copy.19.patch_col
  8.3 0.0 copy-start.1
  8.4 0.0 copy-start.6
  8.4 0.5 copy-done.2
  8.9 0.2 copy-done.1
  9.1 0.8 shard_map.171
  9.9 0.9 constant_dynamic-slice_fusion.2
  10.9 3.0 %all-to-all-done.packed = bf16[4,400,128]{2,1,0:T(8,128)(2,1)S(1)} async-done(((bf16[4,400,128]{2,1,0:T(8,128)(2,1)}), bf16[4,400,128]{2,1,0:T(8,128)(2,1)S(1)}, u32[]{:S(2)}, u32[]{:S(2)}) %all-to-all-start) | async-done | bytes 409632 | tf_op jit(solution)/shard_map/all_to_all | solution.py:429
  13.8 0.6 shard_map.172
  14.4 0.1 reshape.43
  14.5 47.8 %all_to_all.35 = bf16[128,2,640]{2,1,0:T(2,128)(2,1)S(1)} all-to-all(bf16[128,2,640]{2,1,0:T(2,128)(2,1)S(1)} %reshape.43), channel_id=1, replica_groups=mesh['x'=4,'zh'=8,'zl'=2,'c'=2,'y'=4] {'zh','zl','c','x'}, dimensions={0} | all-to-all | bytes 655360 | tf_op jit(solution)/shard_map/all_to_all | solution.py:429
  62.3 0.7 shard_map.173
  63.0 6.8 %all_to_all.36.summed = bf16[4,64,128]{2,1,0:T(8,128)(2,1)S(1)} all-to-all(bf16[4,64,128]{2,1,0:T(8,128)(2,1)S(1)} %get-tuple-element.43), channel_id=1, replica_groups=mesh['x'=4,'zh'=8,'zl'=2,'c'=2,'y'=4] {'y'}, dimensions={0} | all-to-all | bytes 131072 | tf_op jit(solution)/shard_map/all_to_all | solution.py:429
  69.9 1.6 %shard_map.174 = (bf16[64,128]{1,0:T(8,128)(2,1)}, bf16[128,1024]{1,0:T(8,128)(2,1)S(1)}, bf16[64,128]{1,0:T(8,128)(2,1)S(1)}, bf16[512,128]{1,0:T(8,128)(2,1)S(...) custom-call(bf16[4,400,128]{2,1,0:T(8,128)(2,1)S(1)} %all-to-all-done.packed, ...), custom_call_target="tpu_custom_call" | custom-call | flops 268435456 | bytes 1048576 | tf_op jit(solution)/shard_map/pallas_call | solution.py:63
  71.5 0.2 reshape.45
  71.7 29.7 %all_to_all.37 = bf16[128,2,512]{2,1,0:T(2,128)(2,1)S(1)} all-to-all(bf16[128,2,512]{2,1,0:T(2,128)(2,1)S(1)} %reshape.45), channel_id=1, replica_groups=mesh['x'=4,'zh'=8,'zl'=2,'c'=2,'y'=4] {'zh','zl','c','x'}, dimensions={0} | all-to-all | bytes 524288 | tf_op jit(solution)/shard_map/all_to_all | solution.py:429
  101.4 0.6 shard_map.175
  102.0 11.7 %all_to_all.38.parts = bf16[16,104,128]{2,1,0:T(8,128)(2,1)S(1)} all-to-all(bf16[16,104,128]{2,1,0:T(8,128)(2,1)S(1)} %get-tuple-element.62), channel_id=1, replica_groups=mesh['x'=4,'zh'=8,'zl'=2,'c'=2,'y'=4] {'x','zl','c'}, dimensions={0} | all-to-all | bytes 851968 | tf_op jit(solution)/shard_map/all_to_all | solution.py:429
  113.7 0.1 shard_map.178
  113.8 19.5 %all_to_all.39.parts = bf16[8,104,128]{2,1,0:T(8,128)(2,1)S(1)} all-to-all(bf16[8,104,128]{2,1,0:T(8,128)(2,1)S(1)} %shard_map.178), channel_id=1, replica_groups=mesh['x'=4,'zh'=8,'zl'=2,'c'=2,'y'=4] {'zh'}, dimensions={0} | all-to-all | bytes 425984 | tf_op jit(solution)/shard_map/all_to_all | solution.py:429
  133.4 0.8 shard_map.179
  134.2 7.4 %all-to-all-start.6 = ((bf16[16,104,128]{2,1,0:T(8,128)(2,1)}), bf16[16,104,128]{2,1,0:T(8,128)(2,1)S(1)}, u32[]{:S(2)}, u32[]{:S(2)}) async-start(bf16[16,104,128]{2,1,0:T(8,128)(2,1)} %shard_map.179), calls=%async_computation.6 | async-start | bytes 851968 | tf_op jit(solution)/shard_map/all_to_all | solution.py:429
  141.6 2.2 %collective-permute-start = (bf16[320,128]{1,0:T(8,128)(2,1)S(1)}, bf16[320,128]{1,0:T(8,128)(2,1)S(1)}, u32[]{:S(2)}, u32[]{:S(2)}) collective-permute-start(bf16[320,128]{1,0:T(8,128)(2,1)S(1)} %get-tuple-element.59.own), channel_id=1, source_target_pairs={{0,1},{1,0},{2,3},{3,2},{4,5},{5,4},{6,7},{7,6},{8,9},{9,8},{10,11... | collective-permute-start | bytes 245768 | tf_op jit(solution)/shard_map/ppermute | solution.py:427
  143.8 3.5 %collective-permute-done.other = bf16[320,128]{1,0:T(8,128)(2,1)S(1)} collective-permute-done((bf16[320,128]{1,0:T(8,128)(2,1)S(1)}, bf16[320,128]{1,0:T(8,128)(2,1)S(1)}, u32[]{:S(2)}, u32[]{:S(2)}) %collective-permute-start) | collective-permute-done | bytes 81952 | tf_op jit(solution)/shard_map/ppermute | solution.py:427
  147.3 2.8 %collective-permute-start.1 = (bf16[2,320,128]{2,1,0:T(8,128)(2,1)S(1)}, bf16[2,320,128]{2,1,0:T(8,128)(2,1)S(1)}, u32[]{:S(2)}, u32[]{:S(2)}) collective-permute-start(bf16[2,320,128]{2,1,0:T(8,128)(2,1)S(1)} %shard_map.176.near), channel_id=1, source_target_pairs={{0,3},{1,2},{2,1},{3,0},{4,7},{5,6},{6,5},{7,4},{8,11},{9,10},{10,... | collective-permute-start | bytes 491528 | tf_op jit(solution)/shard_map/ppermute | solution.py:427
  150.1 0.9 constant_dynamic-slice_fusion
  151.0 4.0 %collective-permute-done.1.far = bf16[2,320,128]{2,1,0:T(8,128)(2,1)S(1)} collective-permute-done((bf16[2,320,128]{2,1,0:T(8,128)(2,1)S(1)}, bf16[2,320,128]{2,1,0:T(8,128)(2,1)S(1)}, u32[]{:S(2)}, u32[]{:S(2)}) %collective-permute-start.1) | collective-permute-done | bytes 163872 | tf_op jit(solution)/shard_map/ppermute | solution.py:427
  155.0 0.9 shard_map.177
  156.0 0.9 shard_map.180
  (17 shorter events, 0.1 us)
Async XLA Ops:
  0.6 9.3 %copy-start.8 = (bf16[512,512]{1,0:T(8,128)(2,1)S(1)}, bf16[512,512]{1,0:T(8,128)(2,1)}, u32[]{:S(2)}) copy-start(bf16[512,512]{1,0:T(8,128)(2,1)} %param.14) | copy-start | bytes 1572868
  2.4 6.0 %copy-start = (bf16[512,512]{1,0:T(8,128)(2,1)S(1)}, bf16[512,512]{1,0:T(8,128)(2,1)}, u32[]{:S(2)}) copy-start(bf16[512,512]{1,0:T(8,128)(2,1)} %rest_0_.1) | copy-start | bytes 1572868
  2.4 11.5 %all-to-all-start = ((bf16[4,400,128]{2,1,0:T(8,128)(2,1)}), bf16[4,400,128]{2,1,0:T(8,128)(2,1)S(1)}, u32[]{:S(2)}, u32[]{:S(2)}) async-start(bf16[4,400,128]{2,1,0:T(8,128)(2,1)} %shard_map.170), calls=%async_computation | async-start | bytes 819200 | tf_op jit(solution)/shard_map/all_to_all | solution.py:429
  7.5 0.7 copy-start.3
  8.2 0.7 copy-start.2
  8.2 0.7 copy-start.4
  8.2 0.7 copy-start.5
  8.3 0.7 copy-start.1
  8.4 0.7 copy-start.6
  8.4 0.7 copy-start.7
  134.2 21.8 %all-to-all-start.6 = ((bf16[16,104,128]{2,1,0:T(8,128)(2,1)}), bf16[16,104,128]{2,1,0:T(8,128)(2,1)S(1)}, u32[]{:S(2)}, u32[]{:S(2)}) async-start(bf16[16,104,128]{2,1,0:T(8,128)(2,1)} %shard_map.179), calls=%async_computation.6 | async-start | bytes 851968 | tf_op jit(solution)/shard_map/all_to_all | solution.py:429
  141.6 5.6 %collective-permute-start = (bf16[320,128]{1,0:T(8,128)(2,1)S(1)}, bf16[320,128]{1,0:T(8,128)(2,1)S(1)}, u32[]{:S(2)}, u32[]{:S(2)}) collective-permute-start(bf16[320,128]{1,0:T(8,128)(2,1)S(1)} %get-tuple-element.59.own), channel_id=1, source_target_pairs={{0,1},{1,0},{2,3},{3,2},{4,5},{5,4},{6,7},{7,6},{8,9},{9,8},{10,11... | collective-permute-start | bytes 245768 | tf_op jit(solution)/shard_map/ppermute | solution.py:427
  147.3 7.8 %collective-permute-start.1 = (bf16[2,320,128]{2,1,0:T(8,128)(2,1)S(1)}, bf16[2,320,128]{2,1,0:T(8,128)(2,1)S(1)}, u32[]{:S(2)}, u32[]{:S(2)}) collective-permute-start(bf16[2,320,128]{2,1,0:T(8,128)(2,1)S(1)} %shard_map.176.near), channel_id=1, source_target_pairs={{0,3},{1,2},{2,1},{3,0},{4,7},{5,6},{6,5},{7,4},{8,11},{9,10},{10,... | collective-permute-start | bytes 491528 | tf_op jit(solution)/shard_map/ppermute | solution.py:427
